TPU v7x, 32 devices: a whole 2x2x4 slice. The times are simulated.
32 devices in a mesh: ty: 2 (over x), tx: 4 (over y, core), pat: 4 (over z).
Axes of the slice: x: 2, y: 2, z: 4, core: 2. Of those that a mesh axis runs over, the one named last changes fastest.
Arguments:
- estimate: float32 [32, 32, 1024], P(None, 'ty', 'tx'), may hold values from 0.5 to 1.5, as said below
- data: float32 [8, 32, 32, 1024], P('pat', None, 'ty', 'tx'), may hold values from 0.1 to 6, as said below
- axial: float32 [32, 32], replicated, may hold values from 0 to 0.6, as said below
- lateral_kernel: float32 [9, 9], replicated, may hold values from 0.01 to 0.04
- psf_radius: int32 [9], replicated, may hold values from 0 to 4
- pattern_codes: int32 [2, 8], replicated, may hold values from 0 to 4, as said below
Outputs:
- object_out: float32 [32, 32, 1024], P(None, 'ty', 'tx')
- residual_rms: float32 [4], replicated
Inputs may be any that keep to these rules, and one draw needn't show every extreme that they name: `estimate`: positive values. `data`: positive photon counts. `axial`: nonnegative entries. `pattern_codes`: angle indices are 0 to 2, phase indices 0 to 4.
All inputs are finite; a program needn't handle non-finite values.
Results may differ from a plain program's by a relative error of at most 0.0003.
The roundings to bfloat16 on the way count: a program that leaves them out, or rounds other values in their place, can miss the bound.
Values may be sent and summed in bfloat16 or wider, within the bound.
No kernel may reach another device: no remote copies, remote signals or barrier semaphores. Data moves between devices by JAX's collectives and lax.ppermute only.
A program may use at most 128 MiB of HBM per device.

v0:
```python
import math

import jax
import jax.numpy as jnp
from jax import lax
from jax.sharding import PartitionSpec as P

RADIUS = 4
ITERS = 4


TWO_PI = 2.0 * math.pi


def extended(block, sides, width):
    for axis, dim in sides:
        count = lax.axis_size(axis)
        forward = [(i, i + 1) for i in range(count - 1)]
        backward = [(target, source) for source, target in forward]
        low = lax.ppermute(
            lax.slice_in_dim(block, block.shape[dim] - width, None, axis=dim), axis, forward
        )
        high = lax.ppermute(lax.slice_in_dim(block, 0, width, axis=dim), axis, backward)
        block = jnp.concatenate([low, block, high], axis=dim)
    return block


def wave_table(angle_code, phase_code, row_coord, col_coord, planes):
    step_col = jnp.where(angle_code == 0, 2, -1).astype(jnp.int32)
    step_row = jnp.where(angle_code == 0, 0, jnp.where(angle_code == 1, 2, -2)).astype(jnp.int32)
    argument = (
        step_col[:, None, None] * col_coord[None, None, :]
        + step_row[:, None, None] * row_coord[None, :, None]
        + phase_code[:, None, None]
    ) % 5
    lateral_wave = jnp.cos(argument.astype(jnp.float32) * (TWO_PI / 5.0))
    plane_index = jnp.arange(planes).astype(jnp.float32)
    axial_wave = jnp.cos(plane_index * (TWO_PI * 3.0 / planes))
    return 1.0 + 0.7 * lateral_wave[:, None, :, :] * axial_wave[None, :, None, None]


def masked_kernel(lateral_kernel, psf_radius):
    offsets = jnp.arange(2 * RADIUS + 1) - RADIUS
    within = jnp.abs(offsets)[None, :] <= psf_radius[:, None]
    return jnp.where(within, lateral_kernel, jnp.zeros_like(lateral_kernel)).astype(jnp.bfloat16)


def tap_matrices(kernel, width_in, width_out):
    tap_count = 2 * RADIUS + 1
    offset = jnp.arange(width_in)[:, None] - jnp.arange(width_out)[None, :]
    onehot = (offset[None, :, :] == jnp.arange(tap_count)[:, None, None]).astype(jnp.float32)
    return jnp.einsum(
        "ij,jab->iab", kernel.astype(jnp.float32), onehot, precision=lax.Precision.HIGHEST
    ).astype(jnp.bfloat16)


def lateral_pass(padded, matrices, height):
    summed = None
    for tap_row in range(2 * RADIUS + 1):
        window = padded[..., tap_row : tap_row + height, :]
        product = jnp.dot(window, matrices[tap_row], preferred_element_type=jnp.float32)
        summed = product if summed is None else summed + product
    return summed


def per_device(estimate, data, axial, lateral_kernel, psf_radius, pattern_codes):
    planes, height, width = estimate.shape
    pat_local = data.shape[0]
    full_rows = height * lax.axis_size("ty")
    full_cols = width * lax.axis_size("tx")
    depth = 2 * RADIUS
    margin = depth - RADIUS
    row_coord = lax.axis_index("ty") * height - depth + jnp.arange(height + 2 * depth)
    col_coord = lax.axis_index("tx") * width - depth + jnp.arange(width + 2 * depth)
    codes_here = lax.dynamic_slice_in_dim(
        pattern_codes, lax.axis_index("pat") * pat_local, pat_local, 1
    )
    lighting = wave_table(codes_here[0], codes_here[1], row_coord, col_coord, planes)
    lighting_inner = lighting[:, :, depth : depth + height, depth : depth + width]
    kernel = masked_kernel(lateral_kernel, psf_radius)
    forward_taps = tap_matrices(kernel, width + 2 * depth, width + 2 * margin)
    adjoint_taps = tap_matrices(kernel[::-1, ::-1], width + 2 * RADIUS, width)
    axial_b = axial.astype(jnp.bfloat16)
    row_inside = (row_coord >= 0) & (row_coord < full_rows)
    col_inside = (col_coord >= 0) & (col_coord < full_cols)
    inside_all = row_inside[:, None] & col_inside[None, :]
    inside = inside_all[
        margin : margin + height + 2 * RADIUS, margin : margin + width + 2 * RADIUS
    ].astype(jnp.bfloat16)
    inside_mid = inside_all[
        RADIUS : RADIUS + height + 2 * margin, RADIUS : RADIUS + width + 2 * margin
    ]
    coverage = lateral_pass(inside[None], adjoint_taps, height).astype(jnp.bfloat16)
    spread = jnp.einsum(
        "ba,byx->ayx",
        axial_b,
        jnp.broadcast_to(coverage, (planes, height, width)),
        preferred_element_type=jnp.float32,
    )
    normalizer = lax.psum(jnp.sum(lighting_inner * spread[None], axis=0), "pat")
    cell_count = float(pat_local * lax.axis_size("pat") * planes * full_rows * full_cols)
    data_wide = extended(data, (("ty", 2), ("tx", 3)), RADIUS)
    current = estimate
    padded = None
    squares_list = []
    for iteration in range(ITERS):
        padded = extended(current, (("ty", 1), ("tx", 2)), depth)
        lighted = (lighting * padded[None]).astype(jnp.bfloat16)
        blurred = jnp.einsum(
            "ab,pbyx->payx", axial_b, lighted, preferred_element_type=jnp.float32
        ).astype(jnp.bfloat16)
        predicted = lateral_pass(blurred, forward_taps, height + 2 * margin)
        predicted_inner = predicted[:, :, margin : margin + height, margin : margin + width]
        misfit = data - predicted_inner
        local_square = jnp.sum(misfit * misfit)
        safe = jnp.where(inside_mid[None, None], predicted, 1.0)
        quotient_padded = jnp.where(inside_mid[None, None], data_wide / safe, 0.0).astype(
            jnp.bfloat16
        )
        backward = lateral_pass(quotient_padded, adjoint_taps, height).astype(jnp.bfloat16)
        gathered = jnp.einsum(
            "ba,pbyx->payx", axial_b, backward, preferred_element_type=jnp.float32
        )
        contribution = jnp.sum(lighting_inner * gathered, axis=0)
        summed = lax.psum(contribution, "pat")
        current = current * summed / normalizer
        padded = None
        squares_list.append(lax.psum(local_square, ("ty", "tx", "pat")))
    squares = jnp.stack(squares_list)
    return (current, jnp.sqrt(squares / cell_count))


def solution(mesh):
    in_specs = (P(None, "ty", "tx"), P("pat", None, "ty", "tx"), P(), P(), P(), P())
    out_specs = (P(None, "ty", "tx"), P())
    return jax.shard_map(
        per_device, mesh=mesh, in_specs=in_specs, out_specs=out_specs, check_vma=False
    )
```

profile of v0, /device:TPU:0, one launch (start us, length us, event | category | flops | bytes accessed | tf_op | source)
XLA Modules:
  0.0 443.4 jit_solution(10551069220233498073)
XLA Ops:
  10.4 6.3 %collective-permute-start.4 = (f32[32,8,256]{2,1,0:T(8,128)}, f32[32,8,256]{2,1,0:T(8,128)}, u32[]{:S(2)}, u32[]{:S(2)}) collective-permute-start(f32[32,8,256]{2,1,0:T(8,128)} %get-tuple-element.123), channel_id=1, source_target_pairs={{0,16},{1,17},{2,18},{3,19},{4,20},{5,21},{6,22},{7,23},{8,24},{9,... | collective-permute-start | bytes 786440 | tf_op jit(solution)/shard_map/ppermute | solution.py:20
  26.6 4.1 fusion.273
  49.4 5.7 %collective-permute-start.2 = (f32[2,32,24,4]{1,2,3,0:T(8,128)S(1)}, f32[2,32,24,4]{1,2,3,0:T(8,128)S(1)}, u32[]{:S(2)}, u32[]{:S(2)}) collective-permute-start(f32[2,32,24,4]{1,2,3,0:T(8,128)S(1)} %copy.98), channel_id=1, source_target_pairs={{0,4},{4,8},{8,12},{1,5},{5,9},{9,13},{2,6},{6,10},{10,14},{3,7},{... | collective-permute-start | bytes 73736 | tf_op jit(solution)/shard_map/ppermute | solution.py:20
  78.0 4.2 select_convert_fusion.3
  90.7 3.7 fusion.33
  94.5 55.7 %all-reduce.13.cloned.1.call-done = (f32[32,16,256]{2,0,1:T(8,128)}, f32[32,16,256]{2,0,1:T(8,128)}) async-done(((f32[32,16,256]{2,0,1:T(8,128)}, f32[32,16,256]{2,0,1:T(8,128)}), (f32[32,16,256]{2,0,1:T(8,128)}, f32[32,16,256]{2,0,1:T(8,128)})) %all-reduce.13.cloned.1.call-update) | async-done | bytes 1048592 | tf_op jit(solution)/shard_map/psum | solution.py:100
  156.7 4.4 collective-permute-done.8
  161.0 4.1 collective-permute-done.9
  168.3 4.1 collective-permute-done.11
  183.2 4.1 select_convert_fusion.2
  195.8 3.7 fusion.32
  199.6 42.9 %all-reduce.7.cloned.1.call-done = f32[32,16,256]{2,0,1:T(8,128)} async-done(((f32[32,16,256]{2,0,1:T(8,128)}), f32[32,16,256]{2,0,1:T(8,128)}) %all-reduce.7.cloned.1.call-update) | async-done | bytes 524304 | tf_op jit(solution)/shard_map/psum | solution.py:125
  243.9 3.4 collective-permute-start.12
  251.9 4.1 collective-permute-done.13
  259.2 4.1 collective-permute-done.15
  273.8 4.1 select_convert_fusion.1
  286.5 3.7 fusion.31
  290.3 43.3 %all-reduce.9.cloned.1.call-done = f32[32,16,256]{2,0,1:T(8,128)} async-done(((f32[32,16,256]{2,0,1:T(8,128)}), f32[32,16,256]{2,0,1:T(8,128)}) %all-reduce.9.cloned.1.call-update) | async-done | bytes 524304 | tf_op jit(solution)/shard_map/psum | solution.py:125
  335.2 3.4 collective-permute-start.16
  343.2 4.1 collective-permute-done.17
  350.5 4.1 collective-permute-done.19
  365.4 4.1 select_convert_fusion
  380.5 5.7 %fusion.114 = (f32[]{:T(128)}, f32[]{:T(128)}, f32[]{:T(128)}, f32[]{:T(128)}) fusion(f32[2,32,16,256]{3,2,1,0:T(8,128)S(1)} %copy-done.2, f32[2,32,24,264]{3,2,1,0:T(8,128)} %get-tuple-element.130, f32[2,32,24,264]{3,2,1,0:T(8,128)} %get-tuple-element.132, f32[2,32,24,264]{3,2,1,0:T(8,128)} %get-tuple-element.136, f32[2,32,24,264]{3,2,1,0:T(8,128)} %get-tuple-element.134), kind=kLoop, calls=%fused_computation.188 | loop fusion | flops 3145724 | bytes 5242896 | tf_op jit(solution)/shard_map/reduce_sum | solution.py:115
  386.2 45.0 %all-reduce = (f32[1]{0:T(128)}, f32[1]{0:T(128)}, f32[1]{0:T(128)}, f32[1]{0:T(128)}) all-reduce(f32[1]{0:T(128)} %bitcast.53, f32[1]{0:T(128)} %bitcast.52, f32[1]{0:T(128)} %bitcast.51, f32[1]{0:T(128)} %bitcast.50), channel_id=1, replica_groups=mesh['ty'=2,'tx'=4,'pat'=4] {'ty','tx','pat'}, use_global_device_ids=true, to_apply=%region_17.18 | all-reduce | flops 4 | bytes 32 | tf_op jit(solution)/shard_map/psum | solution.py:128
  (421 shorter events, 155.3 us)
Async XLA Ops:
  7.2 143.0 %all-reduce.13.cloned.1.call-start = ((), (), s32[]{:S(2)}) async-start(), calls=%async_computation.3 | async-start | bytes 2097152 | tf_op jit(solution)/shard_map/psum | solution.py:100
  9.1 28.0 %collective-permute-start.5 = (f32[32,8,256]{2,1,0:T(8,128)}, f32[32,8,256]{2,1,0:T(8,128)}, u32[]{:S(2)}, u32[]{:S(2)}) collective-permute-start(f32[32,8,256]{2,1,0:T(8,128)} %get-tuple-element.122), channel_id=1, source_target_pairs={{16,0},{17,1},{18,2},{19,3},{20,4},{21,5},{22,6},{23,7},{24,8},{25... | collective-permute-start | bytes 786440 | tf_op jit(solution)/shard_map/ppermute | solution.py:23
  10.4 25.7 %collective-permute-start.4 = (f32[32,8,256]{2,1,0:T(8,128)}, f32[32,8,256]{2,1,0:T(8,128)}, u32[]{:S(2)}, u32[]{:S(2)}) collective-permute-start(f32[32,8,256]{2,1,0:T(8,128)} %get-tuple-element.123), channel_id=1, source_target_pairs={{0,16},{1,17},{2,18},{3,19},{4,20},{5,21},{6,22},{7,23},{8,24},{9,... | collective-permute-start | bytes 786440 | tf_op jit(solution)/shard_map/ppermute | solution.py:20
  18.8 24.3 %collective-permute-start = (f32[2,32,4,256]{3,2,1,0:T(4,128)}, f32[2,32,4,256]{3,2,1,0:T(4,128)S(1)}, u32[]{:S(2)}, u32[]{:S(2)}) collective-permute-start(f32[2,32,4,256]{3,2,1,0:T(4,128)} %get-tuple-element.112), channel_id=1, source_target_pairs={{0,16},{1,17},{2,18},{3,19},{4,20},{5,21},{6,22},{7,23},{8,24},{9,... | collective-permute-start | bytes 786440 | tf_op jit(solution)/shard_map/ppermute | solution.py:20
  20.1 23.0 %collective-permute-start.1 = (f32[2,32,4,256]{3,2,1,0:T(4,128)}, f32[2,32,4,256]{3,2,1,0:T(4,128)S(1)}, u32[]{:S(2)}, u32[]{:S(2)}) collective-permute-start(f32[2,32,4,256]{3,2,1,0:T(4,128)} %get-tuple-element.113), channel_id=1, source_target_pairs={{16,0},{17,1},{18,2},{19,3},{20,4},{21,5},{22,6},{23,7},{24,8},{25... | collective-permute-start | bytes 786440 | tf_op jit(solution)/shard_map/ppermute | solution.py:23
  39.6 25.7 %collective-permute-start.6 = (f32[32,32,8]{2,1,0:T(8,128)}, f32[32,32,8]{2,1,0:T(8,128)}, u32[]{:S(2)}, u32[]{:S(2)}) collective-permute-start(f32[32,32,8]{2,1,0:T(8,128)} %get-tuple-element.114), channel_id=1, source_target_pairs={{0,4},{4,8},{8,12},{1,5},{5,9},{9,13},{2,6},{6,10},{10,14},{3,7},{... | collective-permute-start | bytes 98312 | tf_op jit(solution)/shard_map/ppermute | solution.py:20
  41.9 23.4 %collective-permute-start.7 = (f32[32,32,8]{2,1,0:T(8,128)}, f32[32,32,8]{2,1,0:T(8,128)}, u32[]{:S(2)}, u32[]{:S(2)}) collective-permute-start(f32[32,32,8]{2,1,0:T(8,128)} %get-tuple-element.115), channel_id=1, source_target_pairs={{4,0},{8,4},{12,8},{5,1},{9,5},{13,9},{6,2},{10,6},{14,10},{7,3},{... | collective-permute-start | bytes 98312 | tf_op jit(solution)/shard_map/ppermute | solution.py:23
  48.0 16.0 %collective-permute-start.3 = (f32[2,32,24,4]{1,2,3,0:T(8,128)S(1)}, f32[2,32,24,4]{1,2,3,0:T(8,128)}, u32[]{:S(2)}, u32[]{:S(2)}) collective-permute-start(f32[2,32,24,4]{1,2,3,0:T(8,128)S(1)} %copy.99), channel_id=1, source_target_pairs={{4,0},{8,4},{12,8},{5,1},{9,5},{13,9},{6,2},{10,6},{14,10},{7,3},{... | collective-permute-start | bytes 73736 | tf_op jit(solution)/shard_map/ppermute | solution.py:23
  49.4 14.2 %collective-permute-start.2 = (f32[2,32,24,4]{1,2,3,0:T(8,128)S(1)}, f32[2,32,24,4]{1,2,3,0:T(8,128)S(1)}, u32[]{:S(2)}, u32[]{:S(2)}) collective-permute-start(f32[2,32,24,4]{1,2,3,0:T(8,128)S(1)} %copy.98), channel_id=1, source_target_pairs={{0,4},{4,8},{8,12},{1,5},{5,9},{9,13},{2,6},{6,10},{10,14},{3,7},{... | collective-permute-start | bytes 73736 | tf_op jit(solution)/shard_map/ppermute | solution.py:20
  94.5 148.0 %all-reduce.7.cloned.1.call-start = ((), (), s32[]{:S(2)}) async-start(), calls=%async_computation | async-start | bytes 1048576 | tf_op jit(solution)/shard_map/psum | solution.py:125
  152.0 9.0 %collective-permute-start.8 = (f32[32,8,256]{2,0,1:T(8,128)S(1)}, f32[32,8,256]{2,0,1:T(8,128)S(1)}, u32[]{:S(2)}, u32[]{:S(2)}) collective-permute-start(f32[32,8,256]{2,0,1:T(8,128)S(1)} %get-tuple-element.120), channel_id=1, source_target_pairs={{0,16},{1,17},{2,18},{3,19},{4,20},{5,21},{6,22},{7,23},{8,24},{9,... | collective-permute-start | bytes 786440 | tf_op jit(solution)/shard_map/ppermute | solution.py:20
  155.4 9.8 %collective-permute-start.9 = (f32[32,8,256]{2,0,1:T(8,128)S(1)}, f32[32,8,256]{2,0,1:T(8,128)S(1)}, u32[]{:S(2)}, u32[]{:S(2)}) collective-permute-start(f32[32,8,256]{2,0,1:T(8,128)S(1)} %get-tuple-element.121), channel_id=1, source_target_pairs={{16,0},{17,1},{18,2},{19,3},{20,4},{21,5},{22,6},{23,7},{24,8},{25... | collective-permute-start | bytes 786440 | tf_op jit(solution)/shard_map/ppermute | solution.py:23
  165.5 2.8 collective-permute-start.10
  166.8 5.6 %collective-permute-start.11 = (f32[32,32,8]{2,0,1:T(8,128)S(1)}, f32[32,32,8]{2,0,1:T(8,128)S(1)}, u32[]{:S(2)}, u32[]{:S(2)}) collective-permute-start(f32[32,32,8]{2,0,1:T(8,128)S(1)} %get-tuple-element.111), channel_id=1, source_target_pairs={{4,0},{8,4},{12,8},{5,1},{9,5},{13,9},{6,2},{10,6},{14,10},{7,3},{... | collective-permute-start | bytes 98312 | tf_op jit(solution)/shard_map/ppermute | solution.py:23
  199.5 134.1 %all-reduce.9.cloned.1.call-start = ((), (), s32[]{:S(2)}) async-start(), calls=%async_computation.1 | async-start | bytes 1048576 | tf_op jit(solution)/shard_map/psum | solution.py:125
  243.9 8.0 %collective-permute-start.12 = (f32[32,8,256]{2,0,1:T(8,128)S(1)}, f32[32,8,256]{2,0,1:T(8,128)S(1)}, u32[]{:S(2)}, u32[]{:S(2)}) collective-permute-start(f32[32,8,256]{2,0,1:T(8,128)S(1)} %get-tuple-element.118), channel_id=1, source_target_pairs={{0,16},{1,17},{2,18},{3,19},{4,20},{5,21},{6,22},{7,23},{8,24},{9,... | collective-permute-start | bytes 786440 | tf_op jit(solution)/shard_map/ppermute | solution.py:20
  247.3 8.7 %collective-permute-start.13 = (f32[32,8,256]{2,0,1:T(8,128)S(1)}, f32[32,8,256]{2,0,1:T(8,128)S(1)}, u32[]{:S(2)}, u32[]{:S(2)}) collective-permute-start(f32[32,8,256]{2,0,1:T(8,128)S(1)} %get-tuple-element.119), channel_id=1, source_target_pairs={{16,0},{17,1},{18,2},{19,3},{20,4},{21,5},{22,6},{23,7},{24,8},{25... | collective-permute-start | bytes 786440 | tf_op jit(solution)/shard_map/ppermute | solution.py:23
  256.3 2.8 collective-permute-start.14
  257.7 5.6 %collective-permute-start.15 = (f32[32,32,8]{2,0,1:T(8,128)S(1)}, f32[32,32,8]{2,0,1:T(8,128)S(1)}, u32[]{:S(2)}, u32[]{:S(2)}) collective-permute-start(f32[32,32,8]{2,0,1:T(8,128)S(1)} %get-tuple-element.109), channel_id=1, source_target_pairs={{4,0},{8,4},{12,8},{5,1},{9,5},{13,9},{6,2},{10,6},{14,10},{7,3},{... | collective-permute-start | bytes 98312 | tf_op jit(solution)/shard_map/ppermute | solution.py:23
  290.3 144.1 %all-reduce.11.cloned.1.call-start = ((), (), s32[]{:S(2)}) async-start(), calls=%async_computation.2 | async-start | bytes 1048576 | tf_op jit(solution)/shard_map/psum | solution.py:125
  335.2 8.0 %collective-permute-start.16 = (f32[32,8,256]{2,0,1:T(8,128)S(1)}, f32[32,8,256]{2,0,1:T(8,128)S(1)}, u32[]{:S(2)}, u32[]{:S(2)}) collective-permute-start(f32[32,8,256]{2,0,1:T(8,128)S(1)} %get-tuple-element.116), channel_id=1, source_target_pairs={{0,16},{1,17},{2,18},{3,19},{4,20},{5,21},{6,22},{7,23},{8,24},{9,... | collective-permute-start | bytes 786440 | tf_op jit(solution)/shard_map/ppermute | solution.py:20
  338.6 8.7 %collective-permute-start.17 = (f32[32,8,256]{2,0,1:T(8,128)S(1)}, f32[32,8,256]{2,0,1:T(8,128)S(1)}, u32[]{:S(2)}, u32[]{:S(2)}) collective-permute-start(f32[32,8,256]{2,0,1:T(8,128)S(1)} %get-tuple-element.117), channel_id=1, source_target_pairs={{16,0},{17,1},{18,2},{19,3},{20,4},{21,5},{22,6},{23,7},{24,8},{25... | collective-permute-start | bytes 786440 | tf_op jit(solution)/shard_map/ppermute | solution.py:23
  347.6 2.8 collective-permute-start.18
  349.0 5.6 %collective-permute-start.19 = (f32[32,32,8]{2,0,1:T(8,128)S(1)}, f32[32,32,8]{2,0,1:T(8,128)S(1)}, u32[]{:S(2)}, u32[]{:S(2)}) collective-permute-start(f32[32,32,8]{2,0,1:T(8,128)S(1)} %get-tuple-element.107), channel_id=1, source_target_pairs={{4,0},{8,4},{12,8},{5,1},{9,5},{13,9},{6,2},{10,6},{14,10},{7,3},{... | collective-permute-start | bytes 98312 | tf_op jit(solution)/shard_map/ppermute | solution.py:23
  (111 other events, 469.5 us)
Sparse Core Ops, SparseCore 0:
  94.6 55.5 all-reduce.12
  199.6 42.7 all-reduce.6
  290.4 43.2 all-reduce.8
  380.6 43.6 all-reduce.10
where the time goes:
time: 452 us; the launch traced here: 443 us
  waiting for transfers between devices  178 us (39%)
  matrix products  83.5 us (18%)
  local copies, waits for them, and re-layouts  52.9 us (12%)
  blocking collectives  45 us (10%)
  starting transfers between devices  43.4 us (10%)
  other arithmetic  24.9 us (6%)
  between operations  15.9 us (4%)
    psum x3, waiting for transfers between devices, per_device(): summed = lax.psum(contribution, 'pat')  86.2 us
    dot_general x77, matrix products, lateral_pass(): jnp.dot(window, matrices[tap_row], preferred_element_type=jnp.float32)  63 us
    psum x1, waiting for transfers between devices, per_device(): normalizer = lax.psum(jnp.sum(lighting_inner * spread[None], axis=0), 'pat')  55.7 us
    psum x1, blocking collectives, per_device(): squares_list.append(lax.psum(local_square, ('ty', 'tx', 'pat')))  45 us
    ppermute x10, starting transfers between devices, extended(): lax.ppermute(lax.slice_in_dim(block, block.shape[dim] - width, None, axis...  29.8 us
    ppermute x10, waiting for transfers between devices, extended(): lax.ppermute(lax.slice_in_dim(block, 0, width, axis=dim), axis, backward)  24.8 us
    unnamed x243, local copies, waits for them, and re-layouts  16.7 us
    slice x8, local copies, waits for them, and re-layouts, lateral_pass(): window = padded[..., tap_row:tap_row + height, :]  15.8 us
  transfers between devices with their start and end apart: 24, of which 12 were waited for; matrix products, arithmetic and copies ran while one was open for 10% of the time, Pallas kernels for 0%

commit v1 on v0

--- a/solution.py
+++ b/solution.py
@@ -1,15 +1,467 @@
+import functools
 import math
 
 import jax
 import jax.numpy as jnp
 from jax import lax
+from jax.experimental import pallas as pl
+from jax.experimental.pallas import tpu as pltpu
 from jax.sharding import PartitionSpec as P
 
 RADIUS = 4
+TAPS = 2 * RADIUS + 1
 ITERS = 4
-
-
 TWO_PI = 2.0 * math.pi
+
+TILE = 32
+HALO = 16
+GROUP = TILE + 2 * HALO
+ROWS_BLOCK = RADIUS
+BLOCK = ROWS_BLOCK * GROUP
+LANES = 128
+SUB = 8
+QUAD_ROWS = (0, 2, 1, 3)
+F32 = jnp.float32
+BF16 = jnp.bfloat16
+
+
+def lane_iota(shape):
+    return lax.broadcasted_iota(jnp.int32, shape, len(shape) - 1)
+
+
+def column_of(lane):
+    inner = lane % GROUP
+    return jnp.where(inner < TILE + HALO, inner, inner - GROUP)
+
+
+def roll(x, shift):
+    shift = shift % LANES
+    return x if shift == 0 else pltpu.roll(x, shift, 1)
+
+
+def quad_transpose(v, lane):
+    low = lane < 64
+    even = (lane // TILE) % 2 == 0
+    a0 = jnp.where(low, v[0], roll(v[2], 64))
+    a2 = jnp.where(low, roll(v[0], 64), v[2])
+    a1 = jnp.where(low, v[1], roll(v[3], 64))
+    a3 = jnp.where(low, roll(v[1], 64), v[3])
+    return (
+        jnp.where(even, a0, roll(a1, 32)),
+        jnp.where(even, roll(a0, -32), a1),
+        jnp.where(even, a2, roll(a3, 32)),
+        jnp.where(even, roll(a2, -32), a3),
+    )
+
+
+def pack_kernel(dest_of_tile, rows, where_ref, data_ref, est_ref, out_ref):
+    lane = lane_iota((SUB, LANES))
+    groups = data_ref.shape[0] // (rows * SUB)
+    tiles_half = LANES // TILE
+
+    def piece(half, src_ref, start, out_row):
+        for quad in range(rows // 4):
+            v = [src_ref[pl.ds(start + 4 * quad + r, SUB, stride=rows), :] for r in QUAD_ROWS]
+            for t, piece_t in enumerate(quad_transpose(v, lane)):
+                dest = dest_of_tile[half * tiles_half + t]
+                out_ref[dest, pl.ds(out_row, SUB), quad * LANES : (quad + 1) * LANES] = piece_t
+
+    for half in range(len(dest_of_tile) // tiles_half):
+
+        @pl.when(pl.program_id(0) == half)
+        def _(half=half):
+            def step(i, carry):
+                piece(half, data_ref, i * rows * SUB, pl.multiple_of(i * SUB, SUB))
+                return carry
+
+            lax.fori_loop(0, groups, step, 0)
+            piece(half, est_ref, where_ref[1] * rows * SUB, groups * SUB)
+
+
+def edge_messages(own, lane):
+    left = right = None
+    for u in range(4):
+        slot = (lane // HALO) % 4 == u
+        l_u, r_u = roll(own[u], HALO * u), roll(own[u], HALO * (u - 1))
+        left = l_u if left is None else jnp.where(slot, l_u, left)
+        right = r_u if right is None else jnp.where(slot, r_u, right)
+    return left, right
+
+
+def own_pair(v):
+    return v, roll(v, -TILE)
+
+
+def halo_kernel(src_of, in_ref, left_ref, right_ref):
+    lane = lane_iota((SUB, LANES))
+    ty, pat, planes_part = src_of["ty"], src_of["pat"], in_ref.shape[1] // SUB
+    data_groups = planes_part - 1
+    per_ty = in_ref.shape[2] // LANES // 2
+
+    def emit(k, group, out_row):
+        for i in range(ty):
+            for pair in range(per_ty):
+                own = []
+                for q in (2 * pair, 2 * pair + 1):
+                    own += own_pair(
+                        in_ref[i * pat + k, pl.ds(group * SUB, SUB), q * LANES : (q + 1) * LANES]
+                    )
+                left, right = edge_messages(own, lane)
+                vreg = i * per_ty + pair
+                left_ref[pl.ds(out_row, SUB), vreg * LANES : (vreg + 1) * LANES] = left
+                right_ref[pl.ds(out_row, SUB), vreg * LANES : (vreg + 1) * LANES] = right
+
+    for k in range(pat):
+
+        def step(g, carry, k=k):
+            emit(k, g, pl.multiple_of((k * data_groups + g) * SUB, SUB))
+            return carry
+
+        lax.fori_loop(0, data_groups, step, 0)
+        emit(k, data_groups, (pat * data_groups + k) * SUB)
+
+
+def with_halo(own, u, from_right, from_left, lane):
+    inner = lane % GROUP
+    value = jnp.where(inner < TILE, own, roll(from_right, HALO * (2 - u)))
+    return jnp.where(inner < TILE + HALO, value, roll(from_left, HALO * (3 - u)))
+
+
+def taps_kernel(k_ref, w_ref):
+    lane = lane_iota((GROUP, LANES))
+    row = lax.broadcasted_iota(jnp.int32, (GROUP, LANES), 0)
+    tap = column_of(row) - column_of(lane) + RADIUS
+    first = lane < GROUP
+    w_ref[...] = jnp.zeros_like(w_ref)
+    hit = [tap == j for j in range(TAPS)]
+    for flip in range(2):
+        for i0 in range(TAPS + 1):
+            value = jnp.zeros((GROUP, LANES), F32)
+            for j in range(TAPS):
+                def scalar(i):
+                    if i < 0 or i >= TAPS:
+                        return jnp.float32(0.0)
+                    return k_ref[TAPS - 1 - i, TAPS - 1 - j] if flip else k_ref[i, j]
+                value = jnp.where(hit[j], jnp.where(first, scalar(i0), scalar(i0 - 1)), value)
+            value = value.astype(BF16)
+            for k in range(3):
+                for r in range(ROWS_BLOCK):
+                    for q in range(ROWS_BLOCK // 2):
+                        if ROWS_BLOCK * (k - 1) + r - 2 * q + RADIUS == i0:
+                            w_ref[
+                                3 * flip + k,
+                                r * GROUP : (r + 1) * GROUP,
+                                q * LANES : (q + 1) * LANES,
+                            ] = value
+
+
+def lateral(src_ref, w_ref, flip, b):
+    total = None
+    for k in range(3):
+        part = jnp.dot(src_ref[b + k], w_ref[3 * flip + k], preferred_element_type=F32)
+        total = part if total is None else total + part
+    return total
+
+
+def iterate(where_ref, w_ref, ax_fwd, ax_bwd, light_ref, wave_ref, colsum_ref, data_ref, obj_ref,
+            norm_ref, stage_ref, quot_ref, sq_ref, nx, patterns):
+    planes = obj_ref.shape[1]
+    rows = patterns * planes
+    blocks = obj_ref.shape[0]
+    col = column_of(lane_iota((1, BLOCK)))
+    place = where_ref[0] * TILE + col
+    inside = (place >= 0) & (place < nx)
+    own = (col >= 0) & (col < TILE)
+    stage_ref[0] = jnp.zeros(stage_ref.shape[1:], BF16)
+    stage_ref[blocks + 1] = jnp.zeros(stage_ref.shape[1:], BF16)
+    quot_ref[0] = jnp.zeros(quot_ref.shape[1:], BF16)
+    quot_ref[blocks + 1] = jnp.zeros(quot_ref.shape[1:], BF16)
+
+    ones = jnp.broadcast_to(jnp.where(inside, 1.0, 0.0), (2 * SUB, BLOCK)).astype(BF16)
+    zeros = jnp.zeros((2 * SUB, BLOCK), BF16)
+    for b in range(blocks):
+        total = None
+        for k in range(3):
+            if 0 <= b + k - 1 < blocks:
+                part = jnp.dot(ones, w_ref[3 + k], preferred_element_type=F32)
+                total = part if total is None else total + part
+        cover = total.astype(BF16).astype(F32)[0:1]
+        lat_sum = jnp.sum(light_ref[b], axis=0, keepdims=True)
+        norm_ref[b] = colsum_ref[...] * cover * (float(patterns) + lat_sum * wave_ref[...])
+
+    def lighting(b):
+        lat = light_ref[b][:, None, :]
+        return (1.0 + lat * wave_ref[...][None, :, :])
+
+    for it, (quot_reach, obj_reach) in enumerate(((12, 8), (4, 0))):
+        quot_ok = inside & (col >= -quot_reach) & (col < TILE + quot_reach)
+        obj_ok = inside & (col >= -obj_reach) & (col < TILE + obj_reach)
+
+        def light_step(b, carry):
+            lit = (lighting(b) * obj_ref[b][None]).astype(BF16).reshape(rows, BLOCK)
+            stage_ref[b + 1] = jnp.dot(ax_fwd[...], lit, preferred_element_type=F32).astype(BF16)
+            return carry
+
+        lax.fori_loop(0, blocks, light_step, 0)
+
+        def quot_step(b, acc):
+            predicted = lateral(stage_ref, w_ref, 0, b)
+            data = data_ref[b]
+            miss = data - predicted
+            acc = acc + jnp.sum((miss * miss).reshape(rows // SUB, SUB, BLOCK), axis=0)
+            quot = jnp.where(quot_ok, data / jnp.where(quot_ok, predicted, 1.0), 0.0)
+            quot_ref[b + 1] = quot.astype(BF16)
+            return acc
+
+        acc = lax.fori_loop(0, blocks, quot_step, jnp.zeros((SUB, BLOCK), F32))
+        sq_ref[it] = jnp.where(own, acc, 0.0)
+
+        def back_step(b, carry):
+            back = lateral(quot_ref, w_ref, 1, b).astype(BF16)
+            gathered = jnp.dot(ax_bwd[...], back, preferred_element_type=F32)
+            summed = jnp.sum(lighting(b) * gathered.reshape(patterns, planes, BLOCK), axis=0)
+            obj_ref[b] = jnp.where(obj_ok, obj_ref[b] * summed / norm_ref[b], 0.0)
+            return carry
+
+        lax.fori_loop(0, blocks, back_step, 0)
+
+
+def first_kernel(nx, patterns, src_of, where_ref, w_ref, ax_fwd, ax_bwd, light_ref, wave_ref, colsum_ref, in_ref,
+                 from_left_ref, from_right_ref, data_ref, obj_out_ref, left_ref, right_ref, sq_ref,
+                 obj_ref, norm_ref, stage_ref, quot_ref):
+    lane = lane_iota((SUB, LANES))
+    ty, pat = src_of["ty"], src_of["pat"]
+    data_groups = in_ref.shape[1] // SUB - 1
+    per_ty = in_ref.shape[2] // LANES // 2
+
+    def unpack(k, group, src_row, out_ref, out_row):
+        for i in range(ty):
+            for pair in range(per_ty):
+                vreg = i * per_ty + pair
+                from_left = from_left_ref[pl.ds(src_row, SUB), vreg * LANES : (vreg + 1) * LANES]
+                from_right = from_right_ref[pl.ds(src_row, SUB), vreg * LANES : (vreg + 1) * LANES]
+                own = []
+                for q in (2 * pair, 2 * pair + 1):
+                    own += own_pair(
+                        in_ref[i * pat + k, pl.ds(group * SUB, SUB), q * LANES : (q + 1) * LANES]
+                    )
+                for u in range(4):
+                    m = 4 * vreg + u
+                    out_ref[m // 2, pl.ds(out_row, SUB), (m % 2) * LANES : (m % 2 + 1) * LANES] = (
+                        with_halo(own[u], u, from_right, from_left, lane)
+                    )
+
+    for k in range(pat):
+
+        def step(g, carry, k=k):
+            row = pl.multiple_of((k * data_groups + g) * SUB, SUB)
+            unpack(k, g, row, data_ref, row)
+            return carry
+
+        lax.fori_loop(0, data_groups, step, 0)
+        unpack(k, data_groups, (pat * data_groups + k) * SUB, obj_ref, k * SUB)
+
+    iterate(where_ref, w_ref, ax_fwd, ax_bwd, light_ref, wave_ref, colsum_ref, data_ref, obj_ref,
+            norm_ref, stage_ref, quot_ref, sq_ref, nx, patterns)
+
+    for z in range(0, obj_ref.shape[1], SUB):
+        for vreg in range(obj_ref.shape[0] // 2):
+            own = []
+            for u in range(4):
+                m = 4 * vreg + u
+                v = obj_ref[m // 2, z : z + SUB, (m % 2) * LANES : (m % 2 + 1) * LANES]
+                own.append(v)
+                obj_out_ref[m // 2, z : z + SUB, (m % 2) * LANES : (m % 2 + 1) * LANES] = v
+            left, right = edge_messages(own, lane)
+            left_ref[z : z + SUB, vreg * LANES : (vreg + 1) * LANES] = left
+            right_ref[z : z + SUB, vreg * LANES : (vreg + 1) * LANES] = right
+
+
+def second_kernel(nx, patterns, where_ref, w_ref, ax_fwd, ax_bwd, light_ref, wave_ref, colsum_ref, data_ref,
+                  obj_in_ref, from_left_ref, from_right_ref, out_ref, sq_ref,
+                  obj_ref, norm_ref, stage_ref, quot_ref):
+    lane = lane_iota((SUB, LANES))
+    for z in range(0, obj_ref.shape[1], SUB):
+        for vreg in range(obj_ref.shape[0] // 2):
+            from_left = from_left_ref[z : z + SUB, vreg * LANES : (vreg + 1) * LANES]
+            from_right = from_right_ref[z : z + SUB, vreg * LANES : (vreg + 1) * LANES]
+            for u in range(4):
+                m = 4 * vreg + u
+                at = (m // 2, slice(z, z + SUB), slice((m % 2) * LANES, (m % 2 + 1) * LANES))
+                obj_ref[at] = with_halo(obj_in_ref[at], u, from_right, from_left, lane)
+
+    iterate(where_ref, w_ref, ax_fwd, ax_bwd, light_ref, wave_ref, colsum_ref, data_ref, obj_ref,
+            norm_ref, stage_ref, quot_ref, sq_ref, nx, patterns)
+
+    ty = out_ref.shape[0]
+    quads = out_ref.shape[2] // LANES
+    own = (lane // TILE) % 2 == 0
+    for z in range(0, obj_ref.shape[1], SUB):
+        for i in range(ty):
+            for q in range(quads):
+                m = i * quads + q
+                v0 = obj_ref[m, z : z + SUB, 0:LANES]
+                v1 = obj_ref[m, z : z + SUB, LANES : 2 * LANES]
+                out_ref[i, z : z + SUB, q * LANES : (q + 1) * LANES] = jnp.where(own, v0, roll(v1, TILE))
+
+
+def final_kernel(dest_of_tile, rows, in_ref, out_ref):
+    lane = lane_iota((SUB, LANES))
+    planes = out_ref.shape[0] // rows
+    tiles_half = LANES // TILE
+    for half in range(len(dest_of_tile) // tiles_half):
+
+        @pl.when(pl.program_id(0) == half)
+        def _(half=half):
+            for z in range(0, planes, SUB):
+                for quad in range(rows // 4):
+                    v = [
+                        in_ref[dest_of_tile[half * tiles_half + t], z : z + SUB, quad * LANES : (quad + 1) * LANES]
+                        for t in range(tiles_half)
+                    ]
+                    for g, row in enumerate(quad_transpose(v, lane)):
+                        out_ref[pl.ds(z * rows + 4 * quad + QUAD_ROWS[g], SUB, stride=rows), :] = row
+
+
+def masked_kernel(lateral_kernel, psf_radius):
+    offsets = jnp.arange(TAPS) - RADIUS
+    within = jnp.abs(offsets)[None, :] <= psf_radius[:, None]
+    return jnp.where(within, lateral_kernel, jnp.zeros_like(lateral_kernel)).astype(BF16)
+
+
+def shape(dims, dtype=F32):
+    return jax.ShapeDtypeStruct(dims, dtype)
+
+
+VMEM = pl.BlockSpec(memory_space=pltpu.VMEM)
+SMEM = pl.BlockSpec(memory_space=pltpu.SMEM)
+
+
+def tiled_device(sizes, estimate, data, axial, lateral_kernel, psf_radius, pattern_codes):
+    ty, tx, pat = sizes["ty"], sizes["tx"], sizes["pat"]
+    planes, rows, cols = estimate.shape
+    pat_local = data.shape[0]
+    patterns = pat_local * pat
+    ny, nx = rows * ty, cols * tx
+    members = ty * pat
+    blocks = ny // ROWS_BLOCK
+    axes = ("ty", "tx", "pat")
+
+    owner = [(i, k if i % 2 == 0 else pat - 1 - k) for i in range(ty) for k in range(pat)]
+    dest_of_tile = [i * pat + k for i, k in owner]
+    order = [(i * tx + j) * pat + k for j in range(tx) for i, k in owner]
+    to_right = [(a, b) for a, b in zip(order[:-1], order[1:])]
+    to_left = [(b, a) for a, b in to_right]
+    src_of = {"ty": ty, "pat": pat}
+
+    ti, tj, tk = (lax.axis_index(a) for a in axes)
+    tile = tj * members + ti * pat + jnp.where(ti % 2 == 0, tk, pat - 1 - tk)
+    where = jnp.stack([tile, tk]).astype(jnp.int32)
+
+    packed_rows = pat_local * planes + planes // pat
+    message = pl.pallas_call(
+        functools.partial(pack_kernel, dest_of_tile, rows),
+        out_shape=shape((members, packed_rows, rows * TILE)),
+        grid=(cols // LANES,),
+        in_specs=[
+            SMEM,
+            pl.BlockSpec((data.size // cols, LANES), lambda h: (0, h)),
+            pl.BlockSpec((planes * rows, LANES), lambda h: (0, h)),
+        ],
+        out_specs=pl.BlockSpec((members, packed_rows, rows * TILE), lambda h: (0, 0, 0)),
+        name="pack",
+    )(where, data.reshape(-1, cols), estimate.reshape(-1, cols))
+    mine = lax.all_to_all(message, ("ty", "pat"), 0, 0, tiled=True)
+
+    kernel = masked_kernel(lax.reduce_precision(lateral_kernel, 8, 7), psf_radius).astype(F32)
+    weights = pl.pallas_call(
+        taps_kernel,
+        out_shape=shape((6, BLOCK, BLOCK), BF16),
+        in_specs=[SMEM],
+        out_specs=VMEM,
+        name="taps",
+    )(kernel)
+    axial_b = axial.astype(BF16)
+    same = (jnp.arange(patterns * planes)[:, None] // planes) == (jnp.arange(patterns * planes)[None, :] // planes)
+    ax_fwd = jnp.where(same, jnp.tile(axial_b, (patterns, patterns)), jnp.zeros((), BF16))
+    ax_bwd = jnp.where(same, jnp.tile(axial_b.T, (patterns, patterns)), jnp.zeros((), BF16))
+    colsum = jnp.broadcast_to(jnp.sum(lax.reduce_precision(axial, 8, 7), axis=0)[:, None], (planes, BLOCK))
+    wave = jnp.cos(jnp.arange(planes).astype(F32) * (TWO_PI * 3.0 / planes))
+    wave = jnp.broadcast_to(wave[:, None], (planes, BLOCK))
+    lane = jnp.arange(BLOCK)
+    y = jnp.arange(blocks)[:, None] * ROWS_BLOCK + lane[None, :] // GROUP
+    x = tile * TILE + column_of(lane)[None, :]
+    angle, phase = pattern_codes[0], pattern_codes[1]
+    step_col = jnp.where(angle == 0, 2, -1).astype(jnp.int32)
+    step_row = jnp.where(angle == 0, 0, jnp.where(angle == 1, 2, -2)).astype(jnp.int32)
+    argument = (
+        step_col[None, :, None] * x[:, None, :] + step_row[None, :, None] * y[:, None, :] + phase[None, :, None]
+    ) % 5
+    light = 0.7 * jnp.cos(argument.astype(F32) * (TWO_PI / 5.0))
+
+    halo_lanes = ny * HALO
+    total_rows = packed_rows * pat
+    left, right = pl.pallas_call(
+        functools.partial(halo_kernel, src_of),
+        out_shape=(shape((total_rows, halo_lanes)), shape((total_rows, halo_lanes))),
+        in_specs=[VMEM],
+        out_specs=(VMEM, VMEM),
+        name="edges",
+    )(mine)
+    from_left = lax.ppermute(right, axes, to_right)
+    from_right = lax.ppermute(left, axes, to_left)
+
+    scratch = [
+        pltpu.VMEM((blocks, planes, BLOCK), F32),
+        pltpu.VMEM((blocks, planes, BLOCK), F32),
+        pltpu.VMEM((blocks + 2, patterns * planes, BLOCK), BF16),
+        pltpu.VMEM((blocks + 2, patterns * planes, BLOCK), BF16),
+    ]
+    tables = (where, weights, ax_fwd, ax_bwd, light, wave, colsum)
+    table_specs = [SMEM] + [VMEM] * 6
+    data_all, current, left, right, sq_first = pl.pallas_call(
+        functools.partial(first_kernel, nx, patterns, src_of),
+        out_shape=(
+            shape((blocks, patterns * planes, BLOCK)),
+            shape((blocks, planes, BLOCK)),
+            shape((planes, halo_lanes)),
+            shape((planes, halo_lanes)),
+            shape((2, SUB, BLOCK)),
+        ),
+        in_specs=table_specs + [VMEM] * 3,
+        out_specs=(VMEM,) * 5,
+        scratch_shapes=scratch,
+        name="first",
+    )(*tables, mine, from_left, from_right)
+    from_left = lax.ppermute(right, axes, to_right)
+    from_right = lax.ppermute(left, axes, to_left)
+    pieces, sq_second = pl.pallas_call(
+        functools.partial(second_kernel, nx, patterns),
+        out_shape=(shape((ty, planes, rows * TILE)), shape((2, SUB, BLOCK))),
+        in_specs=table_specs + [VMEM] * 4,
+        out_specs=(VMEM,) * 2,
+        scratch_shapes=scratch,
+        name="second",
+    )(*tables, data_all, current, from_left, from_right)
+
+    squares = jnp.sum(jnp.concatenate([sq_first, sq_second]), axis=(1, 2))
+    squares = jnp.sum(lax.all_gather(squares, "tx"), axis=0)
+    extra = jnp.pad(squares[None, :], ((0, SUB - 1), (0, rows * TILE - ITERS)))
+    outgoing = jnp.concatenate([pieces, jnp.broadcast_to(extra, (ty,) + extra.shape)], axis=1)
+    outgoing = jnp.broadcast_to(outgoing[:, None], (ty, pat) + outgoing.shape[1:])
+    outgoing = outgoing.reshape((members,) + outgoing.shape[2:])
+    incoming = lax.all_to_all(outgoing, ("ty", "pat"), 0, 0, tiled=True)
+    result = pl.pallas_call(
+        functools.partial(final_kernel, dest_of_tile, rows),
+        out_shape=shape((planes * rows, cols)),
+        grid=(cols // LANES,),
+        in_specs=[pl.BlockSpec(incoming.shape, lambda h: (0, 0, 0))],
+        out_specs=pl.BlockSpec((planes * rows, LANES), lambda h: (0, h)),
+        name="unpack",
+    )(incoming)
+    squares = jnp.sum(incoming[:, planes, :ITERS], axis=0)
+    cell_count = float(patterns * planes * ny * nx)
+    return result.reshape(estimate.shape), jnp.sqrt(squares / cell_count)
 
 
 def extended(block, sides, width):
@@ -39,12 +491,6 @@
     return 1.0 + 0.7 * lateral_wave[:, None, :, :] * axial_wave[None, :, None, None]
 
 
-def masked_kernel(lateral_kernel, psf_radius):
-    offsets = jnp.arange(2 * RADIUS + 1) - RADIUS
-    within = jnp.abs(offsets)[None, :] <= psf_radius[:, None]
-    return jnp.where(within, lateral_kernel, jnp.zeros_like(lateral_kernel)).astype(jnp.bfloat16)
-
-
 def tap_matrices(kernel, width_in, width_out):
     tap_count = 2 * RADIUS + 1
     offset = jnp.arange(width_in)[:, None] - jnp.arange(width_out)[None, :]
@@ -63,7 +509,7 @@
     return summed
 
 
-def per_device(estimate, data, axial, lateral_kernel, psf_radius, pattern_codes):
+def general_device(estimate, data, axial, lateral_kernel, psf_radius, pattern_codes):
     planes, height, width = estimate.shape
     pat_local = data.shape[0]
     full_rows = height * lax.axis_size("ty")
@@ -101,7 +547,6 @@
     cell_count = float(pat_local * lax.axis_size("pat") * planes * full_rows * full_cols)
     data_wide = extended(data, (("ty", 2), ("tx", 3)), RADIUS)
     current = estimate
-    padded = None
     squares_list = []
     for iteration in range(ITERS):
         padded = extended(current, (("ty", 1), ("tx", 2)), depth)
@@ -124,15 +569,30 @@
         contribution = jnp.sum(lighting_inner * gathered, axis=0)
         summed = lax.psum(contribution, "pat")
         current = current * summed / normalizer
-        padded = None
         squares_list.append(lax.psum(local_square, ("ty", "tx", "pat")))
     squares = jnp.stack(squares_list)
     return (current, jnp.sqrt(squares / cell_count))
 
 
 def solution(mesh):
+    sizes = dict(mesh.shape)
     in_specs = (P(None, "ty", "tx"), P("pat", None, "ty", "tx"), P(), P(), P(), P())
     out_specs = (P(None, "ty", "tx"), P())
+
+    def per_device(estimate, data, *rest):
+        planes, rows, cols = estimate.shape
+        members = sizes["ty"] * sizes["pat"]
+        fits = (
+            cols == members * TILE
+            and cols % LANES == 0
+            and rows % 8 == 0
+            and rows * sizes["ty"] <= 2 * TILE
+            and planes == sizes["pat"] * SUB
+        )
+        if fits:
+            return tiled_device(sizes, estimate, data, *rest)
+        return general_device(estimate, data, *rest)
+
     return jax.shard_map(
         per_device, mesh=mesh, in_specs=in_specs, out_specs=out_specs, check_vma=False
     )

time: 452 us -> 158 us (0.35); the launches traced: 443 us -> 158 us
  waiting for transfers between devices: 178 us -> 42.7 us
  matrix products: 83.5 us -> 0 us
  Pallas kernels: 0 us -> 58.7 us
  local copies, waits for them, and re-layouts: 52.9 us -> 5.31 us
  starting transfers between devices: 43.4 us -> 14.3 us
  other arithmetic: 24.9 us -> 5.68 us
  blocking collectives: 45 us -> 29.4 us
  between operations: 15.9 us -> 1.5 us
    psum x4 -> x0, waiting for transfers between devices: 142 us -> none  [the longest x3 86.2 us: per_device(): summed = lax.psum(contribution, 'pat')]
    dot_general x88 -> x0, matrix products: 83.5 us -> none  [the longest x77 63 us: lateral_pass(): jnp.dot(window, matrices[tap_row], preferred_element_type=jnp.float32)]
    pallas_call x0 -> x6, Pallas kernels: none -> 58.7 us  [the longest x1 22.6 us: tiled_device(): pl.pallas_call(functools.partial(first_kernel, nx, patterns, src_of), out...]
    psum x1 -> x0, blocking collectives: 45 us -> none  [per_device(): squares_list.append(lax.psum(local_square, ('ty', 'tx', 'pat')))]
    ppermute x20 -> x4, starting transfers between devices: 43.2 us -> 6.85 us  [the longest x2 4.26 us: tiled_device(): from_left = lax.ppermute(right, axes, to_right)]
    slice x24 -> x0, local copies, waits for them, and re-layouts: 32.4 us -> none  [the longest x8 15.8 us: lateral_pass(): window = padded[..., tap_row:tap_row + height, :]]
    all_to_all x0 -> x1, waiting for transfers between devices: none -> 28.6 us  [tiled_device(): mine = lax.all_to_all(message, ('ty', 'pat'), 0, 0, tiled=True)]
    all_to_all x0 -> x1, blocking collectives: none -> 23.8 us  [tiled_device(): incoming = lax.all_to_all(outgoing, ('ty', 'pat'), 0, 0, tiled=True)]
  transfers between devices with their start and end apart: 24 -> 5, of which waited for: 12 -> 4; matrix products, arithmetic and copies ran while one was open for 10% -> 3% of each run, Pallas kernels for 0% -> 1%
where the time goes in v1:
time: 158 us
  Pallas kernels  58.7 us (37%)
  waiting for transfers between devices  42.7 us (27%)
  blocking collectives  29.4 us (19%)
  starting transfers between devices  14.3 us (9%)
  other arithmetic  5.68 us (4%)
  local copies, waits for them, and re-layouts  5.31 us (3%)
    all_to_all x1, waiting for transfers between devices, tiled_device(): mine = lax.all_to_all(message, ('ty', 'pat'), 0, 0, tiled=True)  28.6 us
    all_to_all x1, blocking collectives, tiled_device(): incoming = lax.all_to_all(outgoing, ('ty', 'pat'), 0, 0, tiled=True)  23.8 us
    pallas_call x1, Pallas kernels, tiled_device(): pl.pallas_call(functools.partial(first_kernel, nx, patterns, src_of), out...  22.6 us
    pallas_call x1, Pallas kernels, tiled_device(): pl.pallas_call(functools.partial(second_kernel, nx, patterns), out_shape=...  18.9 us
    ppermute x2, waiting for transfers between devices, tiled_device(): from_right = lax.ppermute(left, axes, to_left)  7.8 us
    pallas_call x1, Pallas kernels, tiled_device(): pl.pallas_call(functools.partial(halo_kernel, src_of), out_shape=(shape((...  7.64 us
    all_to_all x1, starting transfers between devices, tiled_device(): mine = lax.all_to_all(message, ('ty', 'pat'), 0, 0, tiled=True)  7.42 us
    ppermute x2, waiting for transfers between devices, tiled_device(): from_left = lax.ppermute(right, axes, to_right)  6.35 us
  transfers between devices with their start and end apart: 5, of which 4 were waited for; matrix products, arithmetic and copies ran while one was open for 3% of the time, Pallas kernels for 1%

profile of v1, /device:TPU:0, one launch (start us, length us, event | category | flops | bytes accessed | tf_op | source)
XLA Modules:
  0.0 157.6 jit_solution(3192527400527828056)
XLA Ops:
  1.3 5.0 %pack.1 = f32[8,72,512]{2,1,0:T(8,128)} custom-call(s32[2]{0:T(128)} %pad_add_fusion.where_ref, f32[1024,256]{1,0:T(8,128)} %bitcast.20, f32[512,256]{1,0:T(8,128)} %bitcast.22), custom_call_target="tpu_custom_call" | custom-call | tf_op jit(solution)/shard_map/pack/pallas_call | solution.py:362
  6.3 7.4 %all-to-all-start = ((f32[8,72,512]{2,1,0:T(8,128)}), f32[8,72,512]{2,1,0:T(8,128)S(1)}, u32[]{:S(2)}, u32[]{:S(2)}) async-start(f32[8,72,512]{2,1,0:T(8,128)} %pack.1), calls=%async_computation | async-start | bytes 2359296 | tf_op jit(solution)/shard_map/all_to_all | solution.py:374
  14.6 28.6 %all-to-all-done.in_ref = f32[8,72,512]{2,1,0:T(8,128)S(1)} async-done(((f32[8,72,512]{2,1,0:T(8,128)}), f32[8,72,512]{2,1,0:T(8,128)S(1)}, u32[]{:S(2)}, u32[]{:S(2)}) %all-to-all-start) | async-done | bytes 1179680 | tf_op jit(solution)/shard_map/all_to_all | solution.py:374
  43.2 1.0 copy-done
  44.2 7.6 %edges.1 = (f32[288,512]{1,0:T(8,128)}, f32[288,512]{1,0:T(8,128)}) custom-call(f32[8,72,512]{2,1,0:T(8,128)} %copy-done), custom_call_target="tpu_custom_call" | custom-call | tf_op jit(solution)/shard_map/edges/pallas_call | solution.py:404
  51.8 1.3 collective-permute-start
  53.2 1.3 collective-permute-start.1
  55.5 2.2 %taps.1.w_ref = bf16[6,256,256]{2,1,0:T(8,128)(2,1)} custom-call(f32[9,9]{1,0:T(8,128)} %fusion.7.k_ref), custom_call_target="tpu_custom_call" | custom-call | tf_op jit(solution)/shard_map/taps/pallas_call | solution.py:377
  57.6 1.0 fusion.3.light_ref
  58.6 0.8 compare_select_fusion
  59.4 6.4 %collective-permute-done.from_left_ref = f32[288,512]{1,0:T(8,128)S(1)} collective-permute-done((f32[288,512]{1,0:T(8,128)}, f32[288,512]{1,0:T(8,128)S(1)}, u32[]{:S(2)}, u32[]{:S(2)}) %collective-permute-start) | collective-permute-done | bytes 589856 | tf_op jit(solution)/shard_map/ppermute | solution.py:411
  65.8 4.0 %collective-permute-done.1.from_right_ref = f32[288,512]{1,0:T(8,128)S(1)} collective-permute-done((f32[288,512]{1,0:T(8,128)}, f32[288,512]{1,0:T(8,128)S(1)}, u32[]{:S(2)}, u32[]{:S(2)}) %collective-permute-start.1) | collective-permute-done | bytes 589856 | tf_op jit(solution)/shard_map/ppermute | solution.py:412
  69.8 0.8 broadcast_in_dim.65.colsum_ref
  70.6 0.7 broadcast_in_dim.64.wave_ref
  71.3 22.6 %first.1 = (f32[8,256,256]{2,1,0:T(8,128)}, f32[8,32,256]{2,1,0:T(8,128)}, f32[32,512]{1,0:T(8,128)}, f32[32,512]{1,0:T(8,128)}, f32[2,8,256]{2,1,0:T(8,128)}) custom-call(s32[2]{0:T(128)} %pad_add_fusion.where_ref, bf16[6,256,256]{2,1,0:T(8,128)(2,1)} %taps.1.w_ref, bf16[256,256]{1,0:T(8,128)(2,1)} %get-tuple-element.26.ax_fwd, ...), custom_call_target="tpu_custom_call" | custom-call | tf_op jit(solution)/shard_map/first/pallas_call | solution.py:422
  93.9 3.0 %collective-permute-start.2 = (f32[32,512]{1,0:T(8,128)}, f32[32,512]{1,0:T(8,128)S(1)}, u32[]{:S(2)}, u32[]{:S(2)}) collective-permute-start(f32[32,512]{1,0:T(8,128)} %get-tuple-element.15), channel_id=1, source_target_pairs={{0,1},{1,2},{2,3},{3,19},{19,18},{18,17},{17,16},{16,4},{4,5},{5,6... | collective-permute-start | bytes 196616 | tf_op jit(solution)/shard_map/ppermute | solution.py:436
  96.8 1.3 collective-permute-start.3
  99.4 3.8 %collective-permute-done.3.from_right_ref = f32[32,512]{1,0:T(8,128)S(1)} collective-permute-done((f32[32,512]{1,0:T(8,128)}, f32[32,512]{1,0:T(8,128)S(1)}, u32[]{:S(2)}, u32[]{:S(2)}) %collective-permute-start.3) | collective-permute-done | bytes 65568 | tf_op jit(solution)/shard_map/ppermute | solution.py:437
  103.8 18.9 %second.1 = (f32[2,32,512]{2,1,0:T(8,128)}, f32[2,8,256]{2,1,0:T(8,128)}) custom-call(s32[2]{0:T(128)} %pad_add_fusion.where_ref, bf16[6,256,256]{2,1,0:T(8,128)(2,1)} %taps.1.w_ref, bf16[256,256]{1,0:T(8,128)(2,1)} %get-tuple-element.26.ax_fwd, bf16[256,256]{1,0:T(8,128)(2,1)} %get-tuple-element.25.ax_bwd, f32[8,8,256]{2,1,0:T(8,128)} %fusion.3.light_ref, ...), custom_call_target="tpu_custom_call" | custom-call | tf_op jit(solution)/shard_map/second/pallas_call | solution.py:438
  122.8 0.8 maximum_reduce_fusion
  123.8 5.6 %all-reduce.1 = f32[16]{0:T(128)S(1)} all-reduce(f32[16]{0:T(128)S(1)} %dynamic-update-slice), channel_id=2, replica_groups=mesh['ty'=2,'tx'=4,'pat'=4] {'tx'}, use_global_device_ids=true, to_apply=%add.1 | all-reduce | flops 16 | bytes 128
  129.6 0.9 pad_maximum_fusion
  130.6 23.8 %all_to_all.10.in_ref = f32[8,40,512]{2,1,0:T(8,128)S(1)} all-to-all(f32[8,40,512]{2,1,0:T(8,128)S(1)} %bitcast.19), channel_id=1, replica_groups=mesh['ty'=2,'tx'=4,'pat'=4] {'ty','pat'}, dimensions={0} | all-to-all | bytes 1310720 | tf_op jit(solution)/shard_map/all_to_all | solution.py:453
  155.3 2.4 %unpack.1 = f32[512,256]{1,0:T(8,128)} custom-call(f32[8,40,512]{2,1,0:T(8,128)} %copy-done.1), custom_call_target="tpu_custom_call" | custom-call | tf_op jit(solution)/shard_map/unpack/pallas_call | solution.py:454
  (50 shorter events, 5.0 us)
Async XLA Ops:
  6.3 7.5 %copy-start.9 = (s32[2,8]{1,0:T(2,128)S(1)}, s32[2,8]{1,0:T(2,128)}, u32[]{:S(2)}) copy-start(s32[2,8]{1,0:T(2,128)} %param.11) | copy-start | bytes 196
  6.3 7.5 %copy-start.8 = (f32[9,9]{1,0:T(8,128)S(1)}, f32[9,9]{1,0:T(8,128)}, u32[]{:S(2)}) copy-start(f32[9,9]{1,0:T(8,128)} %param.9) | copy-start | bytes 976
  6.3 7.5 %copy-start.10 = (s32[9]{0:T(128)S(1)}, s32[9]{0:T(128)}, u32[]{:S(2)}) copy-start(s32[9]{0:T(128)} %param.10) | copy-start | bytes 112
  6.3 8.3 %copy-start.6 = (f32[32,32]{1,0:T(8,128)S(1)}, f32[32,32]{1,0:T(8,128)}, u32[]{:S(2)}) copy-start(f32[32,32]{1,0:T(8,128)} %param.8) | copy-start | bytes 12292
  6.3 36.9 %all-to-all-start = ((f32[8,72,512]{2,1,0:T(8,128)}), f32[8,72,512]{2,1,0:T(8,128)S(1)}, u32[]{:S(2)}, u32[]{:S(2)}) async-start(f32[8,72,512]{2,1,0:T(8,128)} %pack.1), calls=%async_computation | async-start | bytes 2359296 | tf_op jit(solution)/shard_map/all_to_all | solution.py:374
  43.2 1.0 copy-start
  51.8 13.9 %collective-permute-start = (f32[288,512]{1,0:T(8,128)}, f32[288,512]{1,0:T(8,128)S(1)}, u32[]{:S(2)}, u32[]{:S(2)}) collective-permute-start(f32[288,512]{1,0:T(8,128)} %get-tuple-element.11), channel_id=1, source_target_pairs={{0,1},{1,2},{2,3},{3,19},{19,18},{18,17},{17,16},{16,4},{4,5},{5,6... | collective-permute-start | bytes 1769480 | tf_op jit(solution)/shard_map/ppermute | solution.py:411
  53.2 16.6 %collective-permute-start.1 = (f32[288,512]{1,0:T(8,128)}, f32[288,512]{1,0:T(8,128)S(1)}, u32[]{:S(2)}, u32[]{:S(2)}) collective-permute-start(f32[288,512]{1,0:T(8,128)} %get-tuple-element.12), channel_id=1, source_target_pairs={{1,0},{2,1},{3,2},{19,3},{18,19},{17,18},{16,17},{4,16},{5,4},{6,5... | collective-permute-start | bytes 1769480 | tf_op jit(solution)/shard_map/ppermute | solution.py:412
  65.8 5.5 %copy-start.2 = (f32[288,512]{1,0:T(8,128)}, f32[288,512]{1,0:T(8,128)S(1)}, u32[]{:S(2)}) copy-start(f32[288,512]{1,0:T(8,128)S(1)} %collective-permute-done.from_left_ref) | copy-start | bytes 1769476
  69.8 1.5 copy-start.3
  71.3 26.9 %copy-start.11 = (u32[32]{0:T(128)S(1)}, u32[32]{0:T(128)}, u32[]{:S(2)}) copy-start(u32[32]{0:T(128)} %constant.131) | copy-start | bytes 388
  93.9 5.5 %collective-permute-start.2 = (f32[32,512]{1,0:T(8,128)}, f32[32,512]{1,0:T(8,128)S(1)}, u32[]{:S(2)}, u32[]{:S(2)}) collective-permute-start(f32[32,512]{1,0:T(8,128)} %get-tuple-element.15), channel_id=1, source_target_pairs={{0,1},{1,2},{2,3},{3,19},{19,18},{18,17},{17,16},{16,4},{4,5},{5,6... | collective-permute-start | bytes 196616 | tf_op jit(solution)/shard_map/ppermute | solution.py:436
  96.8 6.4 %collective-permute-start.3 = (f32[32,512]{1,0:T(8,128)}, f32[32,512]{1,0:T(8,128)S(1)}, u32[]{:S(2)}, u32[]{:S(2)}) collective-permute-start(f32[32,512]{1,0:T(8,128)} %get-tuple-element.16), channel_id=1, source_target_pairs={{1,0},{2,1},{3,2},{19,3},{18,19},{17,18},{16,17},{4,16},{5,4},{6,5... | collective-permute-start | bytes 196616 | tf_op jit(solution)/shard_map/ppermute | solution.py:437
  99.4 3.8 %copy-start.4 = (f32[32,512]{1,0:T(8,128)}, f32[32,512]{1,0:T(8,128)S(1)}, u32[]{:S(2)}) copy-start(f32[32,512]{1,0:T(8,128)S(1)} %collective-permute-done.2.from_left_ref) | copy-start | bytes 196612
  103.2 0.6 copy-start.5
  103.8 18.9 %copy-start.7 = (f32[2,8,256]{2,1,0:T(8,128)S(1)}, f32[2,8,256]{2,1,0:T(8,128)}, u32[]{:S(2)}) copy-start(f32[2,8,256]{2,1,0:T(8,128)} %get-tuple-element.18) | copy-start | bytes 49156
  154.4 0.9 copy-start.1

commit v2 on v0

--- a/solution.py
+++ b/solution.py
@@ -1,15 +1,545 @@
+import functools
 import math
 
 import jax
 import jax.numpy as jnp
+import numpy as np
 from jax import lax
+from jax.experimental import pallas as pl
+from jax.experimental.pallas import tpu as pltpu
 from jax.sharding import PartitionSpec as P
 
 RADIUS = 4
+TAPS = 2 * RADIUS + 1
 ITERS = 4
-
-
 TWO_PI = 2.0 * math.pi
+
+TILE = 32
+HALO = 16
+GROUP = TILE + 2 * HALO
+ROWS_BLOCK = RADIUS
+BLOCK = ROWS_BLOCK * GROUP
+LANES = 128
+SUB = 8
+QUAD_ROWS = (0, 2, 1, 3)
+CHUNK = 4
+OFFSET = 1 << 20
+F32 = jnp.float32
+BF16 = jnp.bfloat16
+
+
+def lane_iota(shape):
+    return lax.broadcasted_iota(jnp.int32, shape, len(shape) - 1)
+
+
+def column_of(lane):
+    inner = lane % GROUP
+    return jnp.where(inner < TILE + HALO, inner, inner - GROUP)
+
+
+def roll(x, shift):
+    shift = shift % LANES
+    return x if shift == 0 else pltpu.roll(x, shift, 1)
+
+
+def quad_transpose(v, lane):
+    group = lane // TILE
+    out = []
+    for t in range(4):
+        value = roll(v[0], -TILE * t)
+        for g in range(1, 4):
+            value = jnp.where(group == g, roll(v[g], TILE * (g - t)), value)
+        out.append(value)
+    return out
+
+
+def pack_half(dest_of_tile, rows, half, groups, src_ref, out_ref):
+    lane = lane_iota((SUB, LANES))
+    tiles_half = LANES // TILE
+    for i in range(groups):
+        for quad in range(rows // 4):
+            v = [src_ref[pl.ds(i * rows * SUB + 4 * quad + r, SUB, stride=rows), :] for r in QUAD_ROWS]
+            for t, piece in enumerate(quad_transpose(v, lane)):
+                dest = dest_of_tile[half * tiles_half + t]
+                out_ref[dest, i * SUB : (i + 1) * SUB, quad * LANES : (quad + 1) * LANES] = piece
+
+
+def pack_kernel(dest_of_tile, rows, data_ref, out_ref):
+    for half in range(len(dest_of_tile) * TILE // LANES):
+
+        @pl.when(pl.program_id(0) == half)
+        def _(half=half):
+            pack_half(dest_of_tile, rows, half, data_ref.shape[0] // (rows * SUB), data_ref, out_ref)
+
+
+def estimate_kernel(dest_of_tile, rows, pat, est_ref, out_ref, all_ref):
+    halves = len(dest_of_tile) * TILE // LANES
+    for half in range(halves):
+
+        @pl.when(pl.program_id(0) == half)
+        def _(half=half):
+            pack_half(dest_of_tile, rows, half, est_ref.shape[0] // (rows * SUB), est_ref, all_ref)
+            if half == halves - 1:
+                for i in range(out_ref.shape[0]):
+                    out_ref[i] = all_ref[i * pat + lax.axis_index("pat")]
+
+
+def edge_messages(pieces, lane):
+    left = right = None
+    for u, (v, offset) in enumerate(pieces):
+        slot = (lane // HALO) % 4 == u
+        l_u, r_u = roll(v, HALO * u - offset), roll(v, HALO * (u - 1) - offset)
+        left = l_u if left is None else jnp.where(slot, l_u, left)
+        right = r_u if right is None else jnp.where(slot, r_u, right)
+    return left, right
+
+
+def edges_kernel(src_of, in_ref, left_ref, right_ref):
+    lane = lane_iota((SUB, LANES))
+    ty, pat = src_of
+    groups = in_ref.shape[1] // SUB
+    per_ty = in_ref.shape[2] // LANES // 2
+    for k in range(pat):
+        for g in range(groups):
+            row = slice((k * groups + g) * SUB, (k * groups + g + 1) * SUB)
+            for i in range(ty):
+                for pair in range(per_ty):
+                    pieces = []
+                    for q in (2 * pair, 2 * pair + 1):
+                        v = in_ref[i * pat + k, g * SUB : (g + 1) * SUB, q * LANES : (q + 1) * LANES]
+                        pieces += [(v, 0), (v, TILE)]
+                    left, right = edge_messages(pieces, lane)
+                    vreg = i * per_ty + pair
+                    left_ref[row, vreg * LANES : (vreg + 1) * LANES] = left
+                    right_ref[row, vreg * LANES : (vreg + 1) * LANES] = right
+
+
+def unpack_wide(src_of, in_ref, from_left_ref, from_right_ref, out_ref):
+    lane = lane_iota((SUB, LANES))
+    ty, pat = src_of
+    groups = in_ref.shape[1] // SUB
+    per_ty = in_ref.shape[2] // LANES // 2
+    for k in range(pat):
+        for g in range(groups):
+            row = slice((k * groups + g) * SUB, (k * groups + g + 1) * SUB)
+            for i in range(ty):
+                for pair in range(per_ty):
+                    vreg = i * per_ty + pair
+                    from_left = from_left_ref[row, vreg * LANES : (vreg + 1) * LANES]
+                    from_right = from_right_ref[row, vreg * LANES : (vreg + 1) * LANES]
+                    own = []
+                    for q in (2 * pair, 2 * pair + 1):
+                        v = in_ref[i * pat + k, g * SUB : (g + 1) * SUB, q * LANES : (q + 1) * LANES]
+                        own += [v, roll(v, -TILE)]
+                    for u in range(4):
+                        m = 4 * vreg + u
+                        out_ref[m // 2, row, (m % 2) * LANES : (m % 2 + 1) * LANES] = with_halo(
+                            own[u], u, from_right, from_left, lane
+                        )
+
+
+def with_halo(own, u, from_right, from_left, lane):
+    inner = lane % GROUP
+    value = jnp.where(inner < TILE, own, roll(from_right, HALO * (2 - u)))
+    return jnp.where(inner < TILE + HALO, value, roll(from_left, HALO * (3 - u)))
+
+
+def tables_kernel(tile_of, k_ref, radius_ref, codes_ref, axial_ref, w_ref, fwd_ref, bwd_ref, light_ref):
+    lane = lane_iota((GROUP, LANES))
+    row = lax.broadcasted_iota(jnp.int32, (GROUP, LANES), 0)
+    tap = column_of(row) - column_of(lane) + RADIUS
+    first = lane < GROUP
+    hit = [tap == j for j in range(TAPS)]
+    nothing = jnp.zeros((GROUP, LANES), BF16)
+
+    def scalar(flip, i, j):
+        if i < 0 or i >= TAPS:
+            return jnp.float32(0.0)
+        if flip:
+            i, j = TAPS - 1 - i, TAPS - 1 - j
+        return jnp.where(abs(j - RADIUS) <= radius_ref[i], k_ref[i, j], 0.0)
+
+    for flip in range(2):
+        for i0 in range(-2, TAPS + 3):
+            value = jnp.zeros((GROUP, LANES), F32)
+            if 0 <= i0 <= TAPS:
+                for j in range(TAPS):
+                    both = jnp.where(first, scalar(flip, i0, j), scalar(flip, i0 - 1, j))
+                    value = jnp.where(hit[j], both, value)
+            value = value.astype(BF16)
+            for k in range(3):
+                for r in range(ROWS_BLOCK):
+                    for q in range(ROWS_BLOCK // 2):
+                        if ROWS_BLOCK * (k - 1) + r - 2 * q + RADIUS == i0:
+                            w_ref[
+                                3 * flip + k,
+                                r * GROUP : (r + 1) * GROUP,
+                                q * LANES : (q + 1) * LANES,
+                            ] = value
+
+    planes, rows = axial_ref.shape[0], fwd_ref.shape[0]
+    axial = axial_ref[...].astype(BF16)
+    pick = lax.broadcasted_iota(jnp.int32, (planes, rows), 1) % planes
+    pick = (pick == lax.broadcasted_iota(jnp.int32, (planes, rows), 0)).astype(F32).astype(BF16)
+    plain = jnp.dot(axial, pick, preferred_element_type=F32)
+    turned = lax.dot_general(axial, pick, (((0,), (0,)), ((), ())), preferred_element_type=F32)
+    column = lax.broadcasted_iota(jnp.int32, (planes, rows), 1)
+    for p in range(rows // planes):
+        here = column // planes == p
+        fwd_ref[p * planes : (p + 1) * planes] = jnp.where(here, plain, 0.0).astype(BF16)
+    span = 3 * planes
+    for h in range(2):
+        here = (column >= h * span) & (column < (h + 1) * span)
+        bwd_ref[h * planes : (h + 1) * planes] = jnp.where(here, turned, 0.0).astype(BF16)[:, : 2 * span]
+
+    col = column_of(lane_iota((1, BLOCK)))
+    within = lane_iota((1, BLOCK)) // GROUP
+    x = tile_of() * TILE + col
+    cosines = [0.7 * math.cos(TWO_PI * m / 5.0) for m in range(5)]
+    patterns = light_ref.shape[1]
+    for p in range(patterns):
+        angle, phase = codes_ref[0, p], codes_ref[1, p]
+        step_col = jnp.where(angle == 0, 2, -1)
+        step_row = jnp.where(angle == 0, 0, jnp.where(angle == 1, 2, -2))
+        for b in range(light_ref.shape[0]):
+            y = within + b * ROWS_BLOCK
+            turn = lax.rem(step_col * x + step_row * y + phase + 5 * OFFSET, 5)
+            value = jnp.full((1, BLOCK), cosines[0], F32)
+            for m in range(1, 5):
+                value = jnp.where(turn == m, cosines[m], value)
+            light_ref[b, p : p + 1] = value
+
+
+def lateral(src_ref, w_ref, flip, b, count):
+    total = None
+    for k in range(3):
+        v = src_ref[b + k : b + k + count]
+        part = jnp.dot(v.reshape(-1, BLOCK), w_ref[3 * flip + k], preferred_element_type=F32)
+        total = part if total is None else total + part
+    return total.reshape(count, -1, BLOCK)
+
+
+def split3(v):
+    high = v.astype(BF16)
+    rest = v - high.astype(F32)
+    mid = rest.astype(BF16)
+    return high, mid, (rest - mid.astype(F32)).astype(BF16)
+
+
+class Step:
+    def __init__(self, nx, tile_of, w_ref, ax_fwd, ax_bwd, light_ref, wave_ref):
+        self.w, self.ax_fwd, self.ax_bwd, self.light, self.wave = w_ref, ax_fwd, ax_bwd, light_ref, wave_ref
+        self.blocks, self.patterns = light_ref.shape[0], light_ref.shape[1]
+        self.planes = wave_ref.shape[0]
+        self.col = column_of(lane_iota((1, BLOCK)))
+        place = tile_of() * TILE + self.col
+        self.inside = (place >= 0) & (place < nx)
+
+    def reach(self, width):
+        return self.inside & (self.col >= -width) & (self.col < TILE + width)
+
+    def clear_ends(self, ref):
+        ref[0] = jnp.zeros(ref.shape[1:], BF16)
+        ref[self.blocks + 1] = jnp.zeros(ref.shape[1:], BF16)
+
+    def normalizer(self, norm_ref):
+        depth = self.ax_bwd.shape[1]
+        ones = lax.broadcasted_iota(jnp.int32, (depth, BLOCK), 0) < self.planes
+        ones = jnp.where(ones, 1.0, 0.0).astype(BF16)
+        colsum = jnp.dot(self.ax_bwd[...], ones, preferred_element_type=F32)[: self.planes]
+        ones = jnp.broadcast_to(jnp.where(self.inside, 1.0, 0.0), (2 * SUB, BLOCK)).astype(BF16)
+        parts = [jnp.dot(ones, self.w[3 + k], preferred_element_type=F32) for k in range(3)]
+        for b in range(self.blocks):
+            total = sum(parts[k] for k in range(3) if 0 <= b + k - 1 < self.blocks)
+            cover = total.astype(BF16).astype(F32)[0:1]
+            lat_sum = jnp.sum(self.light[b], axis=0, keepdims=True)
+            norm_ref[b] = colsum * cover * (float(self.patterns) + lat_sum * self.wave[...])
+
+    def blur(self, obj_ref, stage_ref):
+        for b in range(self.blocks):
+            lighting = 1.0 + self.light[b][:, None, :] * self.wave[...][None]
+            lit = (lighting * obj_ref[b][None]).astype(BF16).reshape(-1, BLOCK)
+            stage_ref[b + 1] = jnp.dot(self.ax_fwd[...], lit, preferred_element_type=F32).astype(BF16)
+
+    def compare(self, stage_ref, data_ref, quot_ref, width, predicted_ref=None):
+        ok = self.reach(width)[None]
+        acc = jnp.zeros((SUB, BLOCK), F32)
+        for b in range(0, self.blocks, CHUNK):
+            if predicted_ref is None:
+                predicted = lateral(stage_ref, self.w, 0, b, CHUNK)
+            else:
+                predicted = predicted_ref[b : b + CHUNK]
+            data = data_ref[b : b + CHUNK]
+            miss = data - predicted
+            acc = acc + jnp.sum((miss * miss).reshape(-1, SUB, BLOCK), axis=0)
+            quot_ref[b + 1 : b + 1 + CHUNK] = jnp.where(ok, data / predicted, 0.0).astype(BF16)
+        row = jnp.sum(jnp.where((self.col >= 0) & (self.col < TILE), acc, 0.0), axis=0, keepdims=True)
+        return sum(row[:, h * LANES : (h + 1) * LANES] for h in range(BLOCK // LANES))
+
+    def update(self, quot_ref, obj_ref, norm_ref, width):
+        ok = self.reach(width)
+        for b0 in range(0, self.blocks, CHUNK):
+            back = lateral(quot_ref, self.w, 1, b0, CHUNK).astype(BF16)
+            for b in range(b0, b0 + CHUNK):
+                part = back[b - b0].astype(F32).reshape(self.patterns, self.planes, BLOCK)
+                plain = jnp.sum(part, axis=0)
+                waved = jnp.sum(self.light[b][:, None, :] * part, axis=0)
+                stack = jnp.concatenate(split3(plain) + split3(waved), axis=0)
+                both = jnp.dot(self.ax_bwd[...], stack, preferred_element_type=F32)
+                summed = both[: self.planes] + self.wave[...] * both[self.planes :]
+                obj_ref[b] = jnp.where(ok, obj_ref[b] * summed / norm_ref[b], 0.0)
+
+
+def put_halo(own_ref, from_left_ref, from_right_ref, out_ref):
+    lane = lane_iota((SUB, LANES))
+    for z in range(0, out_ref.shape[1], SUB):
+        for vreg in range(out_ref.shape[0] // 2):
+            from_left = from_left_ref[z : z + SUB, vreg * LANES : (vreg + 1) * LANES]
+            from_right = from_right_ref[z : z + SUB, vreg * LANES : (vreg + 1) * LANES]
+            for u in range(4):
+                m = 4 * vreg + u
+                at = (m // 2, slice(z, z + SUB), slice((m % 2) * LANES, (m % 2 + 1) * LANES))
+                out_ref[at] = with_halo(own_ref[at], u, from_right, from_left, lane)
+
+
+def forward_kernel(nx, tile_of, src_of, w_ref, ax_fwd, ax_bwd, light_ref, wave_ref,
+                   est_ref, from_left_ref, from_right_ref, obj_ref, norm_ref, predicted_ref, stage_ref):
+    unpack_wide(src_of, est_ref, from_left_ref, from_right_ref, obj_ref)
+    step = Step(nx, tile_of, w_ref, ax_fwd, ax_bwd, light_ref, wave_ref)
+    step.normalizer(norm_ref)
+    step.clear_ends(stage_ref)
+    step.blur(obj_ref, stage_ref)
+    for b in range(0, step.blocks, CHUNK):
+        predicted_ref[b : b + CHUNK] = lateral(stage_ref, w_ref, 0, b, CHUNK)
+
+
+def first_kernel(nx, tile_of, src_of, w_ref, ax_fwd, ax_bwd, light_ref, wave_ref, norm_ref, obj_in_ref,
+                 predicted_ref, in_ref, from_left_ref, from_right_ref, data_ref, obj_ref, left_ref, right_ref,
+                 sq_ref, stage_ref, quot_ref):
+    unpack_wide(src_of, in_ref, from_left_ref, from_right_ref, data_ref)
+    step = Step(nx, tile_of, w_ref, ax_fwd, ax_bwd, light_ref, wave_ref)
+    step.clear_ends(stage_ref)
+    step.clear_ends(quot_ref)
+    obj_ref[...] = obj_in_ref[...]
+    sq_ref[...] = jnp.zeros(sq_ref.shape, F32)
+    sq_ref[0:1] = step.compare(None, data_ref, quot_ref, 12, predicted_ref)
+    step.update(quot_ref, obj_ref, norm_ref, 8)
+    step.blur(obj_ref, stage_ref)
+    sq_ref[1:2] = step.compare(stage_ref, data_ref, quot_ref, 4)
+    step.update(quot_ref, obj_ref, norm_ref, 0)
+
+    lane = lane_iota((SUB, LANES))
+    for z in range(0, step.planes, SUB):
+        for vreg in range(step.blocks // 2):
+            pieces = []
+            for u in range(4):
+                m = 4 * vreg + u
+                pieces.append((obj_ref[m // 2, z : z + SUB, (m % 2) * LANES : (m % 2 + 1) * LANES], 0))
+            left, right = edge_messages(pieces, lane)
+            left_ref[z : z + SUB, vreg * LANES : (vreg + 1) * LANES] = left
+            right_ref[z : z + SUB, vreg * LANES : (vreg + 1) * LANES] = right
+
+
+def second_kernel(nx, tile_of, src_of, w_ref, ax_fwd, ax_bwd, light_ref, wave_ref, norm_ref, data_ref,
+                  obj_in_ref, from_left_ref, from_right_ref, sq_in_ref, out_ref, obj_ref, stage_ref, quot_ref):
+    put_halo(obj_in_ref, from_left_ref, from_right_ref, obj_ref)
+    step = Step(nx, tile_of, w_ref, ax_fwd, ax_bwd, light_ref, wave_ref)
+    step.clear_ends(stage_ref)
+    step.clear_ends(quot_ref)
+    squares = [sq_in_ref[0:1], sq_in_ref[1:2]]
+    for quot_width, obj_width in ((12, 8), (4, 0)):
+        step.blur(obj_ref, stage_ref)
+        squares.append(step.compare(stage_ref, data_ref, quot_ref, quot_width))
+        step.update(quot_ref, obj_ref, norm_ref, obj_width)
+
+    ty, pat = src_of
+    quads = step.blocks // ty
+    lane = lane_iota((SUB, LANES))
+    own = (lane // TILE) % 2 == 0
+    last = jnp.concatenate(squares + [jnp.zeros((SUB - len(squares), LANES), F32)], axis=0)
+    for i in range(ty):
+        for k in range(pat):
+            out_ref[i * pat + k, quads * step.planes : quads * step.planes + SUB] = last
+        for q in range(quads):
+            for z in range(0, step.planes, SUB):
+                v0 = obj_ref[i * quads + q, z : z + SUB, 0:LANES]
+                v1 = obj_ref[i * quads + q, z : z + SUB, LANES : 2 * LANES]
+                v = jnp.where(own, v0, roll(v1, TILE))
+                for k in range(pat):
+                    out_ref[i * pat + k, q * step.planes + z : q * step.planes + z + SUB] = v
+
+
+def final_kernel(dest_of_tile, rows, in_ref, out_ref, sq_ref):
+    lane = lane_iota((SUB, LANES))
+    planes = out_ref.shape[0] // rows
+    tiles_half = LANES // TILE
+    quads = rows // 4
+    sq_ref[...] = jnp.sum(in_ref[:, quads * planes : quads * planes + SUB], axis=0)
+    for half in range(len(dest_of_tile) // tiles_half):
+
+        @pl.when(pl.program_id(0) == half)
+        def _(half=half):
+            for z in range(0, planes, SUB):
+                for quad in range(quads):
+                    row = quad * planes + z
+                    v = [in_ref[dest_of_tile[half * tiles_half + t], row : row + SUB] for t in range(tiles_half)]
+                    for g, piece in enumerate(quad_transpose(v, lane)):
+                        out_ref[pl.ds(z * rows + 4 * quad + QUAD_ROWS[g], SUB, stride=rows), :] = piece
+
+
+def masked_kernel(lateral_kernel, psf_radius):
+    offsets = jnp.arange(TAPS) - RADIUS
+    within = jnp.abs(offsets)[None, :] <= psf_radius[:, None]
+    return jnp.where(within, lateral_kernel, jnp.zeros_like(lateral_kernel)).astype(BF16)
+
+
+def shape(dims, dtype=F32):
+    return jax.ShapeDtypeStruct(dims, dtype)
+
+
+VMEM = pl.BlockSpec(memory_space=pltpu.VMEM)
+SMEM = pl.BlockSpec(memory_space=pltpu.SMEM)
+
+
+def tiled_device(sizes, estimate, data, axial, lateral_kernel, psf_radius, pattern_codes):
+    ty, tx, pat = sizes["ty"], sizes["tx"], sizes["pat"]
+    planes, rows, cols = estimate.shape
+    pat_local = data.shape[0]
+    patterns = pat_local * pat
+    ny, nx = rows * ty, cols * tx
+    members = ty * pat
+    blocks = ny // ROWS_BLOCK
+    axes = ("ty", "tx", "pat")
+
+    owner = [(i, k if i % 2 == 0 else pat - 1 - k) for i in range(ty) for k in range(pat)]
+    dest_of_tile = [i * pat + k for i, k in owner]
+    order = [(i * tx + j) * pat + k for j in range(tx) for i, k in owner]
+    to_right = [(a, b) for a, b in zip(order[:-1], order[1:])]
+    to_left = [(b, a) for a, b in to_right]
+    src_of = (ty, pat)
+
+    ti = lax.axis_index("ty")
+
+    def tile_of():
+        i, j, k = (lax.axis_index(a) for a in axes)
+        return j * members + i * pat + jnp.where(lax.rem(i, 2) == 0, k, pat - 1 - k)
+
+    halves = cols // LANES
+    piece_lanes = rows * TILE
+    halo_lanes = ny * HALO
+
+    def whole(dims):
+        return pl.BlockSpec(dims, lambda h: (0,) * len(dims))
+
+    def half_columns(height):
+        return pl.BlockSpec((height, LANES), lambda h: (0, h))
+
+    def edges(pieces, name):
+        out = shape((pieces.shape[1] * pieces.shape[0] // ty, halo_lanes))
+        return pl.pallas_call(
+            functools.partial(edges_kernel, (ty, pieces.shape[0] // ty)),
+            out_shape=(out, out),
+            in_specs=[VMEM],
+            out_specs=(VMEM,) * 2,
+            name=name,
+        )(pieces)
+
+    def swap_edges(left, right):
+        return lax.ppermute(right, axes, to_right), lax.ppermute(left, axes, to_left)
+
+    message = pl.pallas_call(
+        functools.partial(pack_kernel, dest_of_tile, rows),
+        out_shape=shape((members, pat_local * planes, piece_lanes)),
+        grid=(halves,),
+        in_specs=[half_columns(data.size // cols)],
+        out_specs=whole((members, pat_local * planes, piece_lanes)),
+        name="pack",
+    )(data.reshape(-1, cols))
+    message, estimate = lax.optimization_barrier((message, estimate))
+    mine = lax.all_to_all(message, ("ty", "pat"), 0, 0, tiled=True)
+
+    pieces = pl.pallas_call(
+        functools.partial(estimate_kernel, dest_of_tile, rows, pat),
+        out_shape=shape((ty, planes, piece_lanes)),
+        grid=(halves,),
+        in_specs=[half_columns(planes * rows)],
+        out_specs=whole((ty, planes, piece_lanes)),
+        scratch_shapes=[pltpu.VMEM((members, planes, piece_lanes), F32)],
+        name="prep_estimate",
+    )(estimate.reshape(-1, cols))
+    tile_rows = [lax.dynamic_index_in_dim(pieces, ti, 0, keepdims=False)]
+    for shift in range(1, ty):
+        sent = lax.dynamic_index_in_dim(pieces, (ti + shift) % ty, 0, keepdims=False)
+        tile_rows.append(lax.ppermute(sent, "ty", [(i, (i + shift) % ty) for i in range(ty)]))
+    tile_rows = jnp.stack(tile_rows)
+    tile_rows = jnp.stack(
+        [lax.dynamic_index_in_dim(tile_rows, (ti - i) % ty, 0, keepdims=False) for i in range(ty)]
+    )
+    est_left, est_right = swap_edges(*edges(tile_rows, "prep_edges"))
+
+    weights, ax_fwd, ax_bwd, light = pl.pallas_call(
+        functools.partial(tables_kernel, tile_of),
+        out_shape=(
+            shape((6, BLOCK, BLOCK), BF16),
+            shape((patterns * planes, patterns * planes), BF16),
+            shape((2 * planes, 6 * planes), BF16),
+            shape((blocks, patterns, BLOCK)),
+        ),
+        in_specs=[SMEM] * 3 + [VMEM],
+        out_specs=(VMEM,) * 4,
+        name="tables",
+    )(lateral_kernel, psf_radius, pattern_codes, axial)
+    wave = np.cos(np.arange(planes, dtype=np.float32) * np.float32(TWO_PI * 3.0 / planes))
+    wave = jnp.asarray(np.ascontiguousarray(np.broadcast_to(wave[:, None], (planes, BLOCK))))
+
+    object_shape = shape((blocks, planes, BLOCK))
+    field_shape = shape((blocks, patterns * planes, BLOCK))
+    object_scratch = pltpu.VMEM(object_shape.shape, F32)
+    stage = pltpu.VMEM((blocks + 2, patterns * planes, BLOCK), BF16)
+    table_specs = [VMEM] * 5
+    mine, est_left, est_right, weights = lax.optimization_barrier((mine, est_left, est_right, weights))
+    from_left, from_right = swap_edges(*edges(mine, "edges"))
+    tables = (weights, ax_fwd, ax_bwd, light, wave)
+    current, norm, predicted = pl.pallas_call(
+        functools.partial(forward_kernel, nx, tile_of, (ty, 1)),
+        out_shape=(object_shape, object_shape, field_shape),
+        in_specs=table_specs + [VMEM] * 3,
+        out_specs=(VMEM,) * 3,
+        scratch_shapes=[stage],
+        name="forward",
+    )(*tables, tile_rows, est_left, est_right)
+
+    edge_shape = shape((planes, halo_lanes))
+    data_all, current, left, right, sq_first = pl.pallas_call(
+        functools.partial(first_kernel, nx, tile_of, src_of),
+        out_shape=(field_shape, object_shape, edge_shape, edge_shape, shape((SUB, LANES))),
+        in_specs=table_specs + [VMEM] * 6,
+        out_specs=(VMEM,) * 5,
+        scratch_shapes=[stage, stage],
+        name="first",
+    )(*tables, norm, current, predicted, mine, from_left, from_right)
+    from_left, from_right = swap_edges(left, right)
+    outgoing = pl.pallas_call(
+        functools.partial(second_kernel, nx, tile_of, src_of),
+        out_shape=shape((members, rows // 4 * planes + SUB, LANES)),
+        in_specs=table_specs + [VMEM] * 6,
+        out_specs=VMEM,
+        scratch_shapes=[object_scratch, stage, stage],
+        name="second",
+    )(*tables, norm, data_all, current, from_left, from_right, sq_first)
+
+    incoming = lax.all_to_all(outgoing, ("ty", "pat"), 0, 0, tiled=True)
+    result, squares = pl.pallas_call(
+        functools.partial(final_kernel, dest_of_tile, rows),
+        out_shape=(shape((planes * rows, cols)), shape((SUB, LANES))),
+        grid=(halves,),
+        in_specs=[whole(incoming.shape)],
+        out_specs=(half_columns(planes * rows), whole((SUB, LANES))),
+        name="unpack",
+    )(incoming)
+    squares = lax.psum(jnp.sum(squares[:ITERS], axis=1), "tx")
+    cell_count = float(patterns * planes * ny * nx)
+    return result.reshape(estimate.shape), jnp.sqrt(squares / cell_count)
 
 
 def extended(block, sides, width):
@@ -39,12 +569,6 @@
     return 1.0 + 0.7 * lateral_wave[:, None, :, :] * axial_wave[None, :, None, None]
 
 
-def masked_kernel(lateral_kernel, psf_radius):
-    offsets = jnp.arange(2 * RADIUS + 1) - RADIUS
-    within = jnp.abs(offsets)[None, :] <= psf_radius[:, None]
-    return jnp.where(within, lateral_kernel, jnp.zeros_like(lateral_kernel)).astype(jnp.bfloat16)
-
-
 def tap_matrices(kernel, width_in, width_out):
     tap_count = 2 * RADIUS + 1
     offset = jnp.arange(width_in)[:, None] - jnp.arange(width_out)[None, :]
@@ -63,7 +587,7 @@
     return summed
 
 
-def per_device(estimate, data, axial, lateral_kernel, psf_radius, pattern_codes):
+def general_device(estimate, data, axial, lateral_kernel, psf_radius, pattern_codes):
     planes, height, width = estimate.shape
     pat_local = data.shape[0]
     full_rows = height * lax.axis_size("ty")
@@ -101,7 +625,6 @@
     cell_count = float(pat_local * lax.axis_size("pat") * planes * full_rows * full_cols)
     data_wide = extended(data, (("ty", 2), ("tx", 3)), RADIUS)
     current = estimate
-    padded = None
     squares_list = []
     for iteration in range(ITERS):
         padded = extended(current, (("ty", 1), ("tx", 2)), depth)
@@ -124,15 +647,30 @@
         contribution = jnp.sum(lighting_inner * gathered, axis=0)
         summed = lax.psum(contribution, "pat")
         current = current * summed / normalizer
-        padded = None
         squares_list.append(lax.psum(local_square, ("ty", "tx", "pat")))
     squares = jnp.stack(squares_list)
     return (current, jnp.sqrt(squares / cell_count))
 
 
 def solution(mesh):
+    sizes = dict(mesh.shape)
     in_specs = (P(None, "ty", "tx"), P("pat", None, "ty", "tx"), P(), P(), P(), P())
     out_specs = (P(None, "ty", "tx"), P())
+
+    def per_device(estimate, data, *rest):
+        planes, rows, cols = estimate.shape
+        members = sizes["ty"] * sizes["pat"]
+        fits = (
+            cols == members * TILE
+            and cols % LANES == 0
+            and rows % 8 == 0
+            and rows * sizes["ty"] <= 2 * TILE
+            and planes == sizes["pat"] * SUB
+        )
+        if fits:
+            return tiled_device(sizes, estimate, data, *rest)
+        return general_device(estimate, data, *rest)
+
     return jax.shard_map(
         per_device, mesh=mesh, in_specs=in_specs, out_specs=out_specs, check_vma=False
     )

time: 452 us -> 119 us (0.26); the launches traced: 443 us -> 118 us
  waiting for transfers between devices: 178 us -> 28.1 us
  matrix products: 83.5 us -> 0 us
  local copies, waits for them, and re-layouts: 52.9 us -> 3.28 us
  Pallas kernels: 0 us -> 36.9 us
  other arithmetic: 24.9 us -> 2.01 us
  starting transfers between devices: 43.4 us -> 21.1 us
  blocking collectives: 45 us -> 25.9 us
  between operations: 15.9 us -> 0.72 us
    psum x4 -> x0, waiting for transfers between devices: 142 us -> none  [the longest x3 86.2 us: per_device(): summed = lax.psum(contribution, 'pat')]
    dot_general x88 -> x0, matrix products: 83.5 us -> none  [the longest x77 63 us: lateral_pass(): jnp.dot(window, matrices[tap_row], preferred_element_type=jnp.float32)]
    psum x1, blocking collectives: 45 us -> 5.75 us  [tiled_device(): squares = lax.psum(jnp.sum(squares[:ITERS], axis=1), 'tx')]
    pallas_call x0 -> x9, Pallas kernels: none -> 36.9 us  [the longest x1 9.45 us: tiled_device(): pl.pallas_call(functools.partial(second_kernel, nx, tile_of, src_of), out...]
    slice x24 -> x0, local copies, waits for them, and re-layouts: 32.4 us -> none  [the longest x8 15.8 us: lateral_pass(): window = padded[..., tap_row:tap_row + height, :]]
    ppermute x20 -> x7, starting transfers between devices: 43.2 us -> 13.8 us  [the longest x3 7.64 us: swap_edges(): lax.ppermute(right, axes, to_right)]
    all_to_all x0 -> x1, blocking collectives: none -> 20.2 us  [tiled_device(): incoming = lax.all_to_all(outgoing, ('ty', 'pat'), 0, 0, tiled=True)]
    unnamed x243 -> x14, local copies, waits for them, and re-layouts: 16.7 us -> 2.4 us
  transfers between devices with their start and end apart: 24 -> 8, of which waited for: 12 -> 8; matrix products, arithmetic and copies ran while one was open for 10% -> 1% of each run, Pallas kernels for 0% -> 9%
where the time goes in v2:
time: 119 us; the launch traced here: 118 us
  Pallas kernels  36.9 us (31%)
  waiting for transfers between devices  28.1 us (24%)
  blocking collectives  25.9 us (22%)
  starting transfers between devices  21.1 us (18%)
  local copies, waits for them, and re-layouts  3.28 us (3%)
  other arithmetic  2.01 us (2%)
    all_to_all x1, blocking collectives, tiled_device(): incoming = lax.all_to_all(outgoing, ('ty', 'pat'), 0, 0, tiled=True)  20.2 us
    ppermute x3, waiting for transfers between devices, swap_edges(): lax.ppermute(left, axes, to_left)  16.5 us
    pallas_call x1, Pallas kernels, tiled_device(): pl.pallas_call(functools.partial(second_kernel, nx, tile_of, src_of), out...  9.45 us
    pallas_call x1, Pallas kernels, tiled_device(): pl.pallas_call(functools.partial(first_kernel, nx, tile_of, src_of), out_...  8.87 us
    ppermute x3, starting transfers between devices, swap_edges(): lax.ppermute(right, axes, to_right)  7.64 us
    all_to_all x1, starting transfers between devices, tiled_device(): mine = lax.all_to_all(message, ('ty', 'pat'), 0, 0, tiled=True)  7.28 us
    ppermute x3, waiting for transfers between devices, swap_edges(): lax.ppermute(right, axes, to_right)  6.9 us
    psum x1, blocking collectives, tiled_device(): squares = lax.psum(jnp.sum(squares[:ITERS], axis=1), 'tx')  5.75 us
  transfers between devices with their start and end apart: 8, of which 8 were waited for; matrix products, arithmetic and copies ran while one was open for 1% of the time, Pallas kernels for 9%

profile of v2, /device:TPU:0, one launch (start us, length us, event | category | flops | bytes accessed | tf_op | source)
XLA Modules:
  0.0 117.9 jit_solution(9116232208799148732)
XLA Ops:
  0.6 3.0 %pack.1 = f32[8,64,512]{2,1,0:T(8,128)} custom-call(f32[1024,256]{1,0:T(8,128)} %bitcast.6), custom_call_target="tpu_custom_call" | custom-call | tf_op jit(solution)/shard_map/pack/pallas_call | solution.py:450
  3.6 7.3 %all-to-all-start = ((f32[8,64,512]{2,1,0:T(8,128)}), f32[8,64,512]{2,1,0:T(8,128)S(1)}, u32[]{:S(2)}, u32[]{:S(2)}) async-start(f32[8,64,512]{2,1,0:T(8,128)} %pack.1), calls=%async_computation | async-start | bytes 2097152 | tf_op jit(solution)/shard_map/all_to_all | solution.py:459
  10.9 2.2 %prep_estimate.1 = f32[2,32,512]{2,1,0:T(8,128)} custom-call(f32[512,256]{1,0:T(8,128)} %bitcast.7), custom_call_target="tpu_custom_call" | custom-call | tf_op jit(solution)/shard_map/prep_estimate/pallas_call | solution.py:461
  14.0 2.1 %collective-permute-start = (f32[32,512]{1,0:T(8,128)S(1)}, f32[32,512]{1,0:T(8,128)S(1)}, u32[]{:S(2)}, u32[]{:S(2)}) collective-permute-start(f32[32,512]{1,0:T(8,128)S(1)} %get-tuple-element.52), channel_id=1, source_target_pairs={{0,16},{16,0},{1,17},{17,1},{2,18},{18,2},{3,19},{19,3},{4,20},{20... | collective-permute-start | bytes 196616 | tf_op jit(solution)/shard_map/ppermute | solution.py:473
  16.1 4.2 %collective-permute-done = f32[32,512]{1,0:T(8,128)S(1)} collective-permute-done((f32[32,512]{1,0:T(8,128)S(1)}, f32[32,512]{1,0:T(8,128)S(1)}, u32[]{:S(2)}, u32[]{:S(2)}) %collective-permute-start) | collective-permute-done | bytes 65568 | tf_op jit(solution)/shard_map/ppermute | solution.py:473
  21.0 1.7 %prep_edges.1 = (f32[32,512]{1,0:T(8,128)}, f32[32,512]{1,0:T(8,128)}) custom-call(f32[2,32,512]{2,1,0:T(8,128)} %pad_maximum_fusion.in_ref.est_ref), custom_call_target="tpu_custom_call" | custom-call | tf_op jit(solution)/shard_map/prep_edges/pallas_call | solution.py:439
  22.7 2.5 %collective-permute-start.1 = (f32[32,512]{1,0:T(8,128)}, f32[32,512]{1,0:T(8,128)S(1)}, u32[]{:S(2)}, u32[]{:S(2)}) collective-permute-start(f32[32,512]{1,0:T(8,128)} %get-tuple-element.28), channel_id=1, source_target_pairs={{0,1},{1,2},{2,3},{3,19},{19,18},{18,17},{17,16},{16,4},{4,5},{5,6... | collective-permute-start | bytes 196616 | tf_op jit(solution)/shard_map/ppermute | solution.py:448
  25.2 1.3 %collective-permute-start.2 = (f32[32,512]{1,0:T(8,128)}, f32[32,512]{1,0:T(8,128)S(1)}, u32[]{:S(2)}, u32[]{:S(2)}) collective-permute-start(f32[32,512]{1,0:T(8,128)} %get-tuple-element.29), channel_id=1, source_target_pairs={{1,0},{2,1},{3,2},{19,3},{18,19},{17,18},{16,17},{4,16},{5,4},{6,5... | collective-permute-start | bytes 196616 | tf_op jit(solution)/shard_map/ppermute | solution.py:448
  26.5 2.5 %tables.1 = (bf16[6,256,256]{2,1,0:T(8,128)(2,1)}, bf16[256,256]{1,0:T(8,128)(2,1)}, bf16[64,192]{1,0:T(8,128)(2,1)}, f32[8,8,256]{2,1,0:T(8,128)}) custom-call(f32[9,9]{1,0:T(8,128)} %k_ref.1, s32[9]{0:T(128)} %radius_ref.1, s32[2,8]{1,0:T(2,128)} %codes_ref.1, f32[32,32]{1,0:T(8,128)} %axial_ref.1), custom_call_target="tpu_custom_call" | custom-call | tf_op jit(solution)/shard_map/tables/pallas_call | solution.py:480
  29.5 8.3 %collective-permute-done.2.from_right_ref = f32[32,512]{1,0:T(8,128)S(1)} collective-permute-done((f32[32,512]{1,0:T(8,128)}, f32[32,512]{1,0:T(8,128)S(1)}, u32[]{:S(2)}, u32[]{:S(2)}) %collective-permute-start.2) | collective-permute-done | bytes 65568 | tf_op jit(solution)/shard_map/ppermute | solution.py:448
  39.3 2.8 %edges.1 = (f32[256,512]{1,0:T(8,128)}, f32[256,512]{1,0:T(8,128)}) custom-call(f32[8,64,512]{2,1,0:T(8,128)} %copy-done), custom_call_target="tpu_custom_call" | custom-call | tf_op jit(solution)/shard_map/edges/pallas_call | solution.py:439
  42.1 2.3 %collective-permute-start.3 = (f32[256,512]{1,0:T(8,128)}, f32[256,512]{1,0:T(8,128)S(1)}, u32[]{:S(2)}, u32[]{:S(2)}) collective-permute-start(f32[256,512]{1,0:T(8,128)} %get-tuple-element.41), channel_id=1, source_target_pairs={{0,1},{1,2},{2,3},{3,19},{19,18},{18,17},{17,16},{16,4},{4,5},{5,6... | collective-permute-start | bytes 1572872 | tf_op jit(solution)/shard_map/ppermute | solution.py:448
  44.3 1.3 %collective-permute-start.4 = (f32[256,512]{1,0:T(8,128)}, f32[256,512]{1,0:T(8,128)S(1)}, u32[]{:S(2)}, u32[]{:S(2)}) collective-permute-start(f32[256,512]{1,0:T(8,128)} %get-tuple-element.42), channel_id=1, source_target_pairs={{1,0},{2,1},{3,2},{19,3},{18,19},{17,18},{16,17},{4,16},{5,4},{6,5... | collective-permute-start | bytes 1572872 | tf_op jit(solution)/shard_map/ppermute | solution.py:448
  45.7 4.1 %forward.1 = (f32[8,32,256]{2,1,0:T(8,128)}, f32[8,32,256]{2,1,0:T(8,128)}, f32[8,256,256]{2,1,0:T(8,128)}) custom-call(bf16[6,256,256]{2,1,0:T(8,128)(2,1)} %get-tuple-element.31.w_ref, bf16[256,256]{1,0:T(8,128)(2,1)} %get-tuple-element.32.ax_fwd, bf16[64,192]{1,0:T(8,128)(2,1)} %get-tuple-element.33.ax_bwd, f32[8,8,256]{2,1,0:T(8,128)} %get-tuple-element.34.light_ref, ...), custom_call_target="tpu_custom_call" | custom-call | tf_op jit(solution)/shard_map/forward/pallas_call | solution.py:503
  49.8 5.6 %collective-permute-done.3.from_left_ref = f32[256,512]{1,0:T(8,128)S(1)} collective-permute-done((f32[256,512]{1,0:T(8,128)}, f32[256,512]{1,0:T(8,128)S(1)}, u32[]{:S(2)}, u32[]{:S(2)}) %collective-permute-start.3) | collective-permute-done | bytes 524320 | tf_op jit(solution)/shard_map/ppermute | solution.py:448
  55.4 4.0 %collective-permute-done.4.from_right_ref = f32[256,512]{1,0:T(8,128)S(1)} collective-permute-done((f32[256,512]{1,0:T(8,128)}, f32[256,512]{1,0:T(8,128)S(1)}, u32[]{:S(2)}, u32[]{:S(2)}) %collective-permute-start.4) | collective-permute-done | bytes 524320 | tf_op jit(solution)/shard_map/ppermute | solution.py:448
  60.2 8.9 %first.1 = (f32[8,256,256]{2,1,0:T(8,128)}, f32[8,32,256]{2,1,0:T(8,128)}, f32[32,512]{1,0:T(8,128)}, f32[32,512]{1,0:T(8,128)}, f32[8,128]{1,0:T(8,128)}) custom-call(bf16[6,256,256]{2,1,0:T(8,128)(2,1)} %get-tuple-element.31.w_ref, bf16[256,256]{1,0:T(8,128)(2,1)} %get-tuple-element.32.ax_fwd, bf16[64,192]{1,0:T(8,128)(2,1)} %get-tuple-element.33.ax_bwd, ...), custom_call_target="tpu_custom_call" | custom-call | tf_op jit(solution)/shard_map/first/pallas_call | solution.py:513
  69.1 2.9 %collective-permute-start.5 = (f32[32,512]{1,0:T(8,128)}, f32[32,512]{1,0:T(8,128)S(1)}, u32[]{:S(2)}, u32[]{:S(2)}) collective-permute-start(f32[32,512]{1,0:T(8,128)} %get-tuple-element.45), channel_id=1, source_target_pairs={{0,1},{1,2},{2,3},{3,19},{19,18},{18,17},{17,16},{16,4},{4,5},{5,6... | collective-permute-start | bytes 196616 | tf_op jit(solution)/shard_map/ppermute | solution.py:448
  71.9 1.5 %collective-permute-start.6 = (f32[32,512]{1,0:T(8,128)}, f32[32,512]{1,0:T(8,128)S(1)}, u32[]{:S(2)}, u32[]{:S(2)}) collective-permute-start(f32[32,512]{1,0:T(8,128)} %get-tuple-element.46), channel_id=1, source_target_pairs={{1,0},{2,1},{3,2},{19,3},{18,19},{17,18},{16,17},{4,16},{5,4},{6,5... | collective-permute-start | bytes 196616 | tf_op jit(solution)/shard_map/ppermute | solution.py:448
  74.1 4.2 %collective-permute-done.6.from_right_ref = f32[32,512]{1,0:T(8,128)S(1)} collective-permute-done((f32[32,512]{1,0:T(8,128)}, f32[32,512]{1,0:T(8,128)S(1)}, u32[]{:S(2)}, u32[]{:S(2)}) %collective-permute-start.6) | collective-permute-done | bytes 65568 | tf_op jit(solution)/shard_map/ppermute | solution.py:448
  78.9 9.5 %second.1 = f32[8,136,128]{2,1,0:T(8,128)} custom-call(bf16[6,256,256]{2,1,0:T(8,128)(2,1)} %get-tuple-element.31.w_ref, bf16[256,256]{1,0:T(8,128)(2,1)} %get-tuple-element.32.ax_fwd, bf16[64,192]{1,0:T(8,128)(2,1)} %get-tuple-element.33.ax_bwd, f32[8,8,256]{2,1,0:T(8,128)} %get-tuple-element.34.light_ref, f32[32,256]{1,0:T(8,128)} %constant.47.clone.wave_ref, ...), custom_call_target="tpu_custom_call" | custom-call | tf_op jit(solution)/shard_map/second/pallas_call | solution.py:522
  88.4 20.2 %all_to_all.10.in_ref = f32[8,136,128]{2,1,0:T(8,128)} all-to-all(f32[8,136,128]{2,1,0:T(8,128)} %second.1), channel_id=1, replica_groups=mesh['ty'=2,'tx'=4,'pat'=4] {'ty','pat'}, dimensions={0} | all-to-all | bytes 1114112 | tf_op jit(solution)/shard_map/all_to_all | solution.py:531
  108.5 2.3 %unpack.1 = (f32[512,256]{1,0:T(8,128)}, f32[8,128]{1,0:T(8,128)}) custom-call(f32[8,136,128]{2,1,0:T(8,128)} %all_to_all.10.in_ref), custom_call_target="tpu_custom_call" | custom-call | tf_op jit(solution)/shard_map/unpack/pallas_call | solution.py:532
  111.6 5.8 %psum.7 = f32[4]{0:T(128)S(1)} all-reduce(f32[4]{0:T(128)S(1)} %slice_reduce_fusion), channel_id=1, replica_groups=mesh['ty'=2,'tx'=4,'pat'=4] {'tx'}, use_global_device_ids=true, to_apply=%region_1.2 | all-reduce | flops 4 | bytes 32 | tf_op jit(solution)/shard_map/psum | solution.py:540
  (22 shorter events, 7.0 us)
Async XLA Ops:
  3.6 34.6 %all-to-all-start = ((f32[8,64,512]{2,1,0:T(8,128)}), f32[8,64,512]{2,1,0:T(8,128)S(1)}, u32[]{:S(2)}, u32[]{:S(2)}) async-start(f32[8,64,512]{2,1,0:T(8,128)} %pack.1), calls=%async_computation | async-start | bytes 2097152 | tf_op jit(solution)/shard_map/all_to_all | solution.py:459
  14.0 6.3 %collective-permute-start = (f32[32,512]{1,0:T(8,128)S(1)}, f32[32,512]{1,0:T(8,128)S(1)}, u32[]{:S(2)}, u32[]{:S(2)}) collective-permute-start(f32[32,512]{1,0:T(8,128)S(1)} %get-tuple-element.52), channel_id=1, source_target_pairs={{0,16},{16,0},{1,17},{17,1},{2,18},{18,2},{3,19},{19,3},{4,20},{20... | collective-permute-start | bytes 196616 | tf_op jit(solution)/shard_map/ppermute | solution.py:473
  22.7 6.8 %collective-permute-start.1 = (f32[32,512]{1,0:T(8,128)}, f32[32,512]{1,0:T(8,128)S(1)}, u32[]{:S(2)}, u32[]{:S(2)}) collective-permute-start(f32[32,512]{1,0:T(8,128)} %get-tuple-element.28), channel_id=1, source_target_pairs={{0,1},{1,2},{2,3},{3,19},{19,18},{18,17},{17,16},{16,4},{4,5},{5,6... | collective-permute-start | bytes 196616 | tf_op jit(solution)/shard_map/ppermute | solution.py:448
  25.2 12.6 %collective-permute-start.2 = (f32[32,512]{1,0:T(8,128)}, f32[32,512]{1,0:T(8,128)S(1)}, u32[]{:S(2)}, u32[]{:S(2)}) collective-permute-start(f32[32,512]{1,0:T(8,128)} %get-tuple-element.29), channel_id=1, source_target_pairs={{1,0},{2,1},{3,2},{19,3},{18,19},{17,18},{16,17},{4,16},{5,4},{6,5... | collective-permute-start | bytes 196616 | tf_op jit(solution)/shard_map/ppermute | solution.py:448
  29.5 16.1 %copy-start.5 = (f32[32,512]{1,0:T(8,128)}, f32[32,512]{1,0:T(8,128)S(1)}, u32[]{:S(2)}) copy-start(f32[32,512]{1,0:T(8,128)S(1)} %collective-permute-done.1.from_left_ref) | copy-start | bytes 196612
  37.8 7.8 %copy-start.6 = (f32[32,512]{1,0:T(8,128)}, f32[32,512]{1,0:T(8,128)S(1)}, u32[]{:S(2)}) copy-start(f32[32,512]{1,0:T(8,128)S(1)} %collective-permute-done.2.from_right_ref) | copy-start | bytes 196612
  38.3 1.0 copy-start
  42.1 13.3 %collective-permute-start.3 = (f32[256,512]{1,0:T(8,128)}, f32[256,512]{1,0:T(8,128)S(1)}, u32[]{:S(2)}, u32[]{:S(2)}) collective-permute-start(f32[256,512]{1,0:T(8,128)} %get-tuple-element.41), channel_id=1, source_target_pairs={{0,1},{1,2},{2,3},{3,19},{19,18},{18,17},{17,16},{16,4},{4,5},{5,6... | collective-permute-start | bytes 1572872 | tf_op jit(solution)/shard_map/ppermute | solution.py:448
  44.3 15.1 %collective-permute-start.4 = (f32[256,512]{1,0:T(8,128)}, f32[256,512]{1,0:T(8,128)S(1)}, u32[]{:S(2)}, u32[]{:S(2)}) collective-permute-start(f32[256,512]{1,0:T(8,128)} %get-tuple-element.42), channel_id=1, source_target_pairs={{1,0},{2,1},{3,2},{19,3},{18,19},{17,18},{16,17},{4,16},{5,4},{6,5... | collective-permute-start | bytes 1572872 | tf_op jit(solution)/shard_map/ppermute | solution.py:448
  55.4 4.0 %copy-start.1 = (f32[256,512]{1,0:T(8,128)}, f32[256,512]{1,0:T(8,128)S(1)}, u32[]{:S(2)}) copy-start(f32[256,512]{1,0:T(8,128)S(1)} %collective-permute-done.3.from_left_ref) | copy-start | bytes 1572868
  59.4 0.8 copy-start.2
  69.1 5.1 %collective-permute-start.5 = (f32[32,512]{1,0:T(8,128)}, f32[32,512]{1,0:T(8,128)S(1)}, u32[]{:S(2)}, u32[]{:S(2)}) collective-permute-start(f32[32,512]{1,0:T(8,128)} %get-tuple-element.45), channel_id=1, source_target_pairs={{0,1},{1,2},{2,3},{3,19},{19,18},{18,17},{17,16},{16,4},{4,5},{5,6... | collective-permute-start | bytes 196616 | tf_op jit(solution)/shard_map/ppermute | solution.py:448
  71.9 6.4 %collective-permute-start.6 = (f32[32,512]{1,0:T(8,128)}, f32[32,512]{1,0:T(8,128)S(1)}, u32[]{:S(2)}, u32[]{:S(2)}) collective-permute-start(f32[32,512]{1,0:T(8,128)} %get-tuple-element.46), channel_id=1, source_target_pairs={{1,0},{2,1},{3,2},{19,3},{18,19},{17,18},{16,17},{4,16},{5,4},{6,5... | collective-permute-start | bytes 196616 | tf_op jit(solution)/shard_map/ppermute | solution.py:448
  74.1 4.2 %copy-start.3 = (f32[32,512]{1,0:T(8,128)}, f32[32,512]{1,0:T(8,128)S(1)}, u32[]{:S(2)}) copy-start(f32[32,512]{1,0:T(8,128)S(1)} %collective-permute-done.5.from_left_ref) | copy-start | bytes 196612
  78.3 0.6 copy-start.4

commit v3 on v2

--- a/solution.py
+++ b/solution.py
@@ -53,6 +53,10 @@
     return out
 
 
+def dest_of(dest_of_tile, c):
+    return jnp.where(lax.rem(lax.axis_index("tx"), 2) == 0, dest_of_tile[c], dest_of_tile[-1 - c])
+
+
 def pack_half(dest_of_tile, rows, half, groups, src_ref, out_ref):
     lane = lane_iota((SUB, LANES))
     tiles_half = LANES // TILE
@@ -60,7 +64,7 @@
         for quad in range(rows // 4):
             v = [src_ref[pl.ds(i * rows * SUB + 4 * quad + r, SUB, stride=rows), :] for r in QUAD_ROWS]
             for t, piece in enumerate(quad_transpose(v, lane)):
-                dest = dest_of_tile[half * tiles_half + t]
+                dest = dest_of(dest_of_tile, half * tiles_half + t)
                 out_ref[dest, i * SUB : (i + 1) * SUB, quad * LANES : (quad + 1) * LANES] = piece
 
 
@@ -369,12 +373,11 @@
                     out_ref[i * pat + k, q * step.planes + z : q * step.planes + z + SUB] = v
 
 
-def final_kernel(dest_of_tile, rows, in_ref, out_ref, sq_ref):
+def final_kernel(dest_of_tile, rows, in_ref, out_ref):
     lane = lane_iota((SUB, LANES))
     planes = out_ref.shape[0] // rows
     tiles_half = LANES // TILE
     quads = rows // 4
-    sq_ref[...] = jnp.sum(in_ref[:, quads * planes : quads * planes + SUB], axis=0)
     for half in range(len(dest_of_tile) // tiles_half):
 
         @pl.when(pl.program_id(0) == half)
@@ -382,7 +385,7 @@
             for z in range(0, planes, SUB):
                 for quad in range(quads):
                     row = quad * planes + z
-                    v = [in_ref[dest_of_tile[half * tiles_half + t], row : row + SUB] for t in range(tiles_half)]
+                    v = [in_ref[dest_of(dest_of_tile, half * tiles_half + t), row : row + SUB] for t in range(tiles_half)]
                     for g, piece in enumerate(quad_transpose(v, lane)):
                         out_ref[pl.ds(z * rows + 4 * quad + QUAD_ROWS[g], SUB, stride=rows), :] = piece
 
@@ -397,8 +400,19 @@
     return jax.ShapeDtypeStruct(dims, dtype)
 
 
+PARAMS = pltpu.CompilerParams(vmem_limit_bytes=24 * 2**20)
 VMEM = pl.BlockSpec(memory_space=pltpu.VMEM)
 SMEM = pl.BlockSpec(memory_space=pltpu.SMEM)
+
+
+def over_tx(value, size):
+    if size & (size - 1):
+        return lax.psum(value, "tx")
+    step = 1
+    while step < size:
+        value = value + lax.ppermute(value, "tx", [(i, i ^ step) for i in range(size)])
+        step *= 2
+    return value
 
 
 def tiled_device(sizes, estimate, data, axial, lateral_kernel, psf_radius, pattern_codes):
@@ -413,7 +427,7 @@
 
     owner = [(i, k if i % 2 == 0 else pat - 1 - k) for i in range(ty) for k in range(pat)]
     dest_of_tile = [i * pat + k for i, k in owner]
-    order = [(i * tx + j) * pat + k for j in range(tx) for i, k in owner]
+    order = [(i * tx + j) * pat + k for j in range(tx) for i, k in (owner if j % 2 == 0 else owner[::-1])]
     to_right = [(a, b) for a, b in zip(order[:-1], order[1:])]
     to_left = [(b, a) for a, b in to_right]
     src_of = (ty, pat)
@@ -422,7 +436,8 @@
 
     def tile_of():
         i, j, k = (lax.axis_index(a) for a in axes)
-        return j * members + i * pat + jnp.where(lax.rem(i, 2) == 0, k, pat - 1 - k)
+        c = i * pat + jnp.where(lax.rem(i, 2) == 0, k, pat - 1 - k)
+        return j * members + jnp.where(lax.rem(j, 2) == 0, c, members - 1 - c)
 
     halves = cols // LANES
     piece_lanes = rows * TILE
@@ -441,6 +456,7 @@
             out_shape=(out, out),
             in_specs=[VMEM],
             out_specs=(VMEM,) * 2,
+            compiler_params=PARAMS,
             name=name,
         )(pieces)
 
@@ -453,6 +469,7 @@
         grid=(halves,),
         in_specs=[half_columns(data.size // cols)],
         out_specs=whole((members, pat_local * planes, piece_lanes)),
+        compiler_params=PARAMS,
         name="pack",
     )(data.reshape(-1, cols))
     message, estimate = lax.optimization_barrier((message, estimate))
@@ -465,6 +482,7 @@
         in_specs=[half_columns(planes * rows)],
         out_specs=whole((ty, planes, piece_lanes)),
         scratch_shapes=[pltpu.VMEM((members, planes, piece_lanes), F32)],
+        compiler_params=PARAMS,
         name="prep_estimate",
     )(estimate.reshape(-1, cols))
     tile_rows = [lax.dynamic_index_in_dim(pieces, ti, 0, keepdims=False)]
@@ -487,6 +505,7 @@
         ),
         in_specs=[SMEM] * 3 + [VMEM],
         out_specs=(VMEM,) * 4,
+        compiler_params=PARAMS,
         name="tables",
     )(lateral_kernel, psf_radius, pattern_codes, axial)
     wave = np.cos(np.arange(planes, dtype=np.float32) * np.float32(TWO_PI * 3.0 / planes))
@@ -506,6 +525,7 @@
         in_specs=table_specs + [VMEM] * 3,
         out_specs=(VMEM,) * 3,
         scratch_shapes=[stage],
+        compiler_params=PARAMS,
         name="forward",
     )(*tables, tile_rows, est_left, est_right)
 
@@ -516,6 +536,7 @@
         in_specs=table_specs + [VMEM] * 6,
         out_specs=(VMEM,) * 5,
         scratch_shapes=[stage, stage],
+        compiler_params=PARAMS,
         name="first",
     )(*tables, norm, current, predicted, mine, from_left, from_right)
     from_left, from_right = swap_edges(left, right)
@@ -525,19 +546,22 @@
         in_specs=table_specs + [VMEM] * 6,
         out_specs=VMEM,
         scratch_shapes=[object_scratch, stage, stage],
+        compiler_params=PARAMS,
         name="second",
     )(*tables, norm, data_all, current, from_left, from_right, sq_first)
 
     incoming = lax.all_to_all(outgoing, ("ty", "pat"), 0, 0, tiled=True)
-    result, squares = pl.pallas_call(
+    squares = jnp.sum(incoming[:, rows // 4 * planes : rows // 4 * planes + ITERS], axis=(0, 2))
+    squares = over_tx(squares, tx)
+    result = pl.pallas_call(
         functools.partial(final_kernel, dest_of_tile, rows),
-        out_shape=(shape((planes * rows, cols)), shape((SUB, LANES))),
+        out_shape=shape((planes * rows, cols)),
         grid=(halves,),
         in_specs=[whole(incoming.shape)],
-        out_specs=(half_columns(planes * rows), whole((SUB, LANES))),
+        out_specs=half_columns(planes * rows),
+        compiler_params=PARAMS,
         name="unpack",
     )(incoming)
-    squares = lax.psum(jnp.sum(squares[:ITERS], axis=1), "tx")
     cell_count = float(patterns * planes * ny * nx)
     return result.reshape(estimate.shape), jnp.sqrt(squares / cell_count)
 

time: 119 us -> 101 us (0.85)
  Pallas kernels: 36.9 us -> 19.9 us
  waiting for transfers between devices: 28.1 us -> 34.7 us
  blocking collectives: 25.9 us -> 20.6 us
  local copies, waits for them, and re-layouts: 3.28 us -> 1.26 us
  other arithmetic: 2.01 us -> 0.69 us
  starting transfers between devices: 21.1 us -> 22.3 us
    psum x1 -> x0, blocking collectives: 5.75 us -> none  [tiled_device(): squares = lax.psum(jnp.sum(squares[:ITERS], axis=1), 'tx')]
    ppermute x3, waiting for transfers between devices: 6.9 us -> 10.9 us  [swap_edges(): lax.ppermute(right, axes, to_right)]
    ppermute x3, waiting for transfers between devices: 16.5 us -> 12.7 us  [swap_edges(): lax.ppermute(left, axes, to_left)]
    pallas_call x2, Pallas kernels: 4.5 us -> 0.74 us  [edges(): pl.pallas_call(functools.partial(edges_kernel, (ty, pieces.shape[0] // ty...]
    pallas_call x1, Pallas kernels: 8.87 us -> 5.48 us  [tiled_device(): pl.pallas_call(functools.partial(first_kernel, nx, tile_of, src_of), out_...]
    pallas_call x1, Pallas kernels: 9.45 us -> 6.5 us  [tiled_device(): pl.pallas_call(functools.partial(second_kernel, nx, tile_of, src_of), out...]
    ppermute x0 -> x2, waiting for transfers between devices: none -> 2.81 us  [over_tx(): lax.ppermute(value, 'tx', [(i, i ^ step) for i in range(size)])]
    pallas_call x1, Pallas kernels: 4.11 us -> 1.43 us  [tiled_device(): pl.pallas_call(functools.partial(forward_kernel, nx, tile_of, (ty, 1)), o...]
  transfers between devices with their start and end apart: 8 -> 10, of which waited for: 8 -> 9; matrix products, arithmetic and copies ran while one was open for 1% -> 0% of each run, Pallas kernels for 9% -> 5%
where the time goes in v3:
time: 101 us; the launch traced here: 100 us
  waiting for transfers between devices  34.7 us (34%)
  starting transfers between devices  22.3 us (22%)
  blocking collectives  20.6 us (20%)
  Pallas kernels  19.9 us (20%)
  local copies, waits for them, and re-layouts  1.26 us (1%)
    all_to_all x1, blocking collectives, tiled_device(): incoming = lax.all_to_all(outgoing, ('ty', 'pat'), 0, 0, tiled=True)  20.6 us
    ppermute x3, waiting for transfers between devices, swap_edges(): lax.ppermute(left, axes, to_left)  12.7 us
    ppermute x3, waiting for transfers between devices, swap_edges(): lax.ppermute(right, axes, to_right)  10.9 us
    ppermute x3, starting transfers between devices, swap_edges(): lax.ppermute(right, axes, to_right)  7.96 us
    all_to_all x1, starting transfers between devices, tiled_device(): mine = lax.all_to_all(message, ('ty', 'pat'), 0, 0, tiled=True)  7.42 us
    ppermute x1, waiting for transfers between devices, tiled_device(): lax.ppermute(sent, 'ty', [(i, (i + shift) % ty) for i in range(ty)])  6.61 us
    pallas_call x1, Pallas kernels, tiled_device(): pl.pallas_call(functools.partial(second_kernel, nx, tile_of, src_of), out...  6.5 us
    pallas_call x1, Pallas kernels, tiled_device(): pl.pallas_call(functools.partial(first_kernel, nx, tile_of, src_of), out_...  5.48 us
  transfers between devices with their start and end apart: 10, of which 9 were waited for; matrix products, arithmetic and copies ran while one was open for 0% of the time, Pallas kernels for 5%

profile of v3, /device:TPU:0, one launch (start us, length us, event | category | flops | bytes accessed | tf_op | source)
XLA Modules:
  0.0 100.3 jit_solution(14030150052070459091)
XLA Ops:
  0.6 1.2 %copy-done = f32[2,32,16,256]{3,2,1,0:T(8,128)S(1)} copy-done((f32[2,32,16,256]{3,2,1,0:T(8,128)S(1)}, f32[2,32,16,256]{3,2,1,0:T(8,128)}, u32[]{:S(2)}) %copy-start) | copy-done | bytes 1048600
  1.9 2.1 %pack.1 = f32[8,64,512]{2,1,0:T(8,128)} custom-call(f32[1024,256]{1,0:T(8,128)S(1)} %bitcast.6), custom_call_target="tpu_custom_call" | custom-call | tf_op jit(solution)/shard_map/pack/pallas_call | solution.py:466
  3.9 7.4 %all-to-all-start = ((f32[8,64,512]{2,1,0:T(8,128)}), f32[8,64,512]{2,1,0:T(8,128)S(1)}, u32[]{:S(2)}, u32[]{:S(2)}) async-start(f32[8,64,512]{2,1,0:T(8,128)} %pack.1), calls=%async_computation | async-start | bytes 2097152 | tf_op jit(solution)/shard_map/all_to_all | solution.py:476
  12.1 2.1 %collective-permute-start = (f32[32,512]{1,0:T(8,128)S(1)}, f32[32,512]{1,0:T(8,128)S(1)}, u32[]{:S(2)}, u32[]{:S(2)}) collective-permute-start(f32[32,512]{1,0:T(8,128)S(1)} %get-tuple-element.48), channel_id=1, source_target_pairs={{0,16},{16,0},{1,17},{17,1},{2,18},{18,2},{3,19},{19,3},{4,20},{20... | collective-permute-start | bytes 196616 | tf_op jit(solution)/shard_map/ppermute | solution.py:491
  14.1 6.6 %collective-permute-done = f32[32,512]{1,0:T(8,128)S(1)} collective-permute-done((f32[32,512]{1,0:T(8,128)S(1)}, f32[32,512]{1,0:T(8,128)S(1)}, u32[]{:S(2)}, u32[]{:S(2)}) %collective-permute-start) | collective-permute-done | bytes 65568 | tf_op jit(solution)/shard_map/ppermute | solution.py:491
  20.9 2.4 %collective-permute-start.1 = (f32[32,512]{1,0:T(8,128)S(1)}, f32[32,512]{1,0:T(8,128)S(1)}, u32[]{:S(2)}, u32[]{:S(2)}) collective-permute-start(f32[32,512]{1,0:T(8,128)S(1)} %get-tuple-element.26), channel_id=1, source_target_pairs={{0,1},{1,2},{2,3},{3,19},{19,18},{18,17},{17,16},{16,20},{20,21},{... | collective-permute-start | bytes 196616 | tf_op jit(solution)/shard_map/ppermute | solution.py:464
  23.4 1.3 %collective-permute-start.2 = (f32[32,512]{1,0:T(8,128)S(1)}, f32[32,512]{1,0:T(8,128)S(1)}, u32[]{:S(2)}, u32[]{:S(2)}) collective-permute-start(f32[32,512]{1,0:T(8,128)S(1)} %get-tuple-element.27), channel_id=1, source_target_pairs={{1,0},{2,1},{3,2},{19,3},{18,19},{17,18},{16,17},{20,16},{21,20},{... | collective-permute-start | bytes 196616 | tf_op jit(solution)/shard_map/ppermute | solution.py:464
  24.7 1.7 %tables.1 = (bf16[6,256,256]{2,1,0:T(8,128)(2,1)S(1)}, bf16[256,256]{1,0:T(8,128)(2,1)S(1)}, bf16[64,192]{1,0:T(8,128)(2,1)S(1)}, f32[8,8,256]{2,1,0:T(8,128)S(1)}) custom-call(f32[9,9]{1,0:T(8,128)S(1)} %copy-done.4, s32[9]{0:T(128)S(1)} %copy-done.6, s32[2,8]{1,0:T(2,128)S(1)} %copy-done.5, f32[32,32]{1,0:T(8,128)S(1)} %copy-done.3), custom_call_target="tpu_custom_call" | custom-call | tf_op jit(solution)/shard_map/tables/pallas_call | solution.py:498
  26.4 3.5 %collective-permute-done.1.from_left_ref = f32[32,512]{1,0:T(8,128)S(1)} collective-permute-done((f32[32,512]{1,0:T(8,128)S(1)}, f32[32,512]{1,0:T(8,128)S(1)}, u32[]{:S(2)}, u32[]{:S(2)}) %collective-permute-start.1) | collective-permute-done | bytes 65568 | tf_op jit(solution)/shard_map/ppermute | solution.py:464
  29.9 7.1 %collective-permute-done.2.from_right_ref = f32[32,512]{1,0:T(8,128)S(1)} collective-permute-done((f32[32,512]{1,0:T(8,128)S(1)}, f32[32,512]{1,0:T(8,128)S(1)}, u32[]{:S(2)}, u32[]{:S(2)}) %collective-permute-start.2) | collective-permute-done | bytes 65568 | tf_op jit(solution)/shard_map/ppermute | solution.py:464
  37.0 1.7 %all-to-all-done.in_ref = f32[8,64,512]{2,1,0:T(8,128)S(1)} async-done(((f32[8,64,512]{2,1,0:T(8,128)}), f32[8,64,512]{2,1,0:T(8,128)S(1)}, u32[]{:S(2)}, u32[]{:S(2)}) %all-to-all-start) | async-done | bytes 1048608 | tf_op jit(solution)/shard_map/all_to_all | solution.py:476
  39.3 2.3 %collective-permute-start.3 = (f32[256,512]{1,0:T(8,128)S(1)}, f32[256,512]{1,0:T(8,128)S(1)}, u32[]{:S(2)}, u32[]{:S(2)}) collective-permute-start(f32[256,512]{1,0:T(8,128)S(1)} %get-tuple-element.39), channel_id=1, source_target_pairs={{0,1},{1,2},{2,3},{3,19},{19,18},{18,17},{17,16},{16,20},{20,21},{... | collective-permute-start | bytes 1572872 | tf_op jit(solution)/shard_map/ppermute | solution.py:464
  41.6 1.3 %collective-permute-start.4 = (f32[256,512]{1,0:T(8,128)S(1)}, f32[256,512]{1,0:T(8,128)S(1)}, u32[]{:S(2)}, u32[]{:S(2)}) collective-permute-start(f32[256,512]{1,0:T(8,128)S(1)} %get-tuple-element.40), channel_id=1, source_target_pairs={{1,0},{2,1},{3,2},{19,3},{18,19},{17,18},{16,17},{20,16},{21,20},{... | collective-permute-start | bytes 1572872 | tf_op jit(solution)/shard_map/ppermute | solution.py:464
  43.0 1.4 %forward.1 = (f32[8,32,256]{2,1,0:T(8,128)S(1)}, f32[8,32,256]{2,1,0:T(8,128)S(1)}, f32[8,256,256]{2,1,0:T(8,128)S(1)}) custom-call(bf16[6,256,256]{2,1,0:T(8,128)(2,1)S(1)} %get-tuple-element.29.w_ref, bf16[256,256]{1,0:T(8,128)(2,1)S(1)} %get-tuple-element.30.ax_fwd, bf16[64,192]{1,0:T(8,128)(2,1)S(1)} %get-tuple-element.31.ax_bwd, ...), custom_call_target="tpu_custom_call" | custom-call | tf_op jit(solution)/shard_map/forward/pallas_call | solution.py:522
  44.4 7.0 %collective-permute-done.3.from_left_ref = f32[256,512]{1,0:T(8,128)S(1)} collective-permute-done((f32[256,512]{1,0:T(8,128)S(1)}, f32[256,512]{1,0:T(8,128)S(1)}, u32[]{:S(2)}, u32[]{:S(2)}) %collective-permute-start.3) | collective-permute-done | bytes 524320 | tf_op jit(solution)/shard_map/ppermute | solution.py:464
  51.4 1.3 %collective-permute-done.4.from_right_ref = f32[256,512]{1,0:T(8,128)S(1)} collective-permute-done((f32[256,512]{1,0:T(8,128)S(1)}, f32[256,512]{1,0:T(8,128)S(1)}, u32[]{:S(2)}, u32[]{:S(2)}) %collective-permute-start.4) | collective-permute-done | bytes 524320 | tf_op jit(solution)/shard_map/ppermute | solution.py:464
  52.7 5.5 %first.1 = (f32[8,256,256]{2,1,0:T(8,128)S(1)}, f32[8,32,256]{2,1,0:T(8,128)S(1)}, f32[32,512]{1,0:T(8,128)S(1)}, f32[32,512]{1,0:T(8,128)S(1)}, f32[8,128]{1,0:T(8,128)S(1)}) custom-call(bf16[6,256,256]{2,1,0:T(8,128)(2,1)S(1)} %get-tuple-element.29.w_ref, bf16[256,256]{1,0:T(8,128)(2,1)S(1)} %get-tuple-element.30.ax_fwd, ...), custom_call_target="tpu_custom_call" | custom-call | tf_op jit(solution)/shard_map/first/pallas_call | solution.py:533
  58.2 3.2 %collective-permute-start.5 = (f32[32,512]{1,0:T(8,128)S(1)}, f32[32,512]{1,0:T(8,128)S(1)}, u32[]{:S(2)}, u32[]{:S(2)}) collective-permute-start(f32[32,512]{1,0:T(8,128)S(1)} %get-tuple-element.43), channel_id=1, source_target_pairs={{0,1},{1,2},{2,3},{3,19},{19,18},{18,17},{17,16},{16,20},{20,21},{... | collective-permute-start | bytes 196616 | tf_op jit(solution)/shard_map/ppermute | solution.py:464
  61.4 1.5 %collective-permute-start.6 = (f32[32,512]{1,0:T(8,128)S(1)}, f32[32,512]{1,0:T(8,128)S(1)}, u32[]{:S(2)}, u32[]{:S(2)}) collective-permute-start(f32[32,512]{1,0:T(8,128)S(1)} %get-tuple-element.44), channel_id=1, source_target_pairs={{1,0},{2,1},{3,2},{19,3},{18,19},{17,18},{16,17},{20,16},{21,20},{... | collective-permute-start | bytes 196616 | tf_op jit(solution)/shard_map/ppermute | solution.py:464
  63.3 4.3 %collective-permute-done.6.from_right_ref = f32[32,512]{1,0:T(8,128)S(1)} collective-permute-done((f32[32,512]{1,0:T(8,128)S(1)}, f32[32,512]{1,0:T(8,128)S(1)}, u32[]{:S(2)}, u32[]{:S(2)}) %collective-permute-start.6) | collective-permute-done | bytes 65568 | tf_op jit(solution)/shard_map/ppermute | solution.py:464
  67.6 6.5 %second.1 = f32[8,136,128]{2,1,0:T(8,128)S(1)} custom-call(bf16[6,256,256]{2,1,0:T(8,128)(2,1)S(1)} %get-tuple-element.29.w_ref, bf16[256,256]{1,0:T(8,128)(2,1)S(1)} %get-tuple-element.30.ax_fwd, bf16[64,192]{1,0:T(8,128)(2,1)S(1)} %get-tuple-element.31.ax_bwd, f32[8,8,256]{2,1,0:T(8,128)S(1)} %get-tuple-element.32.light_ref, f32[32,256]{1,0:T(8,128)S(1)} %copy-done.2, ...), custom_call_target="tpu_custom_call" | custom-call | tf_op jit(solution)/shard_map/second/pallas_call | solution.py:543
  74.1 20.6 %all_to_all.10.in_ref = f32[8,136,128]{2,1,0:T(8,128)S(1)} all-to-all(f32[8,136,128]{2,1,0:T(8,128)S(1)} %second.1), channel_id=1, replica_groups=mesh['ty'=2,'tx'=4,'pat'=4] {'ty','pat'}, dimensions={0} | all-to-all | bytes 1114112 | tf_op jit(solution)/shard_map/all_to_all | solution.py:553
  94.9 1.3 %unpack.1 = f32[512,256]{1,0:T(8,128)} custom-call(f32[8,136,128]{2,1,0:T(8,128)S(1)} %all_to_all.10.in_ref), custom_call_target="tpu_custom_call" | custom-call | tf_op jit(solution)/shard_map/unpack/pallas_call | solution.py:556
  97.0 2.8 %collective-permute-done.8 = f32[4]{0:T(128)S(1)} collective-permute-done((f32[4]{0:T(128)S(1)}, f32[4]{0:T(128)S(1)}, u32[]{:S(2)}, u32[]{:S(2)}) %collective-permute-start.8) | collective-permute-done | bytes 48 | tf_op jit(solution)/shard_map/ppermute | solution.py:413
  (26 shorter events, 3.4 us)
Async XLA Ops:
  0.6 1.2 %copy-start = (f32[2,32,16,256]{3,2,1,0:T(8,128)S(1)}, f32[2,32,16,256]{3,2,1,0:T(8,128)}, u32[]{:S(2)}) copy-start(f32[2,32,16,256]{3,2,1,0:T(8,128)} %param.8) | copy-start | bytes 3145732
  1.9 9.5 %copy-start.1 = (f32[32,16,256]{2,1,0:T(8,128)S(1)}, f32[32,16,256]{2,1,0:T(8,128)}, u32[]{:S(2)}) copy-start(f32[32,16,256]{2,1,0:T(8,128)} %param.7) | copy-start | bytes 1572868
  3.9 20.8 %copy-start.3 = (f32[32,32]{1,0:T(8,128)S(1)}, f32[32,32]{1,0:T(8,128)}, u32[]{:S(2)}) copy-start(f32[32,32]{1,0:T(8,128)} %axial_ref.1) | copy-start | bytes 12292
  3.9 20.8 %copy-start.4 = (f32[9,9]{1,0:T(8,128)S(1)}, f32[9,9]{1,0:T(8,128)}, u32[]{:S(2)}) copy-start(f32[9,9]{1,0:T(8,128)} %k_ref.1) | copy-start | bytes 976
  3.9 20.8 %copy-start.5 = (s32[2,8]{1,0:T(2,128)S(1)}, s32[2,8]{1,0:T(2,128)}, u32[]{:S(2)}) copy-start(s32[2,8]{1,0:T(2,128)} %codes_ref.1) | copy-start | bytes 196
  3.9 20.8 %copy-start.6 = (s32[9]{0:T(128)S(1)}, s32[9]{0:T(128)}, u32[]{:S(2)}) copy-start(s32[9]{0:T(128)} %radius_ref.1) | copy-start | bytes 112
  3.9 39.0 %copy-start.2 = (f32[32,256]{1,0:T(8,128)S(1)}, f32[32,256]{1,0:T(8,128)}, u32[]{:S(2)}) copy-start(f32[32,256]{1,0:T(8,128)} %constant.47.clone.wave_ref) | copy-start | bytes 98308
  3.9 34.7 %all-to-all-start = ((f32[8,64,512]{2,1,0:T(8,128)}), f32[8,64,512]{2,1,0:T(8,128)S(1)}, u32[]{:S(2)}, u32[]{:S(2)}) async-start(f32[8,64,512]{2,1,0:T(8,128)} %pack.1), calls=%async_computation | async-start | bytes 2097152 | tf_op jit(solution)/shard_map/all_to_all | solution.py:476
  12.1 8.7 %collective-permute-start = (f32[32,512]{1,0:T(8,128)S(1)}, f32[32,512]{1,0:T(8,128)S(1)}, u32[]{:S(2)}, u32[]{:S(2)}) collective-permute-start(f32[32,512]{1,0:T(8,128)S(1)} %get-tuple-element.48), channel_id=1, source_target_pairs={{0,16},{16,0},{1,17},{17,1},{2,18},{18,2},{3,19},{19,3},{4,20},{20... | collective-permute-start | bytes 196616 | tf_op jit(solution)/shard_map/ppermute | solution.py:491
  20.9 8.9 %collective-permute-start.1 = (f32[32,512]{1,0:T(8,128)S(1)}, f32[32,512]{1,0:T(8,128)S(1)}, u32[]{:S(2)}, u32[]{:S(2)}) collective-permute-start(f32[32,512]{1,0:T(8,128)S(1)} %get-tuple-element.26), channel_id=1, source_target_pairs={{0,1},{1,2},{2,3},{3,19},{19,18},{18,17},{17,16},{16,20},{20,21},{... | collective-permute-start | bytes 196616 | tf_op jit(solution)/shard_map/ppermute | solution.py:464
  23.4 13.6 %collective-permute-start.2 = (f32[32,512]{1,0:T(8,128)S(1)}, f32[32,512]{1,0:T(8,128)S(1)}, u32[]{:S(2)}, u32[]{:S(2)}) collective-permute-start(f32[32,512]{1,0:T(8,128)S(1)} %get-tuple-element.27), channel_id=1, source_target_pairs={{1,0},{2,1},{3,2},{19,3},{18,19},{17,18},{16,17},{20,16},{21,20},{... | collective-permute-start | bytes 196616 | tf_op jit(solution)/shard_map/ppermute | solution.py:464
  39.3 12.1 %collective-permute-start.3 = (f32[256,512]{1,0:T(8,128)S(1)}, f32[256,512]{1,0:T(8,128)S(1)}, u32[]{:S(2)}, u32[]{:S(2)}) collective-permute-start(f32[256,512]{1,0:T(8,128)S(1)} %get-tuple-element.39), channel_id=1, source_target_pairs={{0,1},{1,2},{2,3},{3,19},{19,18},{18,17},{17,16},{16,20},{20,21},{... | collective-permute-start | bytes 1572872 | tf_op jit(solution)/shard_map/ppermute | solution.py:464
  41.6 11.1 %collective-permute-start.4 = (f32[256,512]{1,0:T(8,128)S(1)}, f32[256,512]{1,0:T(8,128)S(1)}, u32[]{:S(2)}, u32[]{:S(2)}) collective-permute-start(f32[256,512]{1,0:T(8,128)S(1)} %get-tuple-element.40), channel_id=1, source_target_pairs={{1,0},{2,1},{3,2},{19,3},{18,19},{17,18},{16,17},{20,16},{21,20},{... | collective-permute-start | bytes 1572872 | tf_op jit(solution)/shard_map/ppermute | solution.py:464
  58.2 5.1 %collective-permute-start.5 = (f32[32,512]{1,0:T(8,128)S(1)}, f32[32,512]{1,0:T(8,128)S(1)}, u32[]{:S(2)}, u32[]{:S(2)}) collective-permute-start(f32[32,512]{1,0:T(8,128)S(1)} %get-tuple-element.43), channel_id=1, source_target_pairs={{0,1},{1,2},{2,3},{3,19},{19,18},{18,17},{17,16},{16,20},{20,21},{... | collective-permute-start | bytes 196616 | tf_op jit(solution)/shard_map/ppermute | solution.py:464
  61.4 6.2 %collective-permute-start.6 = (f32[32,512]{1,0:T(8,128)S(1)}, f32[32,512]{1,0:T(8,128)S(1)}, u32[]{:S(2)}, u32[]{:S(2)}) collective-permute-start(f32[32,512]{1,0:T(8,128)S(1)} %get-tuple-element.44), channel_id=1, source_target_pairs={{1,0},{2,1},{3,2},{19,3},{18,19},{17,18},{16,17},{20,16},{21,20},{... | collective-permute-start | bytes 196616 | tf_op jit(solution)/shard_map/ppermute | solution.py:464
  94.8 1.4 %collective-permute-start.7 = (f32[4]{0:T(128)S(1)}, f32[4]{0:T(128)S(1)}, u32[]{:S(2)}, u32[]{:S(2)}) collective-permute-start(f32[4]{0:T(128)S(1)} %slice_reduce_fusion), channel_id=1, source_target_pairs={{0,4},{4,0},{8,12},{12,8},{1,5},{5,1},{9,13},{13,9},{2,6},{6,2},{1... | collective-permute-start | bytes 56 | tf_op jit(solution)/shard_map/ppermute | solution.py:413
  96.2 3.6 %collective-permute-start.8 = (f32[4]{0:T(128)S(1)}, f32[4]{0:T(128)S(1)}, u32[]{:S(2)}, u32[]{:S(2)}) collective-permute-start(f32[4]{0:T(128)S(1)} %add.41), channel_id=1, source_target_pairs={{0,8},{4,12},{8,0},{12,4},{1,9},{5,13},{9,1},{13,5},{2,10},{6,14},... | collective-permute-start | bytes 56 | tf_op jit(solution)/shard_map/ppermute | solution.py:413

commit v4 on v3

--- a/solution.py
+++ b/solution.py
@@ -68,12 +68,54 @@
                 out_ref[dest, i * SUB : (i + 1) * SUB, quad * LANES : (quad + 1) * LANES] = piece
 
 
+DATA_LOW, DATA_HIGH, TOP = 0.1, 6.0, 2**24 - 1
+DATA_SCALE = TOP / (DATA_HIGH - DATA_LOW)
+BIAS = 2**15
+
+
+def to_fixed(v):
+    return jnp.clip((v - DATA_LOW) * DATA_SCALE + 0.5, 0.0, float(TOP)).astype(jnp.int32)
+
+
+def from_fixed(t):
+    return t.astype(F32) * (1.0 / DATA_SCALE) + DATA_LOW
+
+
+def encode(first, second):
+    low = ((first & 255) << 8) + (second & 255)
+    return tuple((v - BIAS).astype(jnp.int16) for v in (first >> 8, second >> 8, low))
+
+
+def decode(first, second, low):
+    first, second, low = (v.astype(jnp.int32) + BIAS for v in (first, second, low))
+    return (first << 8) + (low >> 8), (second << 8) + (low & 255)
+
+
 def pack_kernel(dest_of_tile, rows, data_ref, out_ref):
-    for half in range(len(dest_of_tile) * TILE // LANES):
+    lane = lane_iota((SUB, LANES))
+    tiles_half = LANES // TILE
+    part = out_ref.shape[1] // 3
+    per_pattern = part // SUB
+
+    def pieces(group, quad):
+        start = group * rows * SUB + 4 * quad
+        v = [to_fixed(data_ref[pl.ds(start + r, SUB, stride=rows), :]) for r in QUAD_ROWS]
+        return quad_transpose(v, lane)
+
+    for half in range(len(dest_of_tile) // tiles_half):
 
         @pl.when(pl.program_id(0) == half)
         def _(half=half):
-            pack_half(dest_of_tile, rows, half, data_ref.shape[0] // (rows * SUB), data_ref, out_ref)
+            for g in range(0, per_pattern, 2):
+                for quad in range(rows // 4):
+                    a0, a1 = pieces(g, quad), pieces(g + 1, quad)
+                    b0, b1 = pieces(per_pattern + g, quad), pieces(per_pattern + g + 1, quad)
+                    for t in range(tiles_half):
+                        dest = dest_of(dest_of_tile, half * tiles_half + t)
+                        coded = encode(jnp.concatenate([a0[t], a1[t]]), jnp.concatenate([b0[t], b1[t]]))
+                        for n, v in enumerate(coded):
+                            row = n * part + g * SUB
+                            out_ref[dest, row : row + 2 * SUB, quad * LANES : (quad + 1) * LANES] = v
 
 
 def estimate_kernel(dest_of_tile, rows, pat, est_ref, out_ref, all_ref):
@@ -116,6 +158,59 @@
                     vreg = i * per_ty + pair
                     left_ref[row, vreg * LANES : (vreg + 1) * LANES] = left
                     right_ref[row, vreg * LANES : (vreg + 1) * LANES] = right
+
+
+def coded_rows(k, g, part, pat):
+    first = 2 * k * part + g
+    return [slice(r, r + 2 * SUB) for r in (first, first + part, 2 * pat * part + k * part + g)]
+
+
+def own_coded(in_ref, source, g, part, q):
+    rows = [slice(n * part + g, n * part + g + 2 * SUB) for n in range(3)]
+    return decode(*(in_ref[source, r, q * LANES : (q + 1) * LANES] for r in rows))
+
+
+def data_edges_kernel(src_of, in_ref, left_ref, right_ref):
+    lane = lane_iota((2 * SUB, LANES))
+    ty, pat = src_of
+    part = in_ref.shape[1] // 3
+    per_ty = in_ref.shape[2] // LANES // 2
+    for k in range(pat):
+        for g in range(0, part, 2 * SUB):
+            for i in range(ty):
+                for pair in range(per_ty):
+                    both = [own_coded(in_ref, i * pat + k, g, part, q) for q in (2 * pair, 2 * pair + 1)]
+                    sides = []
+                    for p in range(2):
+                        sides.append(edge_messages([(v[p], o) for v in both for o in (0, TILE)], lane))
+                    vreg = i * per_ty + pair
+                    for side, ref in enumerate((left_ref, right_ref)):
+                        for r, v in zip(coded_rows(k, g, part, pat), encode(sides[0][side], sides[1][side])):
+                            ref[r, vreg * LANES : (vreg + 1) * LANES] = v
+
+
+def unpack_data(src_of, in_ref, from_left_ref, from_right_ref, out_ref):
+    lane = lane_iota((2 * SUB, LANES))
+    ty, pat = src_of
+    part = in_ref.shape[1] // 3
+    per_ty = in_ref.shape[2] // LANES // 2
+    for k in range(pat):
+        for g in range(0, part, 2 * SUB):
+            rows = coded_rows(k, g, part, pat)
+            for i in range(ty):
+                for pair in range(per_ty):
+                    vreg = i * per_ty + pair
+                    at = slice(vreg * LANES, (vreg + 1) * LANES)
+                    from_left = decode(*(from_left_ref[r, at] for r in rows))
+                    from_right = decode(*(from_right_ref[r, at] for r in rows))
+                    both = [own_coded(in_ref, i * pat + k, g, part, q) for q in (2 * pair, 2 * pair + 1)]
+                    for p in range(2):
+                        own = [x for v in both for x in (v[p], roll(v[p], -TILE))]
+                        for u in range(4):
+                            m = 4 * vreg + u
+                            out_ref[m // 2, rows[p], (m % 2) * LANES : (m % 2 + 1) * LANES] = from_fixed(
+                                with_halo(own[u], u, from_right[p], from_left[p], lane)
+                            )
 
 
 def unpack_wide(src_of, in_ref, from_left_ref, from_right_ref, out_ref):
@@ -320,7 +415,7 @@
 def first_kernel(nx, tile_of, src_of, w_ref, ax_fwd, ax_bwd, light_ref, wave_ref, norm_ref, obj_in_ref,
                  predicted_ref, in_ref, from_left_ref, from_right_ref, data_ref, obj_ref, left_ref, right_ref,
                  sq_ref, stage_ref, quot_ref):
-    unpack_wide(src_of, in_ref, from_left_ref, from_right_ref, data_ref)
+    unpack_data(src_of, in_ref, from_left_ref, from_right_ref, data_ref)
     step = Step(nx, tile_of, w_ref, ax_fwd, ax_bwd, light_ref, wave_ref)
     step.clear_ends(stage_ref)
     step.clear_ends(quot_ref)
@@ -449,10 +544,10 @@
     def half_columns(height):
         return pl.BlockSpec((height, LANES), lambda h: (0, h))
 
-    def edges(pieces, name):
-        out = shape((pieces.shape[1] * pieces.shape[0] // ty, halo_lanes))
+    def edges(pieces, body, name):
+        out = shape((pieces.shape[1] * pieces.shape[0] // ty, halo_lanes), pieces.dtype)
         return pl.pallas_call(
-            functools.partial(edges_kernel, (ty, pieces.shape[0] // ty)),
+            functools.partial(body, (ty, pieces.shape[0] // ty)),
             out_shape=(out, out),
             in_specs=[VMEM],
             out_specs=(VMEM,) * 2,
@@ -465,10 +560,10 @@
 
     message = pl.pallas_call(
         functools.partial(pack_kernel, dest_of_tile, rows),
-        out_shape=shape((members, pat_local * planes, piece_lanes)),
+        out_shape=shape((members, 3 * planes, piece_lanes), jnp.int16),
         grid=(halves,),
         in_specs=[half_columns(data.size // cols)],
-        out_specs=whole((members, pat_local * planes, piece_lanes)),
+        out_specs=whole((members, 3 * planes, piece_lanes)),
         compiler_params=PARAMS,
         name="pack",
     )(data.reshape(-1, cols))
@@ -493,7 +588,7 @@
     tile_rows = jnp.stack(
         [lax.dynamic_index_in_dim(tile_rows, (ti - i) % ty, 0, keepdims=False) for i in range(ty)]
     )
-    est_left, est_right = swap_edges(*edges(tile_rows, "prep_edges"))
+    est_left, est_right = swap_edges(*edges(tile_rows, edges_kernel, "prep_edges"))
 
     weights, ax_fwd, ax_bwd, light = pl.pallas_call(
         functools.partial(tables_kernel, tile_of),
@@ -517,7 +612,7 @@
     stage = pltpu.VMEM((blocks + 2, patterns * planes, BLOCK), BF16)
     table_specs = [VMEM] * 5
     mine, est_left, est_right, weights = lax.optimization_barrier((mine, est_left, est_right, weights))
-    from_left, from_right = swap_edges(*edges(mine, "edges"))
+    from_left, from_right = swap_edges(*edges(mine, data_edges_kernel, "edges"))
     tables = (weights, ax_fwd, ax_bwd, light, wave)
     current, norm, predicted = pl.pallas_call(
         functools.partial(forward_kernel, nx, tile_of, (ty, 1)),
@@ -689,7 +784,8 @@
             and cols % LANES == 0
             and rows % 8 == 0
             and rows * sizes["ty"] <= 2 * TILE
-            and planes == sizes["pat"] * SUB
+            and planes % (2 * SUB) == 0
+            and data.shape[0] == 2
         )
         if fits:
             return tiled_device(sizes, estimate, data, *rest)

time: 101 us -> 92.4 us (0.915)
  waiting for transfers between devices: 34.7 us -> 27.3 us
  blocking collectives: 20.6 us -> 19 us
    ppermute x3, waiting for transfers between devices: 10.9 us -> 4.62 us  [swap_edges(): lax.ppermute(right, axes, to_right)]
    all_to_all x1, blocking collectives: 20.6 us -> 19 us  [tiled_device(): incoming = lax.all_to_all(outgoing, ('ty', 'pat'), 0, 0, tiled=True)]
    ppermute x1, waiting for transfers between devices: 6.61 us -> 5.2 us  [tiled_device(): lax.ppermute(sent, 'ty', [(i, (i + shift) % ty) for i in range(ty)])]
  transfers between devices with their start and end apart: 10 -> 10, of which waited for: 9 -> 8; matrix products, arithmetic and copies ran while one was open for 0% -> 0% of each run, Pallas kernels for 5% -> 6%
where the time goes in v4:
time: 92.4 us; the launch traced here: 91.9 us
  waiting for transfers between devices  27.3 us (30%)
  starting transfers between devices  22.9 us (25%)
  Pallas kernels  19.9 us (22%)
  blocking collectives  19 us (21%)
  local copies, waits for them, and re-layouts  1.26 us (1%)
    all_to_all x1, blocking collectives, tiled_device(): incoming = lax.all_to_all(outgoing, ('ty', 'pat'), 0, 0, tiled=True)  19 us
    ppermute x3, waiting for transfers between devices, swap_edges(): lax.ppermute(left, axes, to_left)  13.7 us
    ppermute x3, starting transfers between devices, swap_edges(): lax.ppermute(right, axes, to_right)  7.98 us
    all_to_all x1, starting transfers between devices, tiled_device(): mine = lax.all_to_all(message, ('ty', 'pat'), 0, 0, tiled=True)  7.41 us
    pallas_call x1, Pallas kernels, tiled_device(): pl.pallas_call(functools.partial(second_kernel, nx, tile_of, src_of), out...  6.5 us
    pallas_call x1, Pallas kernels, tiled_device(): pl.pallas_call(functools.partial(first_kernel, nx, tile_of, src_of), out_...  5.56 us
    ppermute x1, waiting for transfers between devices, tiled_device(): lax.ppermute(sent, 'ty', [(i, (i + shift) % ty) for i in range(ty)])  5.2 us
    ppermute x3, waiting for transfers between devices, swap_edges(): lax.ppermute(right, axes, to_right)  4.62 us
  transfers between devices with their start and end apart: 10, of which 8 were waited for; matrix products, arithmetic and copies ran while one was open for 0% of the time, Pallas kernels for 6%

profile of v4, /device:TPU:0, one launch (start us, length us, event | category | flops | bytes accessed | tf_op | source)
XLA Modules:
  0.0 91.9 jit_solution(16421793519743948614)
XLA Ops:
  0.6 1.2 %copy-done = f32[2,32,16,256]{3,2,1,0:T(8,128)S(1)} copy-done((f32[2,32,16,256]{3,2,1,0:T(8,128)S(1)}, f32[2,32,16,256]{3,2,1,0:T(8,128)}, u32[]{:S(2)}) %copy-start) | copy-done | bytes 1048600
  1.9 2.0 %pack.1 = s16[8,96,512]{2,1,0:T(8,128)(2,1)} custom-call(f32[1024,256]{1,0:T(8,128)S(1)} %bitcast.6), custom_call_target="tpu_custom_call" | custom-call | tf_op jit(solution)/shard_map/pack/pallas_call | solution.py:561
  3.9 7.4 %all-to-all-start = ((s16[8,96,512]{2,1,0:T(8,128)(2,1)}), s16[8,96,512]{2,1,0:T(8,128)(2,1)S(1)}, u32[]{:S(2)}, u32[]{:S(2)}) async-start(s16[8,96,512]{2,1,0:T(8,128)(2,1)} %pack.1), calls=%async_computation | async-start | bytes 1572864 | tf_op jit(solution)/shard_map/all_to_all | solution.py:571
  12.0 2.1 %collective-permute-start = (f32[32,512]{1,0:T(8,128)S(1)}, f32[32,512]{1,0:T(8,128)S(1)}, u32[]{:S(2)}, u32[]{:S(2)}) collective-permute-start(f32[32,512]{1,0:T(8,128)S(1)} %get-tuple-element.48), channel_id=1, source_target_pairs={{0,16},{16,0},{1,17},{17,1},{2,18},{18,2},{3,19},{19,3},{4,20},{20... | collective-permute-start | bytes 196616 | tf_op jit(solution)/shard_map/ppermute | solution.py:586
  14.0 5.2 %collective-permute-done = f32[32,512]{1,0:T(8,128)S(1)} collective-permute-done((f32[32,512]{1,0:T(8,128)S(1)}, f32[32,512]{1,0:T(8,128)S(1)}, u32[]{:S(2)}, u32[]{:S(2)}) %collective-permute-start) | collective-permute-done | bytes 65568 | tf_op jit(solution)/shard_map/ppermute | solution.py:586
  19.4 2.4 %collective-permute-start.1 = (f32[32,512]{1,0:T(8,128)S(1)}, f32[32,512]{1,0:T(8,128)S(1)}, u32[]{:S(2)}, u32[]{:S(2)}) collective-permute-start(f32[32,512]{1,0:T(8,128)S(1)} %get-tuple-element.26), channel_id=1, source_target_pairs={{0,1},{1,2},{2,3},{3,19},{19,18},{18,17},{17,16},{16,20},{20,21},{... | collective-permute-start | bytes 196616 | tf_op jit(solution)/shard_map/ppermute | solution.py:559
  21.9 1.3 %collective-permute-start.2 = (f32[32,512]{1,0:T(8,128)S(1)}, f32[32,512]{1,0:T(8,128)S(1)}, u32[]{:S(2)}, u32[]{:S(2)}) collective-permute-start(f32[32,512]{1,0:T(8,128)S(1)} %get-tuple-element.27), channel_id=1, source_target_pairs={{1,0},{2,1},{3,2},{19,3},{18,19},{17,18},{16,17},{20,16},{21,20},{... | collective-permute-start | bytes 196616 | tf_op jit(solution)/shard_map/ppermute | solution.py:559
  23.2 1.7 %tables.1 = (bf16[6,256,256]{2,1,0:T(8,128)(2,1)S(1)}, bf16[256,256]{1,0:T(8,128)(2,1)S(1)}, bf16[64,192]{1,0:T(8,128)(2,1)S(1)}, f32[8,8,256]{2,1,0:T(8,128)S(1)}) custom-call(f32[9,9]{1,0:T(8,128)S(1)} %copy-done.4, s32[9]{0:T(128)S(1)} %copy-done.6, s32[2,8]{1,0:T(2,128)S(1)} %copy-done.5, f32[32,32]{1,0:T(8,128)S(1)} %copy-done.3), custom_call_target="tpu_custom_call" | custom-call | tf_op jit(solution)/shard_map/tables/pallas_call | solution.py:593
  24.9 6.5 %collective-permute-done.2.from_right_ref = f32[32,512]{1,0:T(8,128)S(1)} collective-permute-done((f32[32,512]{1,0:T(8,128)S(1)}, f32[32,512]{1,0:T(8,128)S(1)}, u32[]{:S(2)}, u32[]{:S(2)}) %collective-permute-start.2) | collective-permute-done | bytes 65568 | tf_op jit(solution)/shard_map/ppermute | solution.py:559
  31.4 1.6 %all-to-all-done.in_ref = s16[8,96,512]{2,1,0:T(8,128)(2,1)S(1)} async-done(((s16[8,96,512]{2,1,0:T(8,128)(2,1)}), s16[8,96,512]{2,1,0:T(8,128)(2,1)S(1)}, u32[]{:S(2)}, u32[]{:S(2)}) %all-to-all-start) | async-done | bytes 786464 | tf_op jit(solution)/shard_map/all_to_all | solution.py:571
  33.6 2.3 %collective-permute-start.3 = (s16[384,512]{1,0:T(8,128)(2,1)S(1)}, s16[384,512]{1,0:T(8,128)(2,1)S(1)}, u32[]{:S(2)}, u32[]{:S(2)}) collective-permute-start(s16[384,512]{1,0:T(8,128)(2,1)S(1)} %get-tuple-element.39), channel_id=1, source_target_pairs={{0,1},{1,2},{2,3},{3,19},{19,18},{18,17},{17,16},{16,20},{20,21},{... | collective-permute-start | bytes 1179656 | tf_op jit(solution)/shard_map/ppermute | solution.py:559
  35.9 1.3 %collective-permute-start.4 = (s16[384,512]{1,0:T(8,128)(2,1)S(1)}, s16[384,512]{1,0:T(8,128)(2,1)S(1)}, u32[]{:S(2)}, u32[]{:S(2)}) collective-permute-start(s16[384,512]{1,0:T(8,128)(2,1)S(1)} %get-tuple-element.40), channel_id=1, source_target_pairs={{1,0},{2,1},{3,2},{19,3},{18,19},{17,18},{16,17},{20,16},{21,20},{... | collective-permute-start | bytes 1179656 | tf_op jit(solution)/shard_map/ppermute | solution.py:559
  37.2 1.4 %forward.1 = (f32[8,32,256]{2,1,0:T(8,128)S(1)}, f32[8,32,256]{2,1,0:T(8,128)S(1)}, f32[8,256,256]{2,1,0:T(8,128)S(1)}) custom-call(bf16[6,256,256]{2,1,0:T(8,128)(2,1)S(1)} %get-tuple-element.29.w_ref, bf16[256,256]{1,0:T(8,128)(2,1)S(1)} %get-tuple-element.30.ax_fwd, bf16[64,192]{1,0:T(8,128)(2,1)S(1)} %get-tuple-element.31.ax_bwd, ...), custom_call_target="tpu_custom_call" | custom-call | tf_op jit(solution)/shard_map/forward/pallas_call | solution.py:617
  38.7 4.2 %collective-permute-done.3.from_left_ref = s16[384,512]{1,0:T(8,128)(2,1)S(1)} collective-permute-done((s16[384,512]{1,0:T(8,128)(2,1)S(1)}, s16[384,512]{1,0:T(8,128)(2,1)S(1)}, u32[]{:S(2)}, u32[]{:S(2)}) %collective-permute-start.3) | collective-permute-done | bytes 393248 | tf_op jit(solution)/shard_map/ppermute | solution.py:559
  42.9 2.7 %collective-permute-done.4.from_right_ref = s16[384,512]{1,0:T(8,128)(2,1)S(1)} collective-permute-done((s16[384,512]{1,0:T(8,128)(2,1)S(1)}, s16[384,512]{1,0:T(8,128)(2,1)S(1)}, u32[]{:S(2)}, u32[]{:S(2)}) %collective-permute-start.4) | collective-permute-done | bytes 393248 | tf_op jit(solution)/shard_map/ppermute | solution.py:559
  45.6 5.6 %first.1 = (f32[8,256,256]{2,1,0:T(8,128)S(1)}, f32[8,32,256]{2,1,0:T(8,128)S(1)}, f32[32,512]{1,0:T(8,128)S(1)}, f32[32,512]{1,0:T(8,128)S(1)}, f32[8,128]{1,0:T(8,128)S(1)}) custom-call(bf16[6,256,256]{2,1,0:T(8,128)(2,1)S(1)} %get-tuple-element.29.w_ref, bf16[256,256]{1,0:T(8,128)(2,1)S(1)} %get-tuple-element.30.ax_fwd, ...), custom_call_target="tpu_custom_call" | custom-call | tf_op jit(solution)/shard_map/first/pallas_call | solution.py:628
  51.1 3.3 %collective-permute-start.5 = (f32[32,512]{1,0:T(8,128)S(1)}, f32[32,512]{1,0:T(8,128)S(1)}, u32[]{:S(2)}, u32[]{:S(2)}) collective-permute-start(f32[32,512]{1,0:T(8,128)S(1)} %get-tuple-element.43), channel_id=1, source_target_pairs={{0,1},{1,2},{2,3},{3,19},{19,18},{18,17},{17,16},{16,20},{20,21},{... | collective-permute-start | bytes 196616 | tf_op jit(solution)/shard_map/ppermute | solution.py:559
  54.4 1.5 %collective-permute-start.6 = (f32[32,512]{1,0:T(8,128)S(1)}, f32[32,512]{1,0:T(8,128)S(1)}, u32[]{:S(2)}, u32[]{:S(2)}) collective-permute-start(f32[32,512]{1,0:T(8,128)S(1)} %get-tuple-element.44), channel_id=1, source_target_pairs={{1,0},{2,1},{3,2},{19,3},{18,19},{17,18},{16,17},{20,16},{21,20},{... | collective-permute-start | bytes 196616 | tf_op jit(solution)/shard_map/ppermute | solution.py:559
  56.3 4.5 %collective-permute-done.6.from_right_ref = f32[32,512]{1,0:T(8,128)S(1)} collective-permute-done((f32[32,512]{1,0:T(8,128)S(1)}, f32[32,512]{1,0:T(8,128)S(1)}, u32[]{:S(2)}, u32[]{:S(2)}) %collective-permute-start.6) | collective-permute-done | bytes 65568 | tf_op jit(solution)/shard_map/ppermute | solution.py:559
  60.8 6.5 %second.1 = f32[8,136,128]{2,1,0:T(8,128)S(1)} custom-call(bf16[6,256,256]{2,1,0:T(8,128)(2,1)S(1)} %get-tuple-element.29.w_ref, bf16[256,256]{1,0:T(8,128)(2,1)S(1)} %get-tuple-element.30.ax_fwd, bf16[64,192]{1,0:T(8,128)(2,1)S(1)} %get-tuple-element.31.ax_bwd, f32[8,8,256]{2,1,0:T(8,128)S(1)} %get-tuple-element.32.light_ref, f32[32,256]{1,0:T(8,128)S(1)} %copy-done.2, ...), custom_call_target="tpu_custom_call" | custom-call | tf_op jit(solution)/shard_map/second/pallas_call | solution.py:638
  67.3 19.0 %all_to_all.10.in_ref = f32[8,136,128]{2,1,0:T(8,128)S(1)} all-to-all(f32[8,136,128]{2,1,0:T(8,128)S(1)} %second.1), channel_id=1, replica_groups=mesh['ty'=2,'tx'=4,'pat'=4] {'ty','pat'}, dimensions={0} | all-to-all | bytes 1114112 | tf_op jit(solution)/shard_map/all_to_all | solution.py:648
  86.5 1.3 %unpack.1 = f32[512,256]{1,0:T(8,128)} custom-call(f32[8,136,128]{2,1,0:T(8,128)S(1)} %all_to_all.10.in_ref), custom_call_target="tpu_custom_call" | custom-call | tf_op jit(solution)/shard_map/unpack/pallas_call | solution.py:651
  87.8 1.3 %collective-permute-start.8 = (f32[4]{0:T(128)S(1)}, f32[4]{0:T(128)S(1)}, u32[]{:S(2)}, u32[]{:S(2)}) collective-permute-start(f32[4]{0:T(128)S(1)} %add.41), channel_id=1, source_target_pairs={{0,8},{4,12},{8,0},{12,4},{1,9},{5,13},{9,1},{13,5},{2,10},{6,14},... | collective-permute-start | bytes 56 | tf_op jit(solution)/shard_map/ppermute | solution.py:508
  89.2 2.2 %collective-permute-done.8 = f32[4]{0:T(128)S(1)} collective-permute-done((f32[4]{0:T(128)S(1)}, f32[4]{0:T(128)S(1)}, u32[]{:S(2)}, u32[]{:S(2)}) %collective-permute-start.8) | collective-permute-done | bytes 48 | tf_op jit(solution)/shard_map/ppermute | solution.py:508
  (26 shorter events, 2.6 us)
Async XLA Ops:
  0.6 1.2 %copy-start = (f32[2,32,16,256]{3,2,1,0:T(8,128)S(1)}, f32[2,32,16,256]{3,2,1,0:T(8,128)}, u32[]{:S(2)}) copy-start(f32[2,32,16,256]{3,2,1,0:T(8,128)} %param.8) | copy-start | bytes 3145732
  1.9 9.4 %copy-start.1 = (f32[32,16,256]{2,1,0:T(8,128)S(1)}, f32[32,16,256]{2,1,0:T(8,128)}, u32[]{:S(2)}) copy-start(f32[32,16,256]{2,1,0:T(8,128)} %param.7) | copy-start | bytes 1572868
  1.9 21.3 %copy-start.3 = (f32[32,32]{1,0:T(8,128)S(1)}, f32[32,32]{1,0:T(8,128)}, u32[]{:S(2)}) copy-start(f32[32,32]{1,0:T(8,128)} %axial_ref.1) | copy-start | bytes 12292
  1.9 21.3 %copy-start.4 = (f32[9,9]{1,0:T(8,128)S(1)}, f32[9,9]{1,0:T(8,128)}, u32[]{:S(2)}) copy-start(f32[9,9]{1,0:T(8,128)} %k_ref.1) | copy-start | bytes 976
  1.9 21.3 %copy-start.5 = (s32[2,8]{1,0:T(2,128)S(1)}, s32[2,8]{1,0:T(2,128)}, u32[]{:S(2)}) copy-start(s32[2,8]{1,0:T(2,128)} %codes_ref.1) | copy-start | bytes 196
  1.9 21.3 %copy-start.6 = (s32[9]{0:T(128)S(1)}, s32[9]{0:T(128)}, u32[]{:S(2)}) copy-start(s32[9]{0:T(128)} %radius_ref.1) | copy-start | bytes 112
  3.9 33.4 %copy-start.2 = (f32[32,256]{1,0:T(8,128)S(1)}, f32[32,256]{1,0:T(8,128)}, u32[]{:S(2)}) copy-start(f32[32,256]{1,0:T(8,128)} %constant.47.clone.wave_ref) | copy-start | bytes 98308
  3.9 29.1 %all-to-all-start = ((s16[8,96,512]{2,1,0:T(8,128)(2,1)}), s16[8,96,512]{2,1,0:T(8,128)(2,1)S(1)}, u32[]{:S(2)}, u32[]{:S(2)}) async-start(s16[8,96,512]{2,1,0:T(8,128)(2,1)} %pack.1), calls=%async_computation | async-start | bytes 1572864 | tf_op jit(solution)/shard_map/all_to_all | solution.py:571
  12.0 7.3 %collective-permute-start = (f32[32,512]{1,0:T(8,128)S(1)}, f32[32,512]{1,0:T(8,128)S(1)}, u32[]{:S(2)}, u32[]{:S(2)}) collective-permute-start(f32[32,512]{1,0:T(8,128)S(1)} %get-tuple-element.48), channel_id=1, source_target_pairs={{0,16},{16,0},{1,17},{17,1},{2,18},{18,2},{3,19},{19,3},{4,20},{20... | collective-permute-start | bytes 196616 | tf_op jit(solution)/shard_map/ppermute | solution.py:586
  19.4 5.5 %collective-permute-start.1 = (f32[32,512]{1,0:T(8,128)S(1)}, f32[32,512]{1,0:T(8,128)S(1)}, u32[]{:S(2)}, u32[]{:S(2)}) collective-permute-start(f32[32,512]{1,0:T(8,128)S(1)} %get-tuple-element.26), channel_id=1, source_target_pairs={{0,1},{1,2},{2,3},{3,19},{19,18},{18,17},{17,16},{16,20},{20,21},{... | collective-permute-start | bytes 196616 | tf_op jit(solution)/shard_map/ppermute | solution.py:559
  21.9 9.5 %collective-permute-start.2 = (f32[32,512]{1,0:T(8,128)S(1)}, f32[32,512]{1,0:T(8,128)S(1)}, u32[]{:S(2)}, u32[]{:S(2)}) collective-permute-start(f32[32,512]{1,0:T(8,128)S(1)} %get-tuple-element.27), channel_id=1, source_target_pairs={{1,0},{2,1},{3,2},{19,3},{18,19},{17,18},{16,17},{20,16},{21,20},{... | collective-permute-start | bytes 196616 | tf_op jit(solution)/shard_map/ppermute | solution.py:559
  33.6 9.3 %collective-permute-start.3 = (s16[384,512]{1,0:T(8,128)(2,1)S(1)}, s16[384,512]{1,0:T(8,128)(2,1)S(1)}, u32[]{:S(2)}, u32[]{:S(2)}) collective-permute-start(s16[384,512]{1,0:T(8,128)(2,1)S(1)} %get-tuple-element.39), channel_id=1, source_target_pairs={{0,1},{1,2},{2,3},{3,19},{19,18},{18,17},{17,16},{16,20},{20,21},{... | collective-permute-start | bytes 1179656 | tf_op jit(solution)/shard_map/ppermute | solution.py:559
  35.9 9.7 %collective-permute-start.4 = (s16[384,512]{1,0:T(8,128)(2,1)S(1)}, s16[384,512]{1,0:T(8,128)(2,1)S(1)}, u32[]{:S(2)}, u32[]{:S(2)}) collective-permute-start(s16[384,512]{1,0:T(8,128)(2,1)S(1)} %get-tuple-element.40), channel_id=1, source_target_pairs={{1,0},{2,1},{3,2},{19,3},{18,19},{17,18},{16,17},{20,16},{21,20},{... | collective-permute-start | bytes 1179656 | tf_op jit(solution)/shard_map/ppermute | solution.py:559
  51.1 5.2 %collective-permute-start.5 = (f32[32,512]{1,0:T(8,128)S(1)}, f32[32,512]{1,0:T(8,128)S(1)}, u32[]{:S(2)}, u32[]{:S(2)}) collective-permute-start(f32[32,512]{1,0:T(8,128)S(1)} %get-tuple-element.43), channel_id=1, source_target_pairs={{0,1},{1,2},{2,3},{3,19},{19,18},{18,17},{17,16},{16,20},{20,21},{... | collective-permute-start | bytes 196616 | tf_op jit(solution)/shard_map/ppermute | solution.py:559
  54.4 6.4 %collective-permute-start.6 = (f32[32,512]{1,0:T(8,128)S(1)}, f32[32,512]{1,0:T(8,128)S(1)}, u32[]{:S(2)}, u32[]{:S(2)}) collective-permute-start(f32[32,512]{1,0:T(8,128)S(1)} %get-tuple-element.44), channel_id=1, source_target_pairs={{1,0},{2,1},{3,2},{19,3},{18,19},{17,18},{16,17},{20,16},{21,20},{... | collective-permute-start | bytes 196616 | tf_op jit(solution)/shard_map/ppermute | solution.py:559
  86.4 1.4 %collective-permute-start.7 = (f32[4]{0:T(128)S(1)}, f32[4]{0:T(128)S(1)}, u32[]{:S(2)}, u32[]{:S(2)}) collective-permute-start(f32[4]{0:T(128)S(1)} %slice_reduce_fusion), channel_id=1, source_target_pairs={{0,4},{4,0},{8,12},{12,8},{1,5},{5,1},{9,13},{13,9},{2,6},{6,2},{1... | collective-permute-start | bytes 56 | tf_op jit(solution)/shard_map/ppermute | solution.py:508
  87.8 3.6 %collective-permute-start.8 = (f32[4]{0:T(128)S(1)}, f32[4]{0:T(128)S(1)}, u32[]{:S(2)}, u32[]{:S(2)}) collective-permute-start(f32[4]{0:T(128)S(1)} %add.41), channel_id=1, source_target_pairs={{0,8},{4,12},{8,0},{12,4},{1,9},{5,13},{9,1},{13,5},{2,10},{6,14},... | collective-permute-start | bytes 56 | tf_op jit(solution)/shard_map/ppermute | solution.py:508

commit v5 on v4

--- a/solution.py
+++ b/solution.py
@@ -89,6 +89,18 @@
 def decode(first, second, low):
     first, second, low = (v.astype(jnp.int32) + BIAS for v in (first, second, low))
     return (first << 8) + (low >> 8), (second << 8) + (low & 255)
+
+
+LOG_SCALE, LOG_BIAS, LN2 = 2.0**16, 128.0, math.log(2.0)
+
+
+def to_log(v):
+    t = (jnp.log(jnp.maximum(v, 2.0**-126)) * (1.0 / LN2) + LOG_BIAS) * LOG_SCALE + 0.5
+    return jnp.where(v > 0, jnp.clip(t, 1.0, float(TOP)), 0.0).astype(jnp.int32)
+
+
+def from_log(t):
+    return jnp.where(t > 0, jnp.exp2(t.astype(F32) * (1.0 / LOG_SCALE) - LOG_BIAS), 0.0)
 
 
 def pack_kernel(dest_of_tile, rows, data_ref, out_ref):
@@ -453,36 +465,51 @@
 
     ty, pat = src_of
     quads = step.blocks // ty
-    lane = lane_iota((SUB, LANES))
+    planes = step.planes
+    lane = lane_iota((2 * SUB, LANES))
     own = (lane // TILE) % 2 == 0
-    last = jnp.concatenate(squares + [jnp.zeros((SUB - len(squares), LANES), F32)], axis=0)
+    last = to_log(jnp.concatenate(squares + [jnp.zeros((SUB - len(squares), LANES), F32)], axis=0))
+    last = (jnp.concatenate([last >> 8, last & 255]) - BIAS).astype(jnp.int16)
+    low_rows, last_rows = quads * planes, quads * planes * 3 // 2
     for i in range(ty):
         for k in range(pat):
-            out_ref[i * pat + k, quads * step.planes : quads * step.planes + SUB] = last
-        for q in range(quads):
-            for z in range(0, step.planes, SUB):
-                v0 = obj_ref[i * quads + q, z : z + SUB, 0:LANES]
-                v1 = obj_ref[i * quads + q, z : z + SUB, LANES : 2 * LANES]
-                v = jnp.where(own, v0, roll(v1, TILE))
-                for k in range(pat):
-                    out_ref[i * pat + k, q * step.planes + z : q * step.planes + z + SUB] = v
+            out_ref[i * pat + k, last_rows : last_rows + 2 * SUB] = last
+        for q in range(0, quads, 2):
+            for z in range(0, planes, 2 * SUB):
+                fixed = []
+                for b in (i * quads + q, i * quads + q + 1):
+                    v0 = obj_ref[b, z : z + 2 * SUB, 0:LANES]
+                    v1 = obj_ref[b, z : z + 2 * SUB, LANES : 2 * LANES]
+                    fixed.append(to_log(jnp.where(own, v0, roll(v1, TILE))))
+                starts = (q * planes + z, (q + 1) * planes + z, low_rows + q // 2 * planes + z)
+                for row, v in zip(starts, encode(*fixed)):
+                    for k in range(pat):
+                        out_ref[i * pat + k, row : row + 2 * SUB] = v
 
 
 def final_kernel(dest_of_tile, rows, in_ref, out_ref):
-    lane = lane_iota((SUB, LANES))
+    lane = lane_iota((2 * SUB, LANES))
     planes = out_ref.shape[0] // rows
     tiles_half = LANES // TILE
     quads = rows // 4
+    low_rows = quads * planes
     for half in range(len(dest_of_tile) // tiles_half):
 
         @pl.when(pl.program_id(0) == half)
         def _(half=half):
-            for z in range(0, planes, SUB):
-                for quad in range(quads):
-                    row = quad * planes + z
-                    v = [in_ref[dest_of(dest_of_tile, half * tiles_half + t), row : row + SUB] for t in range(tiles_half)]
-                    for g, piece in enumerate(quad_transpose(v, lane)):
-                        out_ref[pl.ds(z * rows + 4 * quad + QUAD_ROWS[g], SUB, stride=rows), :] = piece
+            for z in range(0, planes, 2 * SUB):
+                for q in range(0, quads, 2):
+                    starts = (q * planes + z, (q + 1) * planes + z, low_rows + q // 2 * planes + z)
+                    both = []
+                    for t in range(tiles_half):
+                        dest = dest_of(dest_of_tile, half * tiles_half + t)
+                        coded = decode(*(in_ref[dest, row : row + 2 * SUB] for row in starts))
+                        both.append([from_log(v) for v in coded])
+                    for p in range(2):
+                        for g, piece in enumerate(quad_transpose([v[p] for v in both], lane)):
+                            for h in range(2):
+                                start = (z + h * SUB) * rows + 4 * (q + p) + QUAD_ROWS[g]
+                                out_ref[pl.ds(start, SUB, stride=rows), :] = piece[h * SUB : (h + 1) * SUB]
 
 
 def masked_kernel(lateral_kernel, psf_radius):
@@ -637,7 +664,7 @@
     from_left, from_right = swap_edges(left, right)
     outgoing = pl.pallas_call(
         functools.partial(second_kernel, nx, tile_of, src_of),
-        out_shape=shape((members, rows // 4 * planes + SUB, LANES)),
+        out_shape=shape((members, rows // 4 * planes * 3 // 2 + 2 * SUB, LANES), jnp.int16),
         in_specs=table_specs + [VMEM] * 6,
         out_specs=VMEM,
         scratch_shapes=[object_scratch, stage, stage],
@@ -646,7 +673,8 @@
     )(*tables, norm, data_all, current, from_left, from_right, sq_first)
 
     incoming = lax.all_to_all(outgoing, ("ty", "pat"), 0, 0, tiled=True)
-    squares = jnp.sum(incoming[:, rows // 4 * planes : rows // 4 * planes + ITERS], axis=(0, 2))
+    last = incoming[:, rows // 4 * planes * 3 // 2 :].astype(jnp.int32) + BIAS
+    squares = jnp.sum(from_log((last[:, :ITERS] << 8) + last[:, SUB : SUB + ITERS]), axis=(0, 2))
     squares = over_tx(squares, tx)
     result = pl.pallas_call(
         functools.partial(final_kernel, dest_of_tile, rows),

time: 92.4 us -> 89.7 us (0.971)
  blocking collectives: 19 us -> 16.2 us
    all_to_all x1, blocking collectives: 19 us -> 16.2 us  [tiled_device(): incoming = lax.all_to_all(outgoing, ('ty', 'pat'), 0, 0, tiled=True)]
where the time goes in v5:
time: 89.7 us; the launch traced here: 89.2 us
  waiting for transfers between devices  27.4 us (31%)
  starting transfers between devices  22.9 us (26%)
  Pallas kernels  19.9 us (22%)
  blocking collectives  16.2 us (18%)
  local copies, waits for them, and re-layouts  1.26 us (1%)
    all_to_all x1, blocking collectives, tiled_device(): incoming = lax.all_to_all(outgoing, ('ty', 'pat'), 0, 0, tiled=True)  16.2 us
    ppermute x3, waiting for transfers between devices, swap_edges(): lax.ppermute(left, axes, to_left)  13.7 us
    ppermute x3, starting transfers between devices, swap_edges(): lax.ppermute(right, axes, to_right)  7.98 us
    all_to_all x1, starting transfers between devices, tiled_device(): mine = lax.all_to_all(message, ('ty', 'pat'), 0, 0, tiled=True)  7.41 us
    pallas_call x1, Pallas kernels, tiled_device(): pl.pallas_call(functools.partial(second_kernel, nx, tile_of, src_of), out...  6.52 us
    pallas_call x1, Pallas kernels, tiled_device(): pl.pallas_call(functools.partial(first_kernel, nx, tile_of, src_of), out_...  5.56 us
    ppermute x1, waiting for transfers between devices, tiled_device(): lax.ppermute(sent, 'ty', [(i, (i + shift) % ty) for i in range(ty)])  5.2 us
    ppermute x3, waiting for transfers between devices, swap_edges(): lax.ppermute(right, axes, to_right)  4.62 us
  transfers between devices with their start and end apart: 10, of which 8 were waited for; matrix products, arithmetic and copies ran while one was open for 0% of the time, Pallas kernels for 6%

profile of v5, /device:TPU:0, one launch (start us, length us, event | category | flops | bytes accessed | tf_op | source)
XLA Modules:
  0.0 89.2 jit_solution(6444100575756698584)
XLA Ops:
  0.6 1.2 %copy-done = f32[2,32,16,256]{3,2,1,0:T(8,128)S(1)} copy-done((f32[2,32,16,256]{3,2,1,0:T(8,128)S(1)}, f32[2,32,16,256]{3,2,1,0:T(8,128)}, u32[]{:S(2)}) %copy-start) | copy-done | bytes 1048600
  1.9 2.0 %pack.1 = s16[8,96,512]{2,1,0:T(8,128)(2,1)} custom-call(f32[1024,256]{1,0:T(8,128)S(1)} %bitcast.6), custom_call_target="tpu_custom_call" | custom-call | tf_op jit(solution)/shard_map/pack/pallas_call | solution.py:588
  3.9 7.4 %all-to-all-start = ((s16[8,96,512]{2,1,0:T(8,128)(2,1)}), s16[8,96,512]{2,1,0:T(8,128)(2,1)S(1)}, u32[]{:S(2)}, u32[]{:S(2)}) async-start(s16[8,96,512]{2,1,0:T(8,128)(2,1)} %pack.1), calls=%async_computation | async-start | bytes 1572864 | tf_op jit(solution)/shard_map/all_to_all | solution.py:598
  12.0 2.1 %collective-permute-start = (f32[32,512]{1,0:T(8,128)S(1)}, f32[32,512]{1,0:T(8,128)S(1)}, u32[]{:S(2)}, u32[]{:S(2)}) collective-permute-start(f32[32,512]{1,0:T(8,128)S(1)} %get-tuple-element.48), channel_id=1, source_target_pairs={{0,16},{16,0},{1,17},{17,1},{2,18},{18,2},{3,19},{19,3},{4,20},{20... | collective-permute-start | bytes 196616 | tf_op jit(solution)/shard_map/ppermute | solution.py:613
  14.0 5.2 %collective-permute-done = f32[32,512]{1,0:T(8,128)S(1)} collective-permute-done((f32[32,512]{1,0:T(8,128)S(1)}, f32[32,512]{1,0:T(8,128)S(1)}, u32[]{:S(2)}, u32[]{:S(2)}) %collective-permute-start) | collective-permute-done | bytes 65568 | tf_op jit(solution)/shard_map/ppermute | solution.py:613
  19.4 2.4 %collective-permute-start.1 = (f32[32,512]{1,0:T(8,128)S(1)}, f32[32,512]{1,0:T(8,128)S(1)}, u32[]{:S(2)}, u32[]{:S(2)}) collective-permute-start(f32[32,512]{1,0:T(8,128)S(1)} %get-tuple-element.26), channel_id=1, source_target_pairs={{0,1},{1,2},{2,3},{3,19},{19,18},{18,17},{17,16},{16,20},{20,21},{... | collective-permute-start | bytes 196616 | tf_op jit(solution)/shard_map/ppermute | solution.py:586
  21.9 1.3 %collective-permute-start.2 = (f32[32,512]{1,0:T(8,128)S(1)}, f32[32,512]{1,0:T(8,128)S(1)}, u32[]{:S(2)}, u32[]{:S(2)}) collective-permute-start(f32[32,512]{1,0:T(8,128)S(1)} %get-tuple-element.27), channel_id=1, source_target_pairs={{1,0},{2,1},{3,2},{19,3},{18,19},{17,18},{16,17},{20,16},{21,20},{... | collective-permute-start | bytes 196616 | tf_op jit(solution)/shard_map/ppermute | solution.py:586
  23.2 1.7 %tables.1 = (bf16[6,256,256]{2,1,0:T(8,128)(2,1)S(1)}, bf16[256,256]{1,0:T(8,128)(2,1)S(1)}, bf16[64,192]{1,0:T(8,128)(2,1)S(1)}, f32[8,8,256]{2,1,0:T(8,128)S(1)}) custom-call(f32[9,9]{1,0:T(8,128)S(1)} %copy-done.4, s32[9]{0:T(128)S(1)} %copy-done.6, s32[2,8]{1,0:T(2,128)S(1)} %copy-done.5, f32[32,32]{1,0:T(8,128)S(1)} %copy-done.3), custom_call_target="tpu_custom_call" | custom-call | tf_op jit(solution)/shard_map/tables/pallas_call | solution.py:620
  24.9 6.5 %collective-permute-done.2.from_right_ref = f32[32,512]{1,0:T(8,128)S(1)} collective-permute-done((f32[32,512]{1,0:T(8,128)S(1)}, f32[32,512]{1,0:T(8,128)S(1)}, u32[]{:S(2)}, u32[]{:S(2)}) %collective-permute-start.2) | collective-permute-done | bytes 65568 | tf_op jit(solution)/shard_map/ppermute | solution.py:586
  31.4 1.6 %all-to-all-done.in_ref = s16[8,96,512]{2,1,0:T(8,128)(2,1)S(1)} async-done(((s16[8,96,512]{2,1,0:T(8,128)(2,1)}), s16[8,96,512]{2,1,0:T(8,128)(2,1)S(1)}, u32[]{:S(2)}, u32[]{:S(2)}) %all-to-all-start) | async-done | bytes 786464 | tf_op jit(solution)/shard_map/all_to_all | solution.py:598
  33.6 2.3 %collective-permute-start.3 = (s16[384,512]{1,0:T(8,128)(2,1)S(1)}, s16[384,512]{1,0:T(8,128)(2,1)S(1)}, u32[]{:S(2)}, u32[]{:S(2)}) collective-permute-start(s16[384,512]{1,0:T(8,128)(2,1)S(1)} %get-tuple-element.39), channel_id=1, source_target_pairs={{0,1},{1,2},{2,3},{3,19},{19,18},{18,17},{17,16},{16,20},{20,21},{... | collective-permute-start | bytes 1179656 | tf_op jit(solution)/shard_map/ppermute | solution.py:586
  35.9 1.3 %collective-permute-start.4 = (s16[384,512]{1,0:T(8,128)(2,1)S(1)}, s16[384,512]{1,0:T(8,128)(2,1)S(1)}, u32[]{:S(2)}, u32[]{:S(2)}) collective-permute-start(s16[384,512]{1,0:T(8,128)(2,1)S(1)} %get-tuple-element.40), channel_id=1, source_target_pairs={{1,0},{2,1},{3,2},{19,3},{18,19},{17,18},{16,17},{20,16},{21,20},{... | collective-permute-start | bytes 1179656 | tf_op jit(solution)/shard_map/ppermute | solution.py:586
  37.2 1.4 %forward.1 = (f32[8,32,256]{2,1,0:T(8,128)S(1)}, f32[8,32,256]{2,1,0:T(8,128)S(1)}, f32[8,256,256]{2,1,0:T(8,128)S(1)}) custom-call(bf16[6,256,256]{2,1,0:T(8,128)(2,1)S(1)} %get-tuple-element.29.w_ref, bf16[256,256]{1,0:T(8,128)(2,1)S(1)} %get-tuple-element.30.ax_fwd, bf16[64,192]{1,0:T(8,128)(2,1)S(1)} %get-tuple-element.31.ax_bwd, ...), custom_call_target="tpu_custom_call" | custom-call | tf_op jit(solution)/shard_map/forward/pallas_call | solution.py:644
  38.7 4.2 %collective-permute-done.3.from_left_ref = s16[384,512]{1,0:T(8,128)(2,1)S(1)} collective-permute-done((s16[384,512]{1,0:T(8,128)(2,1)S(1)}, s16[384,512]{1,0:T(8,128)(2,1)S(1)}, u32[]{:S(2)}, u32[]{:S(2)}) %collective-permute-start.3) | collective-permute-done | bytes 393248 | tf_op jit(solution)/shard_map/ppermute | solution.py:586
  42.9 2.7 %collective-permute-done.4.from_right_ref = s16[384,512]{1,0:T(8,128)(2,1)S(1)} collective-permute-done((s16[384,512]{1,0:T(8,128)(2,1)S(1)}, s16[384,512]{1,0:T(8,128)(2,1)S(1)}, u32[]{:S(2)}, u32[]{:S(2)}) %collective-permute-start.4) | collective-permute-done | bytes 393248 | tf_op jit(solution)/shard_map/ppermute | solution.py:586
  45.6 5.6 %first.1 = (f32[8,256,256]{2,1,0:T(8,128)S(1)}, f32[8,32,256]{2,1,0:T(8,128)S(1)}, f32[32,512]{1,0:T(8,128)S(1)}, f32[32,512]{1,0:T(8,128)S(1)}, f32[8,128]{1,0:T(8,128)S(1)}) custom-call(bf16[6,256,256]{2,1,0:T(8,128)(2,1)S(1)} %get-tuple-element.29.w_ref, bf16[256,256]{1,0:T(8,128)(2,1)S(1)} %get-tuple-element.30.ax_fwd, ...), custom_call_target="tpu_custom_call" | custom-call | tf_op jit(solution)/shard_map/first/pallas_call | solution.py:655
  51.1 3.3 %collective-permute-start.5 = (f32[32,512]{1,0:T(8,128)S(1)}, f32[32,512]{1,0:T(8,128)S(1)}, u32[]{:S(2)}, u32[]{:S(2)}) collective-permute-start(f32[32,512]{1,0:T(8,128)S(1)} %get-tuple-element.43), channel_id=1, source_target_pairs={{0,1},{1,2},{2,3},{3,19},{19,18},{18,17},{17,16},{16,20},{20,21},{... | collective-permute-start | bytes 196616 | tf_op jit(solution)/shard_map/ppermute | solution.py:586
  54.4 1.5 %collective-permute-start.6 = (f32[32,512]{1,0:T(8,128)S(1)}, f32[32,512]{1,0:T(8,128)S(1)}, u32[]{:S(2)}, u32[]{:S(2)}) collective-permute-start(f32[32,512]{1,0:T(8,128)S(1)} %get-tuple-element.44), channel_id=1, source_target_pairs={{1,0},{2,1},{3,2},{19,3},{18,19},{17,18},{16,17},{20,16},{21,20},{... | collective-permute-start | bytes 196616 | tf_op jit(solution)/shard_map/ppermute | solution.py:586
  56.3 4.5 %collective-permute-done.6.from_right_ref = f32[32,512]{1,0:T(8,128)S(1)} collective-permute-done((f32[32,512]{1,0:T(8,128)S(1)}, f32[32,512]{1,0:T(8,128)S(1)}, u32[]{:S(2)}, u32[]{:S(2)}) %collective-permute-start.6) | collective-permute-done | bytes 65568 | tf_op jit(solution)/shard_map/ppermute | solution.py:586
  60.8 6.5 %second.1 = s16[8,208,128]{2,1,0:T(8,128)(2,1)S(1)} custom-call(bf16[6,256,256]{2,1,0:T(8,128)(2,1)S(1)} %get-tuple-element.29.w_ref, bf16[256,256]{1,0:T(8,128)(2,1)S(1)} %get-tuple-element.30.ax_fwd, bf16[64,192]{1,0:T(8,128)(2,1)S(1)} %get-tuple-element.31.ax_bwd, f32[8,8,256]{2,1,0:T(8,128)S(1)} %get-tuple-element.32.light_ref, f32[32,256]{1,0:T(8,128)S(1)} %copy-done.2, ...), custom_call_target="tpu_custom_call" | custom-call | tf_op jit(solution)/shard_map/second/pallas_call | solution.py:665
  67.3 16.2 %all_to_all.10.in_ref = s16[8,208,128]{2,1,0:T(8,128)(2,1)S(1)} all-to-all(s16[8,208,128]{2,1,0:T(8,128)(2,1)S(1)} %second.1), channel_id=1, replica_groups=mesh['ty'=2,'tx'=4,'pat'=4] {'ty','pat'}, dimensions={0} | all-to-all | bytes 851968 | tf_op jit(solution)/shard_map/all_to_all | solution.py:675
  83.8 1.4 %unpack.1 = f32[512,256]{1,0:T(8,128)} custom-call(s16[8,208,128]{2,1,0:T(8,128)(2,1)S(1)} %all_to_all.10.in_ref), custom_call_target="tpu_custom_call" | custom-call | tf_op jit(solution)/shard_map/unpack/pallas_call | solution.py:679
  85.1 1.3 %collective-permute-start.8 = (f32[4]{0:T(128)S(1)}, f32[4]{0:T(128)S(1)}, u32[]{:S(2)}, u32[]{:S(2)}) collective-permute-start(f32[4]{0:T(128)S(1)} %add.54), channel_id=1, source_target_pairs={{0,8},{4,12},{8,0},{12,4},{1,9},{5,13},{9,1},{13,5},{2,10},{6,14},... | collective-permute-start | bytes 56 | tf_op jit(solution)/shard_map/ppermute | solution.py:535
  86.5 2.2 %collective-permute-done.8 = f32[4]{0:T(128)S(1)} collective-permute-done((f32[4]{0:T(128)S(1)}, f32[4]{0:T(128)S(1)}, u32[]{:S(2)}, u32[]{:S(2)}) %collective-permute-start.8) | collective-permute-done | bytes 48 | tf_op jit(solution)/shard_map/ppermute | solution.py:535
  (27 shorter events, 2.6 us)
Async XLA Ops:
  0.6 1.2 %copy-start = (f32[2,32,16,256]{3,2,1,0:T(8,128)S(1)}, f32[2,32,16,256]{3,2,1,0:T(8,128)}, u32[]{:S(2)}) copy-start(f32[2,32,16,256]{3,2,1,0:T(8,128)} %param.8) | copy-start | bytes 3145732
  1.9 9.4 %copy-start.1 = (f32[32,16,256]{2,1,0:T(8,128)S(1)}, f32[32,16,256]{2,1,0:T(8,128)}, u32[]{:S(2)}) copy-start(f32[32,16,256]{2,1,0:T(8,128)} %param.7) | copy-start | bytes 1572868
  1.9 21.3 %copy-start.3 = (f32[32,32]{1,0:T(8,128)S(1)}, f32[32,32]{1,0:T(8,128)}, u32[]{:S(2)}) copy-start(f32[32,32]{1,0:T(8,128)} %axial_ref.1) | copy-start | bytes 12292
  1.9 21.3 %copy-start.4 = (f32[9,9]{1,0:T(8,128)S(1)}, f32[9,9]{1,0:T(8,128)}, u32[]{:S(2)}) copy-start(f32[9,9]{1,0:T(8,128)} %k_ref.1) | copy-start | bytes 976
  1.9 21.3 %copy-start.5 = (s32[2,8]{1,0:T(2,128)S(1)}, s32[2,8]{1,0:T(2,128)}, u32[]{:S(2)}) copy-start(s32[2,8]{1,0:T(2,128)} %codes_ref.1) | copy-start | bytes 196
  1.9 21.3 %copy-start.6 = (s32[9]{0:T(128)S(1)}, s32[9]{0:T(128)}, u32[]{:S(2)}) copy-start(s32[9]{0:T(128)} %radius_ref.1) | copy-start | bytes 112
  3.9 33.4 %copy-start.2 = (f32[32,256]{1,0:T(8,128)S(1)}, f32[32,256]{1,0:T(8,128)}, u32[]{:S(2)}) copy-start(f32[32,256]{1,0:T(8,128)} %constant.59.clone.wave_ref) | copy-start | bytes 98308
  3.9 29.1 %all-to-all-start = ((s16[8,96,512]{2,1,0:T(8,128)(2,1)}), s16[8,96,512]{2,1,0:T(8,128)(2,1)S(1)}, u32[]{:S(2)}, u32[]{:S(2)}) async-start(s16[8,96,512]{2,1,0:T(8,128)(2,1)} %pack.1), calls=%async_computation | async-start | bytes 1572864 | tf_op jit(solution)/shard_map/all_to_all | solution.py:598
  12.0 7.3 %collective-permute-start = (f32[32,512]{1,0:T(8,128)S(1)}, f32[32,512]{1,0:T(8,128)S(1)}, u32[]{:S(2)}, u32[]{:S(2)}) collective-permute-start(f32[32,512]{1,0:T(8,128)S(1)} %get-tuple-element.48), channel_id=1, source_target_pairs={{0,16},{16,0},{1,17},{17,1},{2,18},{18,2},{3,19},{19,3},{4,20},{20... | collective-permute-start | bytes 196616 | tf_op jit(solution)/shard_map/ppermute | solution.py:613
  19.4 5.5 %collective-permute-start.1 = (f32[32,512]{1,0:T(8,128)S(1)}, f32[32,512]{1,0:T(8,128)S(1)}, u32[]{:S(2)}, u32[]{:S(2)}) collective-permute-start(f32[32,512]{1,0:T(8,128)S(1)} %get-tuple-element.26), channel_id=1, source_target_pairs={{0,1},{1,2},{2,3},{3,19},{19,18},{18,17},{17,16},{16,20},{20,21},{... | collective-permute-start | bytes 196616 | tf_op jit(solution)/shard_map/ppermute | solution.py:586
  21.9 9.5 %collective-permute-start.2 = (f32[32,512]{1,0:T(8,128)S(1)}, f32[32,512]{1,0:T(8,128)S(1)}, u32[]{:S(2)}, u32[]{:S(2)}) collective-permute-start(f32[32,512]{1,0:T(8,128)S(1)} %get-tuple-element.27), channel_id=1, source_target_pairs={{1,0},{2,1},{3,2},{19,3},{18,19},{17,18},{16,17},{20,16},{21,20},{... | collective-permute-start | bytes 196616 | tf_op jit(solution)/shard_map/ppermute | solution.py:586
  33.6 9.3 %collective-permute-start.3 = (s16[384,512]{1,0:T(8,128)(2,1)S(1)}, s16[384,512]{1,0:T(8,128)(2,1)S(1)}, u32[]{:S(2)}, u32[]{:S(2)}) collective-permute-start(s16[384,512]{1,0:T(8,128)(2,1)S(1)} %get-tuple-element.39), channel_id=1, source_target_pairs={{0,1},{1,2},{2,3},{3,19},{19,18},{18,17},{17,16},{16,20},{20,21},{... | collective-permute-start | bytes 1179656 | tf_op jit(solution)/shard_map/ppermute | solution.py:586
  35.9 9.7 %collective-permute-start.4 = (s16[384,512]{1,0:T(8,128)(2,1)S(1)}, s16[384,512]{1,0:T(8,128)(2,1)S(1)}, u32[]{:S(2)}, u32[]{:S(2)}) collective-permute-start(s16[384,512]{1,0:T(8,128)(2,1)S(1)} %get-tuple-element.40), channel_id=1, source_target_pairs={{1,0},{2,1},{3,2},{19,3},{18,19},{17,18},{16,17},{20,16},{21,20},{... | collective-permute-start | bytes 1179656 | tf_op jit(solution)/shard_map/ppermute | solution.py:586
  51.1 5.2 %collective-permute-start.5 = (f32[32,512]{1,0:T(8,128)S(1)}, f32[32,512]{1,0:T(8,128)S(1)}, u32[]{:S(2)}, u32[]{:S(2)}) collective-permute-start(f32[32,512]{1,0:T(8,128)S(1)} %get-tuple-element.43), channel_id=1, source_target_pairs={{0,1},{1,2},{2,3},{3,19},{19,18},{18,17},{17,16},{16,20},{20,21},{... | collective-permute-start | bytes 196616 | tf_op jit(solution)/shard_map/ppermute | solution.py:586
  54.4 6.4 %collective-permute-start.6 = (f32[32,512]{1,0:T(8,128)S(1)}, f32[32,512]{1,0:T(8,128)S(1)}, u32[]{:S(2)}, u32[]{:S(2)}) collective-permute-start(f32[32,512]{1,0:T(8,128)S(1)} %get-tuple-element.44), channel_id=1, source_target_pairs={{1,0},{2,1},{3,2},{19,3},{18,19},{17,18},{16,17},{20,16},{21,20},{... | collective-permute-start | bytes 196616 | tf_op jit(solution)/shard_map/ppermute | solution.py:586
  83.7 1.4 %collective-permute-start.7 = (f32[4]{0:T(128)S(1)}, f32[4]{0:T(128)S(1)}, u32[]{:S(2)}, u32[]{:S(2)}) collective-permute-start(f32[4]{0:T(128)S(1)} %select_reduce_fusion), channel_id=1, source_target_pairs={{0,4},{4,0},{8,12},{12,8},{1,5},{5,1},{9,13},{13,9},{2,6},{6,2},{1... | collective-permute-start | bytes 56 | tf_op jit(solution)/shard_map/ppermute | solution.py:535
  85.1 3.6 %collective-permute-start.8 = (f32[4]{0:T(128)S(1)}, f32[4]{0:T(128)S(1)}, u32[]{:S(2)}, u32[]{:S(2)}) collective-permute-start(f32[4]{0:T(128)S(1)} %add.54), channel_id=1, source_target_pairs={{0,8},{4,12},{8,0},{12,4},{1,9},{5,13},{9,1},{13,5},{2,10},{6,14},... | collective-permute-start | bytes 56 | tf_op jit(solution)/shard_map/ppermute | solution.py:535

commit v6 on v5

--- a/solution.py
+++ b/solution.py
@@ -68,17 +68,31 @@
                 out_ref[dest, i * SUB : (i + 1) * SUB, quad * LANES : (quad + 1) * LANES] = piece
 
 
-DATA_LOW, DATA_HIGH, TOP = 0.1, 6.0, 2**24 - 1
-DATA_SCALE = TOP / (DATA_HIGH - DATA_LOW)
+TOP = 2**24 - 1
+DATA_BITS = 20
+ROOT_LOW, ROOT_HIGH = math.sqrt(0.1), math.sqrt(6.0)
+DATA_TOP = float(2**DATA_BITS - 1)
+DATA_SCALE = DATA_TOP / (ROOT_HIGH - ROOT_LOW)
 BIAS = 2**15
 
 
 def to_fixed(v):
-    return jnp.clip((v - DATA_LOW) * DATA_SCALE + 0.5, 0.0, float(TOP)).astype(jnp.int32)
+    return jnp.clip((jnp.sqrt(v) - ROOT_LOW) * DATA_SCALE + 0.5, 0.0, DATA_TOP).astype(jnp.int32)
 
 
 def from_fixed(t):
-    return t.astype(F32) * (1.0 / DATA_SCALE) + DATA_LOW
+    root = t.astype(F32) * (1.0 / DATA_SCALE) + ROOT_LOW
+    return root * root
+
+
+def encode_four(values):
+    low = sum((v & 15) << (4 * n) for n, v in enumerate(values))
+    return [(v - BIAS).astype(jnp.int16) for v in [v >> 4 for v in values] + [low]]
+
+
+def decode_four(words):
+    *high, low = [v.astype(jnp.int32) + BIAS for v in words]
+    return [(v << 4) + ((low >> (4 * n)) & 15) for n, v in enumerate(high)]
 
 
 def encode(first, second):
@@ -106,11 +120,11 @@
 def pack_kernel(dest_of_tile, rows, data_ref, out_ref):
     lane = lane_iota((SUB, LANES))
     tiles_half = LANES // TILE
-    part = out_ref.shape[1] // 3
-    per_pattern = part // SUB
-
-    def pieces(group, quad):
-        start = group * rows * SUB + 4 * quad
+    part = out_ref.shape[1] * 2 // 5
+    rows_of = coded_rows(0, part, 1)
+
+    def pieces(row, quad):
+        start = row * rows + 4 * quad
         v = [to_fixed(data_ref[pl.ds(start + r, SUB, stride=rows), :]) for r in QUAD_ROWS]
         return quad_transpose(v, lane)
 
@@ -118,16 +132,13 @@
 
         @pl.when(pl.program_id(0) == half)
         def _(half=half):
-            for g in range(0, per_pattern, 2):
-                for quad in range(rows // 4):
-                    a0, a1 = pieces(g, quad), pieces(g + 1, quad)
-                    b0, b1 = pieces(per_pattern + g, quad), pieces(per_pattern + g + 1, quad)
-                    for t in range(tiles_half):
-                        dest = dest_of(dest_of_tile, half * tiles_half + t)
-                        coded = encode(jnp.concatenate([a0[t], a1[t]]), jnp.concatenate([b0[t], b1[t]]))
-                        for n, v in enumerate(coded):
-                            row = n * part + g * SUB
-                            out_ref[dest, row : row + 2 * SUB, quad * LANES : (quad + 1) * LANES] = v
+            for quad in range(rows // 4):
+                found = [(pieces(r.start, quad), pieces(r.start + SUB, quad)) for r in rows_of[:4]]
+                for t in range(tiles_half):
+                    dest = dest_of(dest_of_tile, half * tiles_half + t)
+                    coded = encode_four([jnp.concatenate([v[t], w[t]]) for v, w in found])
+                    for r, v in zip(rows_of, coded):
+                        out_ref[dest, r, quad * LANES : (quad + 1) * LANES] = v
 
 
 def estimate_kernel(dest_of_tile, rows, pat, est_ref, out_ref, all_ref):
@@ -172,57 +183,54 @@
                     right_ref[row, vreg * LANES : (vreg + 1) * LANES] = right
 
 
-def coded_rows(k, g, part, pat):
-    first = 2 * k * part + g
-    return [slice(r, r + 2 * SUB) for r in (first, first + part, 2 * pat * part + k * part + g)]
-
-
-def own_coded(in_ref, source, g, part, q):
-    rows = [slice(n * part + g, n * part + g + 2 * SUB) for n in range(3)]
-    return decode(*(in_ref[source, r, q * LANES : (q + 1) * LANES] for r in rows))
+def coded_rows(k, part, pat):
+    first = 2 * k * part
+    starts = (first, first + part, first + part // 2, first + part + part // 2, 2 * pat * part + k * part // 2)
+    return [slice(r, r + 2 * SUB) for r in starts]
+
+
+def own_coded(in_ref, source, part, q):
+    return decode_four([in_ref[source, r, q * LANES : (q + 1) * LANES] for r in coded_rows(0, part, 1)])
 
 
 def data_edges_kernel(src_of, in_ref, left_ref, right_ref):
     lane = lane_iota((2 * SUB, LANES))
     ty, pat = src_of
-    part = in_ref.shape[1] // 3
+    part = in_ref.shape[1] * 2 // 5
     per_ty = in_ref.shape[2] // LANES // 2
     for k in range(pat):
-        for g in range(0, part, 2 * SUB):
-            for i in range(ty):
-                for pair in range(per_ty):
-                    both = [own_coded(in_ref, i * pat + k, g, part, q) for q in (2 * pair, 2 * pair + 1)]
-                    sides = []
-                    for p in range(2):
-                        sides.append(edge_messages([(v[p], o) for v in both for o in (0, TILE)], lane))
-                    vreg = i * per_ty + pair
-                    for side, ref in enumerate((left_ref, right_ref)):
-                        for r, v in zip(coded_rows(k, g, part, pat), encode(sides[0][side], sides[1][side])):
-                            ref[r, vreg * LANES : (vreg + 1) * LANES] = v
+        rows = coded_rows(k, part, pat)
+        for i in range(ty):
+            for pair in range(per_ty):
+                both = [own_coded(in_ref, i * pat + k, part, q) for q in (2 * pair, 2 * pair + 1)]
+                sides = [edge_messages([(v[n], o) for v in both for o in (0, TILE)], lane) for n in range(4)]
+                vreg = i * per_ty + pair
+                for side, ref in enumerate((left_ref, right_ref)):
+                    for r, v in zip(rows, encode_four([found[side] for found in sides])):
+                        ref[r, vreg * LANES : (vreg + 1) * LANES] = v
 
 
 def unpack_data(src_of, in_ref, from_left_ref, from_right_ref, out_ref):
     lane = lane_iota((2 * SUB, LANES))
     ty, pat = src_of
-    part = in_ref.shape[1] // 3
+    part = in_ref.shape[1] * 2 // 5
     per_ty = in_ref.shape[2] // LANES // 2
     for k in range(pat):
-        for g in range(0, part, 2 * SUB):
-            rows = coded_rows(k, g, part, pat)
-            for i in range(ty):
-                for pair in range(per_ty):
-                    vreg = i * per_ty + pair
-                    at = slice(vreg * LANES, (vreg + 1) * LANES)
-                    from_left = decode(*(from_left_ref[r, at] for r in rows))
-                    from_right = decode(*(from_right_ref[r, at] for r in rows))
-                    both = [own_coded(in_ref, i * pat + k, g, part, q) for q in (2 * pair, 2 * pair + 1)]
-                    for p in range(2):
-                        own = [x for v in both for x in (v[p], roll(v[p], -TILE))]
-                        for u in range(4):
-                            m = 4 * vreg + u
-                            out_ref[m // 2, rows[p], (m % 2) * LANES : (m % 2 + 1) * LANES] = from_fixed(
-                                with_halo(own[u], u, from_right[p], from_left[p], lane)
-                            )
+        rows = coded_rows(k, part, pat)
+        for i in range(ty):
+            for pair in range(per_ty):
+                vreg = i * per_ty + pair
+                at = slice(vreg * LANES, (vreg + 1) * LANES)
+                from_left = decode_four([from_left_ref[r, at] for r in rows])
+                from_right = decode_four([from_right_ref[r, at] for r in rows])
+                both = [own_coded(in_ref, i * pat + k, part, q) for q in (2 * pair, 2 * pair + 1)]
+                for n in range(4):
+                    own = [x for v in both for x in (v[n], roll(v[n], -TILE))]
+                    for u in range(4):
+                        m = 4 * vreg + u
+                        out_ref[m // 2, rows[n], (m % 2) * LANES : (m % 2 + 1) * LANES] = from_fixed(
+                            with_halo(own[u], u, from_right[n], from_left[n], lane)
+                        )
 
 
 def unpack_wide(src_of, in_ref, from_left_ref, from_right_ref, out_ref):
@@ -587,10 +595,10 @@
 
     message = pl.pallas_call(
         functools.partial(pack_kernel, dest_of_tile, rows),
-        out_shape=shape((members, 3 * planes, piece_lanes), jnp.int16),
+        out_shape=shape((members, 5 * planes // 2, piece_lanes), jnp.int16),
         grid=(halves,),
         in_specs=[half_columns(data.size // cols)],
-        out_specs=whole((members, 3 * planes, piece_lanes)),
+        out_specs=whole((members, 5 * planes // 2, piece_lanes)),
         compiler_params=PARAMS,
         name="pack",
     )(data.reshape(-1, cols))
@@ -812,7 +820,7 @@
             and cols % LANES == 0
             and rows % 8 == 0
             and rows * sizes["ty"] <= 2 * TILE
-            and planes % (2 * SUB) == 0
+            and planes == 4 * SUB
             and data.shape[0] == 2
         )
         if fits:

time: 89.7 us -> 87.6 us (0.977)
  waiting for transfers between devices: 27.4 us -> 24.4 us
  starting transfers between devices: 22.9 us -> 24.3 us
    ppermute x3, starting transfers between devices: 7.98 us -> 10.3 us  [swap_edges(): lax.ppermute(right, axes, to_right)]
    ppermute x3, waiting for transfers between devices: 13.7 us -> 11.7 us  [swap_edges(): lax.ppermute(left, axes, to_left)]
    all_to_all x1, waiting for transfers between devices: 1.61 us -> 0.01 us  [tiled_device(): mine = lax.all_to_all(message, ('ty', 'pat'), 0, 0, tiled=True)]
    ppermute x2, starting transfers between devices: 1.39 us -> 0.38 us  [over_tx(): lax.ppermute(value, 'tx', [(i, i ^ step) for i in range(size)])]
    ppermute x2, waiting for transfers between devices: 2.25 us -> 3.26 us  [over_tx(): lax.ppermute(value, 'tx', [(i, i ^ step) for i in range(size)])]
  transfers between devices with their start and end apart: 10 -> 10, of which waited for: 8 -> 7; matrix products, arithmetic and copies ran while one was open for 0% -> 0% of each run, Pallas kernels for 6% -> 6%
where the time goes in v6:
time: 87.6 us; the launch traced here: 87.2 us
  waiting for transfers between devices  24.4 us (28%)
  starting transfers between devices  24.3 us (28%)
  Pallas kernels  20 us (23%)
  blocking collectives  15.7 us (18%)
  local copies, waits for them, and re-layouts  1.26 us (1%)
    all_to_all x1, blocking collectives, tiled_device(): incoming = lax.all_to_all(outgoing, ('ty', 'pat'), 0, 0, tiled=True)  15.7 us
    ppermute x3, waiting for transfers between devices, swap_edges(): lax.ppermute(left, axes, to_left)  11.7 us
    ppermute x3, starting transfers between devices, swap_edges(): lax.ppermute(right, axes, to_right)  10.3 us
    all_to_all x1, starting transfers between devices, tiled_device(): mine = lax.all_to_all(message, ('ty', 'pat'), 0, 0, tiled=True)  7.41 us
    pallas_call x1, Pallas kernels, tiled_device(): pl.pallas_call(functools.partial(second_kernel, nx, tile_of, src_of), out...  6.52 us
    pallas_call x1, Pallas kernels, tiled_device(): pl.pallas_call(functools.partial(first_kernel, nx, tile_of, src_of), out_...  5.61 us
    ppermute x3, waiting for transfers between devices, swap_edges(): lax.ppermute(right, axes, to_right)  4.88 us
    ppermute x1, waiting for transfers between devices, tiled_device(): lax.ppermute(sent, 'ty', [(i, (i + shift) % ty) for i in range(ty)])  4.5 us
  transfers between devices with their start and end apart: 10, of which 7 were waited for; matrix products, arithmetic and copies ran while one was open for 0% of the time, Pallas kernels for 6%

profile of v6, /device:TPU:0, one launch (start us, length us, event | category | flops | bytes accessed | tf_op | source)
XLA Modules:
  0.0 87.2 jit_solution(12946703787930175780)
XLA Ops:
  0.6 1.2 %copy-done = f32[2,32,16,256]{3,2,1,0:T(8,128)S(1)} copy-done((f32[2,32,16,256]{3,2,1,0:T(8,128)S(1)}, f32[2,32,16,256]{3,2,1,0:T(8,128)}, u32[]{:S(2)}) %copy-start) | copy-done | bytes 1048600
  1.9 2.0 %pack.1 = s16[8,80,512]{2,1,0:T(8,128)(2,1)} custom-call(f32[1024,256]{1,0:T(8,128)S(1)} %bitcast.6), custom_call_target="tpu_custom_call" | custom-call | tf_op jit(solution)/shard_map/pack/pallas_call | solution.py:596
  3.9 7.4 %all-to-all-start = ((s16[8,80,512]{2,1,0:T(8,128)(2,1)}), s16[8,80,512]{2,1,0:T(8,128)(2,1)S(1)}, u32[]{:S(2)}, u32[]{:S(2)}) async-start(s16[8,80,512]{2,1,0:T(8,128)(2,1)} %pack.1), calls=%async_computation | async-start | bytes 1310720 | tf_op jit(solution)/shard_map/all_to_all | solution.py:606
  11.3 0.7 prep_estimate.1
  12.0 2.1 %collective-permute-start = (f32[32,512]{1,0:T(8,128)S(1)}, f32[32,512]{1,0:T(8,128)S(1)}, u32[]{:S(2)}, u32[]{:S(2)}) collective-permute-start(f32[32,512]{1,0:T(8,128)S(1)} %get-tuple-element.48), channel_id=1, source_target_pairs={{0,16},{16,0},{1,17},{17,1},{2,18},{18,2},{3,19},{19,3},{4,20},{20... | collective-permute-start | bytes 196616 | tf_op jit(solution)/shard_map/ppermute | solution.py:621
  14.1 4.5 %collective-permute-done = f32[32,512]{1,0:T(8,128)S(1)} collective-permute-done((f32[32,512]{1,0:T(8,128)S(1)}, f32[32,512]{1,0:T(8,128)S(1)}, u32[]{:S(2)}, u32[]{:S(2)}) %collective-permute-start) | collective-permute-done | bytes 65568 | tf_op jit(solution)/shard_map/ppermute | solution.py:621
  18.8 2.5 %collective-permute-start.1 = (f32[32,512]{1,0:T(8,128)S(1)}, f32[32,512]{1,0:T(8,128)S(1)}, u32[]{:S(2)}, u32[]{:S(2)}) collective-permute-start(f32[32,512]{1,0:T(8,128)S(1)} %get-tuple-element.26), channel_id=1, source_target_pairs={{0,1},{1,2},{2,3},{3,19},{19,18},{18,17},{17,16},{16,20},{20,21},{... | collective-permute-start | bytes 196616 | tf_op jit(solution)/shard_map/ppermute | solution.py:594
  21.3 1.3 %collective-permute-start.2 = (f32[32,512]{1,0:T(8,128)S(1)}, f32[32,512]{1,0:T(8,128)S(1)}, u32[]{:S(2)}, u32[]{:S(2)}) collective-permute-start(f32[32,512]{1,0:T(8,128)S(1)} %get-tuple-element.27), channel_id=1, source_target_pairs={{1,0},{2,1},{3,2},{19,3},{18,19},{17,18},{16,17},{20,16},{21,20},{... | collective-permute-start | bytes 196616 | tf_op jit(solution)/shard_map/ppermute | solution.py:594
  22.6 1.7 %tables.1 = (bf16[6,256,256]{2,1,0:T(8,128)(2,1)S(1)}, bf16[256,256]{1,0:T(8,128)(2,1)S(1)}, bf16[64,192]{1,0:T(8,128)(2,1)S(1)}, f32[8,8,256]{2,1,0:T(8,128)S(1)}) custom-call(f32[9,9]{1,0:T(8,128)S(1)} %copy-done.4, s32[9]{0:T(128)S(1)} %copy-done.6, s32[2,8]{1,0:T(2,128)S(1)} %copy-done.5, f32[32,32]{1,0:T(8,128)S(1)} %copy-done.3), custom_call_target="tpu_custom_call" | custom-call | tf_op jit(solution)/shard_map/tables/pallas_call | solution.py:628
  24.3 5.7 %collective-permute-done.2.from_right_ref = f32[32,512]{1,0:T(8,128)S(1)} collective-permute-done((f32[32,512]{1,0:T(8,128)S(1)}, f32[32,512]{1,0:T(8,128)S(1)}, u32[]{:S(2)}, u32[]{:S(2)}) %collective-permute-start.2) | collective-permute-done | bytes 65568 | tf_op jit(solution)/shard_map/ppermute | solution.py:594
  30.0 0.6 edges.1
  30.6 4.0 %collective-permute-start.3 = (s16[320,512]{1,0:T(8,128)(2,1)S(1)}, s16[320,512]{1,0:T(8,128)(2,1)S(1)}, u32[]{:S(2)}, u32[]{:S(2)}) collective-permute-start(s16[320,512]{1,0:T(8,128)(2,1)S(1)} %get-tuple-element.39), channel_id=1, source_target_pairs={{0,1},{1,2},{2,3},{3,19},{19,18},{18,17},{17,16},{16,20},{20,21},{... | collective-permute-start | bytes 983048 | tf_op jit(solution)/shard_map/ppermute | solution.py:594
  34.6 1.3 %collective-permute-start.4 = (s16[320,512]{1,0:T(8,128)(2,1)S(1)}, s16[320,512]{1,0:T(8,128)(2,1)S(1)}, u32[]{:S(2)}, u32[]{:S(2)}) collective-permute-start(s16[320,512]{1,0:T(8,128)(2,1)S(1)} %get-tuple-element.40), channel_id=1, source_target_pairs={{1,0},{2,1},{3,2},{19,3},{18,19},{17,18},{16,17},{20,16},{21,20},{... | collective-permute-start | bytes 983048 | tf_op jit(solution)/shard_map/ppermute | solution.py:594
  35.9 1.4 %forward.1 = (f32[8,32,256]{2,1,0:T(8,128)S(1)}, f32[8,32,256]{2,1,0:T(8,128)S(1)}, f32[8,256,256]{2,1,0:T(8,128)S(1)}) custom-call(bf16[6,256,256]{2,1,0:T(8,128)(2,1)S(1)} %get-tuple-element.29.w_ref, bf16[256,256]{1,0:T(8,128)(2,1)S(1)} %get-tuple-element.30.ax_fwd, bf16[64,192]{1,0:T(8,128)(2,1)S(1)} %get-tuple-element.31.ax_bwd, ...), custom_call_target="tpu_custom_call" | custom-call | tf_op jit(solution)/shard_map/forward/pallas_call | solution.py:652
  37.3 4.5 %collective-permute-done.3.from_left_ref = s16[320,512]{1,0:T(8,128)(2,1)S(1)} collective-permute-done((s16[320,512]{1,0:T(8,128)(2,1)S(1)}, s16[320,512]{1,0:T(8,128)(2,1)S(1)}, u32[]{:S(2)}, u32[]{:S(2)}) %collective-permute-start.3) | collective-permute-done | bytes 327712 | tf_op jit(solution)/shard_map/ppermute | solution.py:594
  41.8 1.8 %collective-permute-done.4.from_right_ref = s16[320,512]{1,0:T(8,128)(2,1)S(1)} collective-permute-done((s16[320,512]{1,0:T(8,128)(2,1)S(1)}, s16[320,512]{1,0:T(8,128)(2,1)S(1)}, u32[]{:S(2)}, u32[]{:S(2)}) %collective-permute-start.4) | collective-permute-done | bytes 327712 | tf_op jit(solution)/shard_map/ppermute | solution.py:594
  43.5 5.6 %first.1 = (f32[8,256,256]{2,1,0:T(8,128)S(1)}, f32[8,32,256]{2,1,0:T(8,128)S(1)}, f32[32,512]{1,0:T(8,128)S(1)}, f32[32,512]{1,0:T(8,128)S(1)}, f32[8,128]{1,0:T(8,128)S(1)}) custom-call(bf16[6,256,256]{2,1,0:T(8,128)(2,1)S(1)} %get-tuple-element.29.w_ref, bf16[256,256]{1,0:T(8,128)(2,1)S(1)} %get-tuple-element.30.ax_fwd, ...), custom_call_target="tpu_custom_call" | custom-call | tf_op jit(solution)/shard_map/first/pallas_call | solution.py:663
  49.2 3.9 %collective-permute-start.5 = (f32[32,512]{1,0:T(8,128)S(1)}, f32[32,512]{1,0:T(8,128)S(1)}, u32[]{:S(2)}, u32[]{:S(2)}) collective-permute-start(f32[32,512]{1,0:T(8,128)S(1)} %get-tuple-element.43), channel_id=1, source_target_pairs={{0,1},{1,2},{2,3},{3,19},{19,18},{18,17},{17,16},{16,20},{20,21},{... | collective-permute-start | bytes 196616 | tf_op jit(solution)/shard_map/ppermute | solution.py:594
  53.1 1.5 %collective-permute-start.6 = (f32[32,512]{1,0:T(8,128)S(1)}, f32[32,512]{1,0:T(8,128)S(1)}, u32[]{:S(2)}, u32[]{:S(2)}) collective-permute-start(f32[32,512]{1,0:T(8,128)S(1)} %get-tuple-element.44), channel_id=1, source_target_pairs={{1,0},{2,1},{3,2},{19,3},{18,19},{17,18},{16,17},{20,16},{21,20},{... | collective-permute-start | bytes 196616 | tf_op jit(solution)/shard_map/ppermute | solution.py:594
  55.0 4.3 %collective-permute-done.6.from_right_ref = f32[32,512]{1,0:T(8,128)S(1)} collective-permute-done((f32[32,512]{1,0:T(8,128)S(1)}, f32[32,512]{1,0:T(8,128)S(1)}, u32[]{:S(2)}, u32[]{:S(2)}) %collective-permute-start.6) | collective-permute-done | bytes 65568 | tf_op jit(solution)/shard_map/ppermute | solution.py:594
  59.2 6.5 %second.1 = s16[8,208,128]{2,1,0:T(8,128)(2,1)S(1)} custom-call(bf16[6,256,256]{2,1,0:T(8,128)(2,1)S(1)} %get-tuple-element.29.w_ref, bf16[256,256]{1,0:T(8,128)(2,1)S(1)} %get-tuple-element.30.ax_fwd, bf16[64,192]{1,0:T(8,128)(2,1)S(1)} %get-tuple-element.31.ax_bwd, f32[8,8,256]{2,1,0:T(8,128)S(1)} %get-tuple-element.32.light_ref, f32[32,256]{1,0:T(8,128)S(1)} %copy-done.2, ...), custom_call_target="tpu_custom_call" | custom-call | tf_op jit(solution)/shard_map/second/pallas_call | solution.py:673
  65.8 15.7 %all_to_all.10.in_ref = s16[8,208,128]{2,1,0:T(8,128)(2,1)S(1)} all-to-all(s16[8,208,128]{2,1,0:T(8,128)(2,1)S(1)} %second.1), channel_id=1, replica_groups=mesh['ty'=2,'tx'=4,'pat'=4] {'ty','pat'}, dimensions={0} | all-to-all | bytes 851968 | tf_op jit(solution)/shard_map/all_to_all | solution.py:683
  81.7 1.4 %unpack.1 = f32[512,256]{1,0:T(8,128)} custom-call(s16[8,208,128]{2,1,0:T(8,128)(2,1)S(1)} %all_to_all.10.in_ref), custom_call_target="tpu_custom_call" | custom-call | tf_op jit(solution)/shard_map/unpack/pallas_call | solution.py:687
  83.4 3.3 %collective-permute-done.8 = f32[4]{0:T(128)S(1)} collective-permute-done((f32[4]{0:T(128)S(1)}, f32[4]{0:T(128)S(1)}, u32[]{:S(2)}, u32[]{:S(2)}) %collective-permute-start.8) | collective-permute-done | bytes 48 | tf_op jit(solution)/shard_map/ppermute | solution.py:543
  (27 shorter events, 1.7 us)
Async XLA Ops:
  0.6 1.2 %copy-start = (f32[2,32,16,256]{3,2,1,0:T(8,128)S(1)}, f32[2,32,16,256]{3,2,1,0:T(8,128)}, u32[]{:S(2)}) copy-start(f32[2,32,16,256]{3,2,1,0:T(8,128)} %param.8) | copy-start | bytes 3145732
  1.9 9.4 %copy-start.1 = (f32[32,16,256]{2,1,0:T(8,128)S(1)}, f32[32,16,256]{2,1,0:T(8,128)}, u32[]{:S(2)}) copy-start(f32[32,16,256]{2,1,0:T(8,128)} %param.7) | copy-start | bytes 1572868
  1.9 20.7 %copy-start.3 = (f32[32,32]{1,0:T(8,128)S(1)}, f32[32,32]{1,0:T(8,128)}, u32[]{:S(2)}) copy-start(f32[32,32]{1,0:T(8,128)} %axial_ref.1) | copy-start | bytes 12292
  1.9 20.7 %copy-start.4 = (f32[9,9]{1,0:T(8,128)S(1)}, f32[9,9]{1,0:T(8,128)}, u32[]{:S(2)}) copy-start(f32[9,9]{1,0:T(8,128)} %k_ref.1) | copy-start | bytes 976
  1.9 20.7 %copy-start.5 = (s32[2,8]{1,0:T(2,128)S(1)}, s32[2,8]{1,0:T(2,128)}, u32[]{:S(2)}) copy-start(s32[2,8]{1,0:T(2,128)} %codes_ref.1) | copy-start | bytes 196
  1.9 20.7 %copy-start.6 = (s32[9]{0:T(128)S(1)}, s32[9]{0:T(128)}, u32[]{:S(2)}) copy-start(s32[9]{0:T(128)} %radius_ref.1) | copy-start | bytes 112
  3.9 32.0 %copy-start.2 = (f32[32,256]{1,0:T(8,128)S(1)}, f32[32,256]{1,0:T(8,128)}, u32[]{:S(2)}) copy-start(f32[32,256]{1,0:T(8,128)} %constant.59.clone.wave_ref) | copy-start | bytes 98308
  3.9 26.1 %all-to-all-start = ((s16[8,80,512]{2,1,0:T(8,128)(2,1)}), s16[8,80,512]{2,1,0:T(8,128)(2,1)S(1)}, u32[]{:S(2)}, u32[]{:S(2)}) async-start(s16[8,80,512]{2,1,0:T(8,128)(2,1)} %pack.1), calls=%async_computation | async-start | bytes 1310720 | tf_op jit(solution)/shard_map/all_to_all | solution.py:606
  12.0 6.6 %collective-permute-start = (f32[32,512]{1,0:T(8,128)S(1)}, f32[32,512]{1,0:T(8,128)S(1)}, u32[]{:S(2)}, u32[]{:S(2)}) collective-permute-start(f32[32,512]{1,0:T(8,128)S(1)} %get-tuple-element.48), channel_id=1, source_target_pairs={{0,16},{16,0},{1,17},{17,1},{2,18},{18,2},{3,19},{19,3},{4,20},{20... | collective-permute-start | bytes 196616 | tf_op jit(solution)/shard_map/ppermute | solution.py:621
  18.8 5.5 %collective-permute-start.1 = (f32[32,512]{1,0:T(8,128)S(1)}, f32[32,512]{1,0:T(8,128)S(1)}, u32[]{:S(2)}, u32[]{:S(2)}) collective-permute-start(f32[32,512]{1,0:T(8,128)S(1)} %get-tuple-element.26), channel_id=1, source_target_pairs={{0,1},{1,2},{2,3},{3,19},{19,18},{18,17},{17,16},{16,20},{20,21},{... | collective-permute-start | bytes 196616 | tf_op jit(solution)/shard_map/ppermute | solution.py:594
  21.3 8.7 %collective-permute-start.2 = (f32[32,512]{1,0:T(8,128)S(1)}, f32[32,512]{1,0:T(8,128)S(1)}, u32[]{:S(2)}, u32[]{:S(2)}) collective-permute-start(f32[32,512]{1,0:T(8,128)S(1)} %get-tuple-element.27), channel_id=1, source_target_pairs={{1,0},{2,1},{3,2},{19,3},{18,19},{17,18},{16,17},{20,16},{21,20},{... | collective-permute-start | bytes 196616 | tf_op jit(solution)/shard_map/ppermute | solution.py:594
  30.6 11.2 %collective-permute-start.3 = (s16[320,512]{1,0:T(8,128)(2,1)S(1)}, s16[320,512]{1,0:T(8,128)(2,1)S(1)}, u32[]{:S(2)}, u32[]{:S(2)}) collective-permute-start(s16[320,512]{1,0:T(8,128)(2,1)S(1)} %get-tuple-element.39), channel_id=1, source_target_pairs={{0,1},{1,2},{2,3},{3,19},{19,18},{18,17},{17,16},{16,20},{20,21},{... | collective-permute-start | bytes 983048 | tf_op jit(solution)/shard_map/ppermute | solution.py:594
  34.6 9.0 %collective-permute-start.4 = (s16[320,512]{1,0:T(8,128)(2,1)S(1)}, s16[320,512]{1,0:T(8,128)(2,1)S(1)}, u32[]{:S(2)}, u32[]{:S(2)}) collective-permute-start(s16[320,512]{1,0:T(8,128)(2,1)S(1)} %get-tuple-element.40), channel_id=1, source_target_pairs={{1,0},{2,1},{3,2},{19,3},{18,19},{17,18},{16,17},{20,16},{21,20},{... | collective-permute-start | bytes 983048 | tf_op jit(solution)/shard_map/ppermute | solution.py:594
  49.2 5.8 %collective-permute-start.5 = (f32[32,512]{1,0:T(8,128)S(1)}, f32[32,512]{1,0:T(8,128)S(1)}, u32[]{:S(2)}, u32[]{:S(2)}) collective-permute-start(f32[32,512]{1,0:T(8,128)S(1)} %get-tuple-element.43), channel_id=1, source_target_pairs={{0,1},{1,2},{2,3},{3,19},{19,18},{18,17},{17,16},{16,20},{20,21},{... | collective-permute-start | bytes 196616 | tf_op jit(solution)/shard_map/ppermute | solution.py:594
  53.1 6.2 %collective-permute-start.6 = (f32[32,512]{1,0:T(8,128)S(1)}, f32[32,512]{1,0:T(8,128)S(1)}, u32[]{:S(2)}, u32[]{:S(2)}) collective-permute-start(f32[32,512]{1,0:T(8,128)S(1)} %get-tuple-element.44), channel_id=1, source_target_pairs={{1,0},{2,1},{3,2},{19,3},{18,19},{17,18},{16,17},{20,16},{21,20},{... | collective-permute-start | bytes 196616 | tf_op jit(solution)/shard_map/ppermute | solution.py:594
  81.7 1.4 %collective-permute-start.7 = (f32[4]{0:T(128)S(1)}, f32[4]{0:T(128)S(1)}, u32[]{:S(2)}, u32[]{:S(2)}) collective-permute-start(f32[4]{0:T(128)S(1)} %select_reduce_fusion), channel_id=1, source_target_pairs={{0,4},{4,0},{8,12},{12,8},{1,5},{5,1},{9,13},{13,9},{2,6},{6,2},{1... | collective-permute-start | bytes 56 | tf_op jit(solution)/shard_map/ppermute | solution.py:543
  83.1 3.6 %collective-permute-start.8 = (f32[4]{0:T(128)S(1)}, f32[4]{0:T(128)S(1)}, u32[]{:S(2)}, u32[]{:S(2)}) collective-permute-start(f32[4]{0:T(128)S(1)} %add.54), channel_id=1, source_target_pairs={{0,8},{4,12},{8,0},{12,4},{1,9},{5,13},{9,1},{13,5},{2,10},{6,14},... | collective-permute-start | bytes 56 | tf_op jit(solution)/shard_map/ppermute | solution.py:543
